TPU v7x, 32 devices: a whole 2x2x4 slice. The times are simulated.
32 devices in a mesh: row: 4 (over x, core), col: 8 (over z, y).
Axes of the slice: x: 2, y: 2, z: 4, core: 2. Of those that a mesh axis runs over, the one named last changes fastest.
Arguments:
- rhs: float32 [4, 8, 8, 4, 128], P('row', 'col'), may hold values from -6 to 6
- diag0: float32 [4, 8, 8, 128], P('row', 'col'), may hold values from 2 to 4
- blocks0: float32 [4, 8, 8, 14, 128, 128], P('row', 'col'), may hold values from -0.1875 to 0.1875
- cols0: int32 [4, 8, 8, 14], P('row', 'col'), may hold values from 0 to 23
- sends0: int32 [4, 8, 4, 4], P('row', 'col'), may hold values from 0 to 7
- pro0: float32 [4, 8, 8, 128, 128], P('row', 'col'), may hold values from -0.5 to 0.5
- agg0: int32 [4, 8, 8], P('row', 'col'), may hold values from 0 to 1
- diag1: float32 [4, 8, 2, 128], P('row', 'col'), may hold values from 2 to 4
- blocks1: float32 [4, 8, 2, 14, 128, 128], P('row', 'col'), may hold values from -0.1875 to 0.1875
- cols1: int32 [4, 8, 2, 14], P('row', 'col'), may hold values from 0 to 9
- sends1: int32 [4, 8, 4, 2], P('row', 'col'), may hold values from 0 to 1
- pro1: float32 [4, 8, 2, 128, 128], P('row', 'col'), may hold values from -0.25 to 0.25
- agg1: int32 [4, 8, 2], P('row', 'col'), may hold values from 0 to 7
- cinv: float32 [1024, 1024], P(('row', 'col')), may hold values from -0.1875 to 0.1875
Outputs:
- solution: float32 [4, 8, 8, 4, 128], P('row', 'col')
Inputs may be any that keep to these rules, and one draw needn't show every extreme that they name: `sends0`: indices of the sender's own fine blocks. `sends1`: indices of the sender's own level-one blocks. `cols0`: indices into the extended fine vector of 24 blocks. `cols1`: indices into the extended level-one vector of 10 blocks. `agg0`: a level-one block of the same partition. `agg1`: a coarsest block, on any partition.
All inputs are finite; a program needn't handle non-finite values.
Results may differ from a plain program's by a relative error of at most 0.0001.
Values sent between devices are 32-bit elements; how exact they have to be, the bound alone decides.
No kernel may reach another device: no remote copies, remote signals or barrier semaphores. Data moves between devices by JAX's collectives and lax.ppermute only.
A program may use at most 64 MiB of HBM per device.

v0:
```python
import jax
import jax.numpy as jnp
from jax import lax
from jax.sharding import PartitionSpec as P

NU = 2


HIGH = lax.Precision.HIGHEST
OMEGA = 0.3


def padded_2(value, sides, width):
    for axis, dim in sides:
        size, length = (lax.axis_size(axis), value.shape[dim])
        up = [(i, (i + 1) % size) for i in range(size - 1)]
        down = [(j, i) for i, j in up]
        last = lax.slice_in_dim(value, length - width, length, axis=dim)
        leading = lax.slice_in_dim(value, 0, width, axis=dim)
        before = lax.ppermute(last, axis, up)
        after = lax.ppermute(leading, axis, down)
        value = jnp.concatenate([before, value, after], axis=dim)
    return value


def gather_ghosts(vector, sends):
    packed = vector[sends]
    padded = padded_2(packed[None, None], (("row", 0), ("col", 1)), 1)
    return jnp.concatenate(
        [vector, padded[0, 1, 0], padded[2, 1, 1], padded[1, 0, 2], padded[1, 2, 3]], axis=0
    )


def apply_op(vector, diag, blocks, cols, sends):
    extended = gather_ghosts(vector, sends)
    nearby = extended[cols]
    coupled = jnp.einsum("bkij,bkrj->bri", blocks, nearby, precision=HIGH)
    return diag[:, None, :] * vector + coupled


def smooth(vector, right_side, diag, blocks, cols, sends, count):
    for sweep in range(count):
        vector = (
            vector
            + OMEGA * (right_side - apply_op(vector, diag, blocks, cols, sends)) / diag[:, None, :]
        )
    return vector


def on_device(
    rhs, diag0, blocks0, cols0, sends0, pro0, agg0, diag1, blocks1, cols1, sends1, pro1, agg1, cinv
):
    fine_rhs = rhs[0, 0]
    fine_diag = diag0[0, 0]
    fine_blocks = blocks0[0, 0]
    fine_cols = cols0[0, 0]
    fine_sends = sends0[0, 0]
    fine_pro = pro0[0, 0]
    level_diag = diag1[0, 0]
    level_blocks = blocks1[0, 0]
    level_cols = cols1[0, 0]
    level_sends = sends1[0, 0]
    level_pro = pro1[0, 0]
    level_count = level_diag.shape[0]
    block_size = level_diag.shape[1]
    loads = fine_rhs.shape[1]
    coarse_total = cinv.shape[1]
    coarse_count = coarse_total // block_size
    fine_x = OMEGA * fine_rhs / fine_diag[:, None, :]
    fine_x = smooth(fine_x, fine_rhs, fine_diag, fine_blocks, fine_cols, fine_sends, NU - 1)
    fine_res = fine_rhs - apply_op(fine_x, fine_diag, fine_blocks, fine_cols, fine_sends)
    onehot0 = (agg0[0, 0][:, None] == jnp.arange(level_count)).astype(jnp.float32)
    restricted = jnp.einsum("bij,bri->brj", fine_pro, fine_res, precision=HIGH)
    level_rhs = jnp.einsum("bc,brj->crj", onehot0, restricted, precision=HIGH)
    level_x = OMEGA * level_rhs / level_diag[:, None, :]
    level_x = smooth(level_x, level_rhs, level_diag, level_blocks, level_cols, level_sends, NU - 1)
    level_res = level_rhs - apply_op(level_x, level_diag, level_blocks, level_cols, level_sends)
    onehot1 = (agg1[0, 0][:, None] == jnp.arange(coarse_count)).astype(jnp.float32)
    contrib = jnp.einsum("bij,bri->brj", level_pro, level_res, precision=HIGH)
    term = jnp.einsum("bc,brj->rcj", onehot1, contrib, precision=HIGH).reshape(loads, coarse_total)
    coarse_rhs = lax.psum(term, ("row", "col"))
    own_rows = jnp.einsum("ij,rj->ri", cinv, coarse_rhs, precision=HIGH)
    coarse_x = lax.all_gather(own_rows, ("row", "col"), axis=1, tiled=True)
    coarse_blocks = coarse_x.reshape(loads, coarse_count, block_size)
    picked = jnp.einsum("bc,rcj->brj", onehot1, coarse_blocks, precision=HIGH)
    level_x = level_x + jnp.einsum("bij,brj->bri", level_pro, picked, precision=HIGH)
    level_x = smooth(level_x, level_rhs, level_diag, level_blocks, level_cols, level_sends, NU)
    lifted = jnp.einsum("bc,crj->brj", onehot0, level_x, precision=HIGH)
    fine_x = fine_x + jnp.einsum("bij,brj->bri", fine_pro, lifted, precision=HIGH)
    fine_x = smooth(fine_x, fine_rhs, fine_diag, fine_blocks, fine_cols, fine_sends, NU)
    return fine_x[None, None]


def solution(mesh):
    return jax.shard_map(
        on_device,
        mesh=mesh,
        in_specs=(
            P("row", "col", None, None, None),
            P("row", "col", None, None),
            P("row", "col", None, None, None, None),
            P("row", "col", None, None),
            P("row", "col", None, None),
            P("row", "col", None, None, None),
            P("row", "col", None),
            P("row", "col", None, None),
            P("row", "col", None, None, None, None),
            P("row", "col", None, None),
            P("row", "col", None, None),
            P("row", "col", None, None, None),
            P("row", "col", None),
            P(("row", "col"), None),
        ),
        out_specs=P("row", "col", None, None, None),
        check_vma=False,
    )
```

profile of v0, /device:TPU:1, one launch (start us, length us, event | category | flops | bytes accessed | tf_op | source)
XLA Modules:
  0.0 297.1 jit_solution(16686773013737030327)
XLA Ops:
  3.1 4.5 %collective-permute-start = (f32[1,1,4,4,4,128]{5,4,3,2,1,0:T(4,128)S(1)}, f32[1,1,4,4,4,128]{5,4,3,2,1,0:T(4,128)S(1)}, u32[]{:S(2)}, u32[]{:S(2)}) collective-permute-start(f32[1,1,4,4,4,128]{5,4,3,2,1,0:T(4,128)S(1)} %bitcast.453), channel_id=1, source_target_pairs={{0,8},{8,16},{16,24},{1,9},{9,17},{17,25},{2,10},{10,18},{18,26},{... | collective-permute-start | bytes 98312 | tf_op jit(solution)/shard_map/ppermute | solution.py:20
  12.9 3.1 %collective-permute-start.2 = (f32[3,1,4,4,4,128]{5,4,3,2,1,0:T(4,128)S(1)}, f32[3,1,4,4,4,128]{5,4,3,2,1,0:T(4,128)S(1)}, u32[]{:S(2)}, u32[]{:S(2)}) collective-permute-start(f32[3,1,4,4,4,128]{5,4,3,2,1,0:T(4,128)S(1)} %pad_maximum_fusion), channel_id=1, source_target_pairs={{0,1},{1,2},{2,3},{3,4},{4,5},{5,6},{6,7},{8,9},{9,10},{10,11},{11... | collective-permute-start | bytes 294920 | tf_op jit(solution)/shard_map/ppermute | solution.py:20
  17.7 3.7 %collective-permute-done.3 = f32[3,1,4,4,4,128]{5,4,3,2,1,0:T(4,128)S(1)} collective-permute-done((f32[3,1,4,4,4,128]{5,4,3,2,1,0:T(4,128)S(1)}, f32[3,1,4,4,4,128]{5,4,3,2,1,0:T(4,128)S(1)}, u32[]{:S(2)}, u32[]{:S(2)}) %collective-permute-start.3) | collective-permute-done | bytes 98336 | tf_op jit(solution)/shard_map/ppermute | solution.py:21
  22.2 8.3 %constant_dynamic-update-slice_fusion.9 = (f32[24,4,128]{2,1,0:T(4,128)S(1)}, f32[8,4,128]{2,1,0:T(4,128)S(1)}) fusion(f32[8,14,4,128]{3,2,1,0:T(4,128)S(1)} %bitcast.438, f32[1,1,8,14,128,128]{5,4,3,2,1,0:T(8,128)} %param.16, f32[8,128]{1,0:T(8,128)} %bitcast.466, f32[1,1,8,4,128]{4,3,2,1,0:T(4,128)} %param.14), kind=kOutput, calls=%fused_computation.94 | convolution fusion | flops 88113152 | bytes 7622656 | tf_op jit(solution)/shard_map/bkij,bkrj->bri/dot_general | solution.py:37
  31.1 3.3 %collective-permute-start.4 = (f32[1,1,4,4,4,128]{5,4,3,2,1,0:T(4,128)S(1)}, f32[1,1,4,4,4,128]{5,4,3,2,1,0:T(4,128)S(1)}, u32[]{:S(2)}, u32[]{:S(2)}) collective-permute-start(f32[1,1,4,4,4,128]{5,4,3,2,1,0:T(4,128)S(1)} %bitcast.456), channel_id=1, source_target_pairs={{0,8},{8,16},{16,24},{1,9},{9,17},{17,25},{2,10},{10,18},{18,26},{... | collective-permute-start | bytes 98312 | tf_op jit(solution)/shard_map/ppermute | solution.py:20
  36.5 3.2 %collective-permute-done.5 = f32[1,1,4,4,4,128]{5,4,3,2,1,0:T(4,128)S(1)} collective-permute-done((f32[1,1,4,4,4,128]{5,4,3,2,1,0:T(4,128)S(1)}, f32[1,1,4,4,4,128]{5,4,3,2,1,0:T(4,128)S(1)}, u32[]{:S(2)}, u32[]{:S(2)}) %collective-permute-start.5) | collective-permute-done | bytes 32800 | tf_op jit(solution)/shard_map/ppermute | solution.py:21
  39.7 4.0 %collective-permute-start.6 = (f32[3,1,4,4,4,128]{5,4,3,2,1,0:T(4,128)S(1)}, f32[3,1,4,4,4,128]{5,4,3,2,1,0:T(4,128)S(1)}, u32[]{:S(2)}, u32[]{:S(2)}) collective-permute-start(f32[3,1,4,4,4,128]{5,4,3,2,1,0:T(4,128)S(1)} %pad_maximum_fusion.1), channel_id=1, source_target_pairs={{0,1},{1,2},{2,3},{3,4},{4,5},{5,6},{6,7},{8,9},{9,10},{10,11},{11... | collective-permute-start | bytes 294920 | tf_op jit(solution)/shard_map/ppermute | solution.py:20
  45.4 3.7 %collective-permute-done.7 = f32[3,1,4,4,4,128]{5,4,3,2,1,0:T(4,128)S(1)} collective-permute-done((f32[3,1,4,4,4,128]{5,4,3,2,1,0:T(4,128)S(1)}, f32[3,1,4,4,4,128]{5,4,3,2,1,0:T(4,128)S(1)}, u32[]{:S(2)}, u32[]{:S(2)}) %collective-permute-start.7) | collective-permute-done | bytes 98336 | tf_op jit(solution)/shard_map/ppermute | solution.py:21
  49.9 8.2 %fusion.64 = f32[8,4,128]{2,1,0:T(4,128)S(1)} fusion(f32[8,14,4,128]{3,2,1,0:T(4,128)S(1)} %bitcast.440, f32[1,1,8,14,128,128]{5,4,3,2,1,0:T(8,128)} %param.16, f32[1,1,8,4,128]{4,3,2,1,0:T(4,128)S(1)} %copy-done.3, f32[8,4,128]{2,1,0:T(4,128)S(1)} %get-tuple-element.10, f32[8,128]{1,0:T(8,128)S(1)} %bitcast.467), kind=kOutput, calls=%fused_computation.50 | convolution fusion | flops 88092672 | bytes 7622656 | tf_op jit(solution)/shard_map/bkij,bkrj->bri/dot_general | solution.py:37
  59.4 3.3 %collective-permute-start.8 = (f32[1,1,4,2,4,128]{5,4,3,2,1,0:T(4,128)S(1)}, f32[1,1,4,2,4,128]{5,4,3,2,1,0:T(4,128)S(1)}, u32[]{:S(2)}, u32[]{:S(2)}) collective-permute-start(f32[1,1,4,2,4,128]{5,4,3,2,1,0:T(4,128)S(1)} %copy.90), channel_id=1, source_target_pairs={{0,8},{8,16},{16,24},{1,9},{9,17},{17,25},{2,10},{10,18},{18,26},{... | collective-permute-start | bytes 49160 | tf_op jit(solution)/shard_map/ppermute | solution.py:20
  64.7 3.1 %collective-permute-done.9 = f32[1,1,4,2,4,128]{5,4,3,2,1,0:T(4,128)S(1)} collective-permute-done((f32[1,1,4,2,4,128]{5,4,3,2,1,0:T(4,128)S(1)}, f32[1,1,4,2,4,128]{5,4,3,2,1,0:T(4,128)S(1)}, u32[]{:S(2)}, u32[]{:S(2)}) %collective-permute-start.9) | collective-permute-done | bytes 16416 | tf_op jit(solution)/shard_map/ppermute | solution.py:21
  67.8 3.1 %collective-permute-start.10 = (f32[3,1,4,2,4,128]{5,4,3,2,1,0:T(4,128)S(1)}, f32[3,1,4,2,4,128]{5,4,3,2,1,0:T(4,128)S(1)}, u32[]{:S(2)}, u32[]{:S(2)}) collective-permute-start(f32[3,1,4,2,4,128]{5,4,3,2,1,0:T(4,128)S(1)} %constant_dynamic-update-slice_fusion.10), channel_id=1, source_target_pairs={{0,1},{1,2},{2,3},{3,4},{4,5},{5,6},{6,7},{8,9},{9,10},{10,11},{11... | collective-permute-start | bytes 147464 | tf_op jit(solution)/shard_map/ppermute | solution.py:20
  72.3 3.5 %collective-permute-done.11 = f32[3,1,4,2,4,128]{5,4,3,2,1,0:T(4,128)S(1)} collective-permute-done((f32[3,1,4,2,4,128]{5,4,3,2,1,0:T(4,128)S(1)}, f32[3,1,4,2,4,128]{5,4,3,2,1,0:T(4,128)S(1)}, u32[]{:S(2)}, u32[]{:S(2)}) %collective-permute-start.11) | collective-permute-done | bytes 49184 | tf_op jit(solution)/shard_map/ppermute | solution.py:21
  78.7 3.4 %collective-permute-start.12 = (f32[1,1,4,2,4,128]{5,4,3,2,1,0:T(4,128)S(1)}, f32[1,1,4,2,4,128]{5,4,3,2,1,0:T(4,128)S(1)}, u32[]{:S(2)}, u32[]{:S(2)}) collective-permute-start(f32[1,1,4,2,4,128]{5,4,3,2,1,0:T(4,128)S(1)} %copy.95), channel_id=1, source_target_pairs={{0,8},{8,16},{16,24},{1,9},{9,17},{17,25},{2,10},{10,18},{18,26},{... | collective-permute-start | bytes 49160 | tf_op jit(solution)/shard_map/ppermute | solution.py:20
  84.0 3.1 %collective-permute-done.13 = f32[1,1,4,2,4,128]{5,4,3,2,1,0:T(4,128)S(1)} collective-permute-done((f32[1,1,4,2,4,128]{5,4,3,2,1,0:T(4,128)S(1)}, f32[1,1,4,2,4,128]{5,4,3,2,1,0:T(4,128)S(1)}, u32[]{:S(2)}, u32[]{:S(2)}) %collective-permute-start.13) | collective-permute-done | bytes 16416 | tf_op jit(solution)/shard_map/ppermute | solution.py:21
  87.1 4.0 %collective-permute-start.14 = (f32[3,1,4,2,4,128]{5,4,3,2,1,0:T(4,128)S(1)}, f32[3,1,4,2,4,128]{5,4,3,2,1,0:T(4,128)S(1)}, u32[]{:S(2)}, u32[]{:S(2)}) collective-permute-start(f32[3,1,4,2,4,128]{5,4,3,2,1,0:T(4,128)S(1)} %constant_dynamic-update-slice_fusion.18), channel_id=1, source_target_pairs={{0,1},{1,2},{2,3},{3,4},{4,5},{5,6},{6,7},{8,9},{9,10},{10,11},{11... | collective-permute-start | bytes 147464 | tf_op jit(solution)/shard_map/ppermute | solution.py:20
  92.5 3.5 %collective-permute-done.15 = f32[3,1,4,2,4,128]{5,4,3,2,1,0:T(4,128)S(1)} collective-permute-done((f32[3,1,4,2,4,128]{5,4,3,2,1,0:T(4,128)S(1)}, f32[3,1,4,2,4,128]{5,4,3,2,1,0:T(4,128)S(1)}, u32[]{:S(2)}, u32[]{:S(2)}) %collective-permute-start.15) | collective-permute-done | bytes 49184 | tf_op jit(solution)/shard_map/ppermute | solution.py:21
  98.7 39.2 %psum.7 = f32[4,1024]{1,0:T(4,128)S(1)} all-reduce(f32[4,1024]{1,0:T(4,128)S(1)} %bitcast.470), channel_id=1, replica_groups=mesh['row'=4,'col'=8] {'row','col'}, use_global_device_ids=true, to_apply=%region_0.0 | all-reduce | flops 4096 | bytes 32768 | tf_op jit(solution)/shard_map/psum | solution.py:81
  138.1 61.0 %all-gather = f32[32,32,4]{1,2,0:T(4,128)S(1)} all-gather(f32[1,32,4]{1,2,0:T(4,128)S(1)} %convolution_bitcast_fusion.1), channel_id=1, replica_groups=mesh['row'=4,'col'=8] {'row','col'}, dimensions={0}, use_global_device_ids=true | all-gather | bytes 16896 | tf_op jit(solution)/shard_map/all_gather | solution.py:83
  200.3 8.7 %collective-permute-start.16 = (f32[1,1,4,2,4,128]{5,4,3,2,1,0:T(4,128)S(1)}, f32[1,1,4,2,4,128]{5,4,3,2,1,0:T(4,128)S(1)}, u32[]{:S(2)}, u32[]{:S(2)}) collective-permute-start(f32[1,1,4,2,4,128]{5,4,3,2,1,0:T(4,128)S(1)} %copy.103), channel_id=1, source_target_pairs={{0,8},{8,16},{16,24},{1,9},{9,17},{17,25},{2,10},{10,18},{18,26},{... | collective-permute-start | bytes 49160 | tf_op jit(solution)/shard_map/ppermute | solution.py:20
  214.1 3.4 %collective-permute-start.18 = (f32[3,1,4,2,4,128]{5,4,3,2,1,0:T(4,128)S(1)}, f32[3,1,4,2,4,128]{5,4,3,2,1,0:T(4,128)S(1)}, u32[]{:S(2)}, u32[]{:S(2)}) collective-permute-start(f32[3,1,4,2,4,128]{5,4,3,2,1,0:T(4,128)S(1)} %constant_dynamic-update-slice_fusion.26), channel_id=1, source_target_pairs={{0,1},{1,2},{2,3},{3,4},{4,5},{5,6},{6,7},{8,9},{9,10},{10,11},{11... | collective-permute-start | bytes 147464 | tf_op jit(solution)/shard_map/ppermute | solution.py:20
  218.8 3.5 %collective-permute-done.19 = f32[3,1,4,2,4,128]{5,4,3,2,1,0:T(4,128)S(1)} collective-permute-done((f32[3,1,4,2,4,128]{5,4,3,2,1,0:T(4,128)S(1)}, f32[3,1,4,2,4,128]{5,4,3,2,1,0:T(4,128)S(1)}, u32[]{:S(2)}, u32[]{:S(2)}) %collective-permute-start.19) | collective-permute-done | bytes 49184 | tf_op jit(solution)/shard_map/ppermute | solution.py:21
  225.1 3.4 %collective-permute-start.20 = (f32[1,1,4,2,4,128]{5,4,3,2,1,0:T(4,128)S(1)}, f32[1,1,4,2,4,128]{5,4,3,2,1,0:T(4,128)S(1)}, u32[]{:S(2)}, u32[]{:S(2)}) collective-permute-start(f32[1,1,4,2,4,128]{5,4,3,2,1,0:T(4,128)S(1)} %copy.108), channel_id=1, source_target_pairs={{0,8},{8,16},{16,24},{1,9},{9,17},{17,25},{2,10},{10,18},{18,26},{... | collective-permute-start | bytes 49160 | tf_op jit(solution)/shard_map/ppermute | solution.py:20
  237.4 3.5 %collective-permute-done.23 = f32[3,1,4,2,4,128]{5,4,3,2,1,0:T(4,128)S(1)} collective-permute-done((f32[3,1,4,2,4,128]{5,4,3,2,1,0:T(4,128)S(1)}, f32[3,1,4,2,4,128]{5,4,3,2,1,0:T(4,128)S(1)}, u32[]{:S(2)}, u32[]{:S(2)}) %collective-permute-start.23) | collective-permute-done | bytes 49184 | tf_op jit(solution)/shard_map/ppermute | solution.py:21
  244.9 3.4 %collective-permute-start.24 = (f32[1,1,4,4,4,128]{5,4,3,2,1,0:T(4,128)S(1)}, f32[1,1,4,4,4,128]{5,4,3,2,1,0:T(4,128)S(1)}, u32[]{:S(2)}, u32[]{:S(2)}) collective-permute-start(f32[1,1,4,4,4,128]{5,4,3,2,1,0:T(4,128)S(1)} %bitcast.462), channel_id=1, source_target_pairs={{0,8},{8,16},{16,24},{1,9},{9,17},{17,25},{2,10},{10,18},{18,26},{... | collective-permute-start | bytes 98312 | tf_op jit(solution)/shard_map/ppermute | solution.py:20
  250.2 3.3 %collective-permute-done.25 = f32[1,1,4,4,4,128]{5,4,3,2,1,0:T(4,128)S(1)} collective-permute-done((f32[1,1,4,4,4,128]{5,4,3,2,1,0:T(4,128)S(1)}, f32[1,1,4,4,4,128]{5,4,3,2,1,0:T(4,128)S(1)}, u32[]{:S(2)}, u32[]{:S(2)}) %collective-permute-start.25) | collective-permute-done | bytes 32800 | tf_op jit(solution)/shard_map/ppermute | solution.py:21
  257.7 3.7 %collective-permute-done.27 = f32[3,1,4,4,4,128]{5,4,3,2,1,0:T(4,128)S(1)} collective-permute-done((f32[3,1,4,4,4,128]{5,4,3,2,1,0:T(4,128)S(1)}, f32[3,1,4,4,4,128]{5,4,3,2,1,0:T(4,128)S(1)}, u32[]{:S(2)}, u32[]{:S(2)}) %collective-permute-start.27) | collective-permute-done | bytes 98336 | tf_op jit(solution)/shard_map/ppermute | solution.py:21
  262.2 8.2 %constant_dynamic-update-slice_fusion.51 = (f32[24,4,128]{2,1,0:T(4,128)S(1)}, f32[8,4,128]{2,1,0:T(4,128)S(1)}) fusion(f32[8,4,128]{2,1,0:T(4,128)S(1)} %get-tuple-element.18, f32[8,14,4,128]{3,2,1,0:T(4,128)S(1)} %bitcast.437, f32[1,1,8,14,128,128]{5,4,3,2,1,0:T(8,128)} %param.16, f32[8,128]{1,0:T(8,128)S(1)} %bitcast.468, ...), kind=kOutput, calls=%fused_computation.136 | convolution fusion | flops 88104960 | bytes 7639040 | tf_op jit(solution)/shard_map/bkij,bkrj->bri/dot_general | solution.py:37
  271.0 3.3 %collective-permute-start.28 = (f32[1,1,4,4,4,128]{5,4,3,2,1,0:T(4,128)S(1)}, f32[1,1,4,4,4,128]{5,4,3,2,1,0:T(4,128)S(1)}, u32[]{:S(2)}, u32[]{:S(2)}) collective-permute-start(f32[1,1,4,4,4,128]{5,4,3,2,1,0:T(4,128)S(1)} %bitcast.459), channel_id=1, source_target_pairs={{0,8},{8,16},{16,24},{1,9},{9,17},{17,25},{2,10},{10,18},{18,26},{... | collective-permute-start | bytes 98312 | tf_op jit(solution)/shard_map/ppermute | solution.py:20
  276.3 3.3 %collective-permute-done.29 = f32[1,1,4,4,4,128]{5,4,3,2,1,0:T(4,128)S(1)} collective-permute-done((f32[1,1,4,4,4,128]{5,4,3,2,1,0:T(4,128)S(1)}, f32[1,1,4,4,4,128]{5,4,3,2,1,0:T(4,128)S(1)}, u32[]{:S(2)}, u32[]{:S(2)}) %collective-permute-start.29) | collective-permute-done | bytes 32800 | tf_op jit(solution)/shard_map/ppermute | solution.py:21
  283.8 3.7 %collective-permute-done.31 = f32[3,1,4,4,4,128]{5,4,3,2,1,0:T(4,128)S(1)} collective-permute-done((f32[3,1,4,4,4,128]{5,4,3,2,1,0:T(4,128)S(1)}, f32[3,1,4,4,4,128]{5,4,3,2,1,0:T(4,128)S(1)}, u32[]{:S(2)}, u32[]{:S(2)}) %collective-permute-start.31) | collective-permute-done | bytes 98336 | tf_op jit(solution)/shard_map/ppermute | solution.py:21
  288.3 8.8 %fusion.43 = f32[1,1,8,4,128]{4,3,2,1,0:T(4,128)} fusion(f32[8,4,128]{2,1,0:T(4,128)S(1)} %get-tuple-element.20, f32[8,14,4,128]{3,2,1,0:T(4,128)S(1)} %bitcast.439, f32[1,1,8,14,128,128]{5,4,3,2,1,0:T(8,128)} %param.16, f32[1,1,8,4,128]{4,3,2,1,0:T(4,128)S(1)} %copy-done.3, f32[8,128]{1,0:T(8,128)S(1)} %bitcast.469), kind=kOutput, calls=%fused_computation.43 | convolution fusion | flops 88104960 | bytes 7622656 | tf_op jit(solution)/shard_map/bkij,bkrj->bri/dot_general | solution.py:37
  (160 shorter events, 66.7 us)
Async XLA Ops:
  3.1 7.2 %collective-permute-start = (f32[1,1,4,4,4,128]{5,4,3,2,1,0:T(4,128)S(1)}, f32[1,1,4,4,4,128]{5,4,3,2,1,0:T(4,128)S(1)}, u32[]{:S(2)}, u32[]{:S(2)}) collective-permute-start(f32[1,1,4,4,4,128]{5,4,3,2,1,0:T(4,128)S(1)} %bitcast.453), channel_id=1, source_target_pairs={{0,8},{8,16},{16,24},{1,9},{9,17},{17,25},{2,10},{10,18},{18,26},{... | collective-permute-start | bytes 98312 | tf_op jit(solution)/shard_map/ppermute | solution.py:20
  7.6 5.2 %collective-permute-start.1 = (f32[1,1,4,4,4,128]{5,4,3,2,1,0:T(4,128)S(1)}, f32[1,1,4,4,4,128]{5,4,3,2,1,0:T(4,128)S(1)}, u32[]{:S(2)}, u32[]{:S(2)}) collective-permute-start(f32[1,1,4,4,4,128]{5,4,3,2,1,0:T(4,128)S(1)} %bitcast.454), channel_id=1, source_target_pairs={{8,0},{16,8},{24,16},{9,1},{17,9},{25,17},{10,2},{18,10},{26,18},{... | collective-permute-start | bytes 98312 | tf_op jit(solution)/shard_map/ppermute | solution.py:21
  12.9 4.8 %collective-permute-start.2 = (f32[3,1,4,4,4,128]{5,4,3,2,1,0:T(4,128)S(1)}, f32[3,1,4,4,4,128]{5,4,3,2,1,0:T(4,128)S(1)}, u32[]{:S(2)}, u32[]{:S(2)}) collective-permute-start(f32[3,1,4,4,4,128]{5,4,3,2,1,0:T(4,128)S(1)} %pad_maximum_fusion), channel_id=1, source_target_pairs={{0,1},{1,2},{2,3},{3,4},{4,5},{5,6},{6,7},{8,9},{9,10},{10,11},{11... | collective-permute-start | bytes 294920 | tf_op jit(solution)/shard_map/ppermute | solution.py:20
  16.1 5.4 %collective-permute-start.3 = (f32[3,1,4,4,4,128]{5,4,3,2,1,0:T(4,128)S(1)}, f32[3,1,4,4,4,128]{5,4,3,2,1,0:T(4,128)S(1)}, u32[]{:S(2)}, u32[]{:S(2)}) collective-permute-start(f32[3,1,4,4,4,128]{5,4,3,2,1,0:T(4,128)S(1)} %pad_maximum_fusion), channel_id=1, source_target_pairs={{1,0},{2,1},{3,2},{4,3},{5,4},{6,5},{7,6},{9,8},{10,9},{11,10},{12... | collective-permute-start | bytes 294920 | tf_op jit(solution)/shard_map/ppermute | solution.py:21
  31.1 5.4 %collective-permute-start.4 = (f32[1,1,4,4,4,128]{5,4,3,2,1,0:T(4,128)S(1)}, f32[1,1,4,4,4,128]{5,4,3,2,1,0:T(4,128)S(1)}, u32[]{:S(2)}, u32[]{:S(2)}) collective-permute-start(f32[1,1,4,4,4,128]{5,4,3,2,1,0:T(4,128)S(1)} %bitcast.456), channel_id=1, source_target_pairs={{0,8},{8,16},{16,24},{1,9},{9,17},{17,25},{2,10},{10,18},{18,26},{... | collective-permute-start | bytes 98312 | tf_op jit(solution)/shard_map/ppermute | solution.py:20
  34.5 5.2 %collective-permute-start.5 = (f32[1,1,4,4,4,128]{5,4,3,2,1,0:T(4,128)S(1)}, f32[1,1,4,4,4,128]{5,4,3,2,1,0:T(4,128)S(1)}, u32[]{:S(2)}, u32[]{:S(2)}) collective-permute-start(f32[1,1,4,4,4,128]{5,4,3,2,1,0:T(4,128)S(1)} %bitcast.457), channel_id=1, source_target_pairs={{8,0},{16,8},{24,16},{9,1},{17,9},{25,17},{10,2},{18,10},{26,18},{... | collective-permute-start | bytes 98312 | tf_op jit(solution)/shard_map/ppermute | solution.py:21
  39.7 5.7 %collective-permute-start.6 = (f32[3,1,4,4,4,128]{5,4,3,2,1,0:T(4,128)S(1)}, f32[3,1,4,4,4,128]{5,4,3,2,1,0:T(4,128)S(1)}, u32[]{:S(2)}, u32[]{:S(2)}) collective-permute-start(f32[3,1,4,4,4,128]{5,4,3,2,1,0:T(4,128)S(1)} %pad_maximum_fusion.1), channel_id=1, source_target_pairs={{0,1},{1,2},{2,3},{3,4},{4,5},{5,6},{6,7},{8,9},{9,10},{10,11},{11... | collective-permute-start | bytes 294920 | tf_op jit(solution)/shard_map/ppermute | solution.py:20
  43.8 5.4 %collective-permute-start.7 = (f32[3,1,4,4,4,128]{5,4,3,2,1,0:T(4,128)S(1)}, f32[3,1,4,4,4,128]{5,4,3,2,1,0:T(4,128)S(1)}, u32[]{:S(2)}, u32[]{:S(2)}) collective-permute-start(f32[3,1,4,4,4,128]{5,4,3,2,1,0:T(4,128)S(1)} %pad_maximum_fusion.1), channel_id=1, source_target_pairs={{1,0},{2,1},{3,2},{4,3},{5,4},{6,5},{7,6},{9,8},{10,9},{11,10},{12... | collective-permute-start | bytes 294920 | tf_op jit(solution)/shard_map/ppermute | solution.py:21
  59.4 5.3 %collective-permute-start.8 = (f32[1,1,4,2,4,128]{5,4,3,2,1,0:T(4,128)S(1)}, f32[1,1,4,2,4,128]{5,4,3,2,1,0:T(4,128)S(1)}, u32[]{:S(2)}, u32[]{:S(2)}) collective-permute-start(f32[1,1,4,2,4,128]{5,4,3,2,1,0:T(4,128)S(1)} %copy.90), channel_id=1, source_target_pairs={{0,8},{8,16},{16,24},{1,9},{9,17},{17,25},{2,10},{10,18},{18,26},{... | collective-permute-start | bytes 49160 | tf_op jit(solution)/shard_map/ppermute | solution.py:20
  62.8 5.1 %collective-permute-start.9 = (f32[1,1,4,2,4,128]{5,4,3,2,1,0:T(4,128)S(1)}, f32[1,1,4,2,4,128]{5,4,3,2,1,0:T(4,128)S(1)}, u32[]{:S(2)}, u32[]{:S(2)}) collective-permute-start(f32[1,1,4,2,4,128]{5,4,3,2,1,0:T(4,128)S(1)} %copy.90), channel_id=1, source_target_pairs={{8,0},{16,8},{24,16},{9,1},{17,9},{25,17},{10,2},{18,10},{26,18},{... | collective-permute-start | bytes 49160 | tf_op jit(solution)/shard_map/ppermute | solution.py:21
  67.8 4.5 %collective-permute-start.10 = (f32[3,1,4,2,4,128]{5,4,3,2,1,0:T(4,128)S(1)}, f32[3,1,4,2,4,128]{5,4,3,2,1,0:T(4,128)S(1)}, u32[]{:S(2)}, u32[]{:S(2)}) collective-permute-start(f32[3,1,4,2,4,128]{5,4,3,2,1,0:T(4,128)S(1)} %constant_dynamic-update-slice_fusion.10), channel_id=1, source_target_pairs={{0,1},{1,2},{2,3},{3,4},{4,5},{5,6},{6,7},{8,9},{9,10},{10,11},{11... | collective-permute-start | bytes 147464 | tf_op jit(solution)/shard_map/ppermute | solution.py:20
  71.0 4.8 %collective-permute-start.11 = (f32[3,1,4,2,4,128]{5,4,3,2,1,0:T(4,128)S(1)}, f32[3,1,4,2,4,128]{5,4,3,2,1,0:T(4,128)S(1)}, u32[]{:S(2)}, u32[]{:S(2)}) collective-permute-start(f32[3,1,4,2,4,128]{5,4,3,2,1,0:T(4,128)S(1)} %constant_dynamic-update-slice_fusion.10), channel_id=1, source_target_pairs={{1,0},{2,1},{3,2},{4,3},{5,4},{6,5},{7,6},{9,8},{10,9},{11,10},{12... | collective-permute-start | bytes 147464 | tf_op jit(solution)/shard_map/ppermute | solution.py:21
  78.7 5.3 %collective-permute-start.12 = (f32[1,1,4,2,4,128]{5,4,3,2,1,0:T(4,128)S(1)}, f32[1,1,4,2,4,128]{5,4,3,2,1,0:T(4,128)S(1)}, u32[]{:S(2)}, u32[]{:S(2)}) collective-permute-start(f32[1,1,4,2,4,128]{5,4,3,2,1,0:T(4,128)S(1)} %copy.95), channel_id=1, source_target_pairs={{0,8},{8,16},{16,24},{1,9},{9,17},{17,25},{2,10},{10,18},{18,26},{... | collective-permute-start | bytes 49160 | tf_op jit(solution)/shard_map/ppermute | solution.py:20
  82.0 5.1 %collective-permute-start.13 = (f32[1,1,4,2,4,128]{5,4,3,2,1,0:T(4,128)S(1)}, f32[1,1,4,2,4,128]{5,4,3,2,1,0:T(4,128)S(1)}, u32[]{:S(2)}, u32[]{:S(2)}) collective-permute-start(f32[1,1,4,2,4,128]{5,4,3,2,1,0:T(4,128)S(1)} %copy.95), channel_id=1, source_target_pairs={{8,0},{16,8},{24,16},{9,1},{17,9},{25,17},{10,2},{18,10},{26,18},{... | collective-permute-start | bytes 49160 | tf_op jit(solution)/shard_map/ppermute | solution.py:21
  87.1 5.4 %collective-permute-start.14 = (f32[3,1,4,2,4,128]{5,4,3,2,1,0:T(4,128)S(1)}, f32[3,1,4,2,4,128]{5,4,3,2,1,0:T(4,128)S(1)}, u32[]{:S(2)}, u32[]{:S(2)}) collective-permute-start(f32[3,1,4,2,4,128]{5,4,3,2,1,0:T(4,128)S(1)} %constant_dynamic-update-slice_fusion.18), channel_id=1, source_target_pairs={{0,1},{1,2},{2,3},{3,4},{4,5},{5,6},{6,7},{8,9},{9,10},{10,11},{11... | collective-permute-start | bytes 147464 | tf_op jit(solution)/shard_map/ppermute | solution.py:20
  91.1 4.8 %collective-permute-start.15 = (f32[3,1,4,2,4,128]{5,4,3,2,1,0:T(4,128)S(1)}, f32[3,1,4,2,4,128]{5,4,3,2,1,0:T(4,128)S(1)}, u32[]{:S(2)}, u32[]{:S(2)}) collective-permute-start(f32[3,1,4,2,4,128]{5,4,3,2,1,0:T(4,128)S(1)} %constant_dynamic-update-slice_fusion.18), channel_id=1, source_target_pairs={{1,0},{2,1},{3,2},{4,3},{5,4},{6,5},{7,6},{9,8},{10,9},{11,10},{12... | collective-permute-start | bytes 147464 | tf_op jit(solution)/shard_map/ppermute | solution.py:21
  200.3 10.6 %collective-permute-start.16 = (f32[1,1,4,2,4,128]{5,4,3,2,1,0:T(4,128)S(1)}, f32[1,1,4,2,4,128]{5,4,3,2,1,0:T(4,128)S(1)}, u32[]{:S(2)}, u32[]{:S(2)}) collective-permute-start(f32[1,1,4,2,4,128]{5,4,3,2,1,0:T(4,128)S(1)} %copy.103), channel_id=1, source_target_pairs={{0,8},{8,16},{16,24},{1,9},{9,17},{17,25},{2,10},{10,18},{18,26},{... | collective-permute-start | bytes 49160 | tf_op jit(solution)/shard_map/ppermute | solution.py:20
  209.0 5.1 %collective-permute-start.17 = (f32[1,1,4,2,4,128]{5,4,3,2,1,0:T(4,128)S(1)}, f32[1,1,4,2,4,128]{5,4,3,2,1,0:T(4,128)S(1)}, u32[]{:S(2)}, u32[]{:S(2)}) collective-permute-start(f32[1,1,4,2,4,128]{5,4,3,2,1,0:T(4,128)S(1)} %copy.103), channel_id=1, source_target_pairs={{8,0},{16,8},{24,16},{9,1},{17,9},{25,17},{10,2},{18,10},{26,18},{... | collective-permute-start | bytes 49160 | tf_op jit(solution)/shard_map/ppermute | solution.py:21
  214.1 4.7 %collective-permute-start.18 = (f32[3,1,4,2,4,128]{5,4,3,2,1,0:T(4,128)S(1)}, f32[3,1,4,2,4,128]{5,4,3,2,1,0:T(4,128)S(1)}, u32[]{:S(2)}, u32[]{:S(2)}) collective-permute-start(f32[3,1,4,2,4,128]{5,4,3,2,1,0:T(4,128)S(1)} %constant_dynamic-update-slice_fusion.26), channel_id=1, source_target_pairs={{0,1},{1,2},{2,3},{3,4},{4,5},{5,6},{6,7},{8,9},{9,10},{10,11},{11... | collective-permute-start | bytes 147464 | tf_op jit(solution)/shard_map/ppermute | solution.py:20
  217.5 4.8 %collective-permute-start.19 = (f32[3,1,4,2,4,128]{5,4,3,2,1,0:T(4,128)S(1)}, f32[3,1,4,2,4,128]{5,4,3,2,1,0:T(4,128)S(1)}, u32[]{:S(2)}, u32[]{:S(2)}) collective-permute-start(f32[3,1,4,2,4,128]{5,4,3,2,1,0:T(4,128)S(1)} %constant_dynamic-update-slice_fusion.26), channel_id=1, source_target_pairs={{1,0},{2,1},{3,2},{4,3},{5,4},{6,5},{7,6},{9,8},{10,9},{11,10},{12... | collective-permute-start | bytes 147464 | tf_op jit(solution)/shard_map/ppermute | solution.py:21
  225.1 5.3 %collective-permute-start.20 = (f32[1,1,4,2,4,128]{5,4,3,2,1,0:T(4,128)S(1)}, f32[1,1,4,2,4,128]{5,4,3,2,1,0:T(4,128)S(1)}, u32[]{:S(2)}, u32[]{:S(2)}) collective-permute-start(f32[1,1,4,2,4,128]{5,4,3,2,1,0:T(4,128)S(1)} %copy.108), channel_id=1, source_target_pairs={{0,8},{8,16},{16,24},{1,9},{9,17},{17,25},{2,10},{10,18},{18,26},{... | collective-permute-start | bytes 49160 | tf_op jit(solution)/shard_map/ppermute | solution.py:20
  228.5 5.1 %collective-permute-start.21 = (f32[1,1,4,2,4,128]{5,4,3,2,1,0:T(4,128)S(1)}, f32[1,1,4,2,4,128]{5,4,3,2,1,0:T(4,128)S(1)}, u32[]{:S(2)}, u32[]{:S(2)}) collective-permute-start(f32[1,1,4,2,4,128]{5,4,3,2,1,0:T(4,128)S(1)} %copy.108), channel_id=1, source_target_pairs={{8,0},{16,8},{24,16},{9,1},{17,9},{25,17},{10,2},{18,10},{26,18},{... | collective-permute-start | bytes 49160 | tf_op jit(solution)/shard_map/ppermute | solution.py:21
  233.6 3.9 %collective-permute-start.22 = (f32[3,1,4,2,4,128]{5,4,3,2,1,0:T(4,128)S(1)}, f32[3,1,4,2,4,128]{5,4,3,2,1,0:T(4,128)S(1)}, u32[]{:S(2)}, u32[]{:S(2)}) collective-permute-start(f32[3,1,4,2,4,128]{5,4,3,2,1,0:T(4,128)S(1)} %constant_dynamic-update-slice_fusion.34), channel_id=1, source_target_pairs={{0,1},{1,2},{2,3},{3,4},{4,5},{5,6},{6,7},{8,9},{9,10},{10,11},{11... | collective-permute-start | bytes 147464 | tf_op jit(solution)/shard_map/ppermute | solution.py:20
  236.1 4.8 %collective-permute-start.23 = (f32[3,1,4,2,4,128]{5,4,3,2,1,0:T(4,128)S(1)}, f32[3,1,4,2,4,128]{5,4,3,2,1,0:T(4,128)S(1)}, u32[]{:S(2)}, u32[]{:S(2)}) collective-permute-start(f32[3,1,4,2,4,128]{5,4,3,2,1,0:T(4,128)S(1)} %constant_dynamic-update-slice_fusion.34), channel_id=1, source_target_pairs={{1,0},{2,1},{3,2},{4,3},{5,4},{6,5},{7,6},{9,8},{10,9},{11,10},{12... | collective-permute-start | bytes 147464 | tf_op jit(solution)/shard_map/ppermute | solution.py:21
  244.9 5.3 %collective-permute-start.24 = (f32[1,1,4,4,4,128]{5,4,3,2,1,0:T(4,128)S(1)}, f32[1,1,4,4,4,128]{5,4,3,2,1,0:T(4,128)S(1)}, u32[]{:S(2)}, u32[]{:S(2)}) collective-permute-start(f32[1,1,4,4,4,128]{5,4,3,2,1,0:T(4,128)S(1)} %bitcast.462), channel_id=1, source_target_pairs={{0,8},{8,16},{16,24},{1,9},{9,17},{17,25},{2,10},{10,18},{18,26},{... | collective-permute-start | bytes 98312 | tf_op jit(solution)/shard_map/ppermute | solution.py:20
  248.3 5.2 %collective-permute-start.25 = (f32[1,1,4,4,4,128]{5,4,3,2,1,0:T(4,128)S(1)}, f32[1,1,4,4,4,128]{5,4,3,2,1,0:T(4,128)S(1)}, u32[]{:S(2)}, u32[]{:S(2)}) collective-permute-start(f32[1,1,4,4,4,128]{5,4,3,2,1,0:T(4,128)S(1)} %bitcast.463), channel_id=1, source_target_pairs={{8,0},{16,8},{24,16},{9,1},{17,9},{25,17},{10,2},{18,10},{26,18},{... | collective-permute-start | bytes 98312 | tf_op jit(solution)/shard_map/ppermute | solution.py:21
  253.5 4.2 %collective-permute-start.26 = (f32[3,1,4,4,4,128]{5,4,3,2,1,0:T(4,128)S(1)}, f32[3,1,4,4,4,128]{5,4,3,2,1,0:T(4,128)S(1)}, u32[]{:S(2)}, u32[]{:S(2)}) collective-permute-start(f32[3,1,4,4,4,128]{5,4,3,2,1,0:T(4,128)S(1)} %pad_maximum_fusion.2), channel_id=1, source_target_pairs={{0,1},{1,2},{2,3},{3,4},{4,5},{5,6},{6,7},{8,9},{9,10},{10,11},{11... | collective-permute-start | bytes 294920 | tf_op jit(solution)/shard_map/ppermute | solution.py:20
  256.1 5.4 %collective-permute-start.27 = (f32[3,1,4,4,4,128]{5,4,3,2,1,0:T(4,128)S(1)}, f32[3,1,4,4,4,128]{5,4,3,2,1,0:T(4,128)S(1)}, u32[]{:S(2)}, u32[]{:S(2)}) collective-permute-start(f32[3,1,4,4,4,128]{5,4,3,2,1,0:T(4,128)S(1)} %pad_maximum_fusion.2), channel_id=1, source_target_pairs={{1,0},{2,1},{3,2},{4,3},{5,4},{6,5},{7,6},{9,8},{10,9},{11,10},{12... | collective-permute-start | bytes 294920 | tf_op jit(solution)/shard_map/ppermute | solution.py:21
  271.0 5.3 %collective-permute-start.28 = (f32[1,1,4,4,4,128]{5,4,3,2,1,0:T(4,128)S(1)}, f32[1,1,4,4,4,128]{5,4,3,2,1,0:T(4,128)S(1)}, u32[]{:S(2)}, u32[]{:S(2)}) collective-permute-start(f32[1,1,4,4,4,128]{5,4,3,2,1,0:T(4,128)S(1)} %bitcast.459), channel_id=1, source_target_pairs={{0,8},{8,16},{16,24},{1,9},{9,17},{17,25},{2,10},{10,18},{18,26},{... | collective-permute-start | bytes 98312 | tf_op jit(solution)/shard_map/ppermute | solution.py:20
  274.4 5.2 %collective-permute-start.29 = (f32[1,1,4,4,4,128]{5,4,3,2,1,0:T(4,128)S(1)}, f32[1,1,4,4,4,128]{5,4,3,2,1,0:T(4,128)S(1)}, u32[]{:S(2)}, u32[]{:S(2)}) collective-permute-start(f32[1,1,4,4,4,128]{5,4,3,2,1,0:T(4,128)S(1)} %bitcast.460), channel_id=1, source_target_pairs={{8,0},{16,8},{24,16},{9,1},{17,9},{25,17},{10,2},{18,10},{26,18},{... | collective-permute-start | bytes 98312 | tf_op jit(solution)/shard_map/ppermute | solution.py:21
  279.6 4.2 %collective-permute-start.30 = (f32[3,1,4,4,4,128]{5,4,3,2,1,0:T(4,128)S(1)}, f32[3,1,4,4,4,128]{5,4,3,2,1,0:T(4,128)S(1)}, u32[]{:S(2)}, u32[]{:S(2)}) collective-permute-start(f32[3,1,4,4,4,128]{5,4,3,2,1,0:T(4,128)S(1)} %pad_maximum_fusion.3), channel_id=1, source_target_pairs={{0,1},{1,2},{2,3},{3,4},{4,5},{5,6},{6,7},{8,9},{9,10},{10,11},{11... | collective-permute-start | bytes 294920 | tf_op jit(solution)/shard_map/ppermute | solution.py:20
  282.2 5.4 %collective-permute-start.31 = (f32[3,1,4,4,4,128]{5,4,3,2,1,0:T(4,128)S(1)}, f32[3,1,4,4,4,128]{5,4,3,2,1,0:T(4,128)S(1)}, u32[]{:S(2)}, u32[]{:S(2)}) collective-permute-start(f32[3,1,4,4,4,128]{5,4,3,2,1,0:T(4,128)S(1)} %pad_maximum_fusion.3), channel_id=1, source_target_pairs={{1,0},{2,1},{3,2},{4,3},{5,4},{6,5},{7,6},{9,8},{10,9},{11,10},{12... | collective-permute-start | bytes 294920 | tf_op jit(solution)/shard_map/ppermute | solution.py:21
  (10 other events, 564.7 us)
where the time goes:
time: 298 us; the launch traced here: 297 us
  blocking collectives  100 us (34%)
  starting transfers between devices  84.3 us (28%)
  waiting for transfers between devices  54.8 us (18%)
  matrix products  43 us (14%)
  local copies, waits for them, and re-layouts  11 us (4%)
  other arithmetic  3.06 us (1%)
    all_gather x1, blocking collectives, on_device(): coarse_x = lax.all_gather(own_rows, ('row', 'col'), axis=1, tiled=True)  61 us
    ppermute x16, starting transfers between devices, padded_2(): before = lax.ppermute(last, axis, up)  58.6 us
    ppermute x16, waiting for transfers between devices, padded_2(): after = lax.ppermute(leading, axis, down)  53.6 us
    dot_general x8, matrix products, apply_op(): coupled = jnp.einsum('bkij,bkrj->bri', blocks, nearby, precision=HIGH)  40 us
    psum x1, blocking collectives, on_device(): coarse_rhs = lax.psum(term, ('row', 'col'))  39.2 us
    ppermute x16, starting transfers between devices, padded_2(): after = lax.ppermute(leading, axis, down)  25.7 us
  transfers between devices with their start and end apart: 32, of which 20 were waited for; matrix products, arithmetic and copies ran while one was open for 0% of the time, Pallas kernels for 0%

commit v1 on v0

v1 whole, which is shorter than its diff:
```python
import jax
import jax.numpy as jnp
from jax import lax
from jax.experimental import pallas as pl
from jax.experimental.pallas import tpu as pltpu
from jax.sharding import PartitionSpec as P


OMEGA = 0.3
AXES = ("row", "col")
F32, BF16 = jnp.float32, jnp.bfloat16
VM = pl.BlockSpec(memory_space=pltpu.VMEM)
SM = pl.BlockSpec(memory_space=pltpu.SMEM)
MIB = 1 << 20

ORDER = ("colb", "rowb", "cola", "rowa")


def partners(rows, cols):
    def flip(i):
        return i + 1 if i % 2 == 0 else i - 1

    def step(i):
        return i + 1 if i % 2 else i - 1

    table = {name: [] for name in ORDER}
    for p in range(rows):
        for q in range(cols):
            inner = 0 <= step(q) < cols
            table["rowa"].append((p * cols + q, flip(p) * cols + q))
            table["rowb"].append((p * cols + q, (step(p) % rows) * cols + q))
            table["cola"].append((p * cols + q, p * cols + flip(q)))
            table["colb"].append((p * cols + q, p * cols + step(q) if inner else flip(p) * cols + q))
    return table


def exchange(sent, table):
    got = {}
    for name in ORDER:
        got[name] = lax.ppermute(sent[name], AXES, table[name])
    return got


def sides():
    p, q = lax.axis_index("row"), lax.axis_index("col")
    rows, cols = lax.axis_size("row"), lax.axis_size("col")
    pp, qq = p % 2, q % 2
    row_in = jnp.logical_and(p > 0, p < rows - 1)
    col_in = jnp.logical_and(q > 0, q < cols - 1)
    yes = p >= 0
    return {
        "rowa": (pp, 1 - pp, yes),
        "rowb": (1 - pp, pp, row_in),
        "cola": (2 + qq, 3 - qq, yes),
        "colb": (3 - qq, 2 + qq, col_in),
    }


def halves(block):
    high = block.astype(BF16).astype(F32)
    low = block - high
    rest = jnp.zeros((16 - 2 * block.shape[0], block.shape[1]), F32)
    return jnp.concatenate([high, low, rest], axis=0).astype(BF16)


def split_weight(weight):
    high = weight.astype(BF16)
    low = (weight - high.astype(F32)).astype(BF16)
    return jnp.concatenate([high, low], axis=1)


def folded(product, loads):
    both = product[:, :128] + product[:, 128:]
    return both[:loads] + both[loads : 2 * loads]


def dot(a, b):
    return jnp.dot(a, b, preferred_element_type=F32)


def fill_ghosts(ext, recv, own, ghosts, loads):
    for name, (_, slot, inside) in sides().items():
        for g in range(ghosts):
            block = recv[name][g * loads : (g + 1) * loads, :]
            block = jnp.where(inside, block, 0.0)
            ext[own + slot * ghosts + g] = halves(block)


def coupled(ext, cols, weights, own, count, loads):
    parts = []
    for b in range(own):
        left = jnp.concatenate([ext[cols[b, k]] for k in range(count)], axis=1)
        parts.append(folded(dot(left, weights[b]), loads))
    return jnp.concatenate(parts, axis=0)


def pack(x_ref, sends, out, ghosts, loads):
    for name, (line, _, _) in sides().items():
        for g in range(ghosts):
            out[name][g * loads : (g + 1) * loads, :] = x_ref[sends[line, g]]


def named(refs):
    return dict(zip(ORDER, refs))


def own_halves(ext, x, own, loads):
    for b in range(own):
        ext[b] = halves(x[b * loads : (b + 1) * loads])


def keep(x3, x, own, loads):
    for b in range(own):
        x3[b] = x[b * loads : (b + 1) * loads]


def spread(diag, own, loads):
    return jnp.concatenate(
        [jnp.broadcast_to(diag[b : b + 1, :], (loads, diag.shape[1])) for b in range(own)], axis=0
    )


def call(body, outs, ins, scratch=(), limit=16):
    return pl.pallas_call(
        body,
        out_shape=[jax.ShapeDtypeStruct(s, d) for s, d in outs],
        in_specs=ins,
        out_specs=[VM] * len(outs),
        scratch_shapes=list(scratch),
        compiler_params=pltpu.CompilerParams(vmem_limit_bytes=limit * MIB),
    )


def on_device(
    rhs, diag0, blocks0, cols0, sends0, pro0, agg0, diag1, blocks1, cols1, sends1, pro1, agg1, cinv
):
    nb, loads, bs = rhs.shape[2:]
    nb1 = diag1.shape[2]
    k0, k1 = cols0.shape[3], cols1.shape[3]
    g0, g1 = sends0.shape[3], sends1.shape[3]
    own_rows, ncu = cinv.shape
    ncb = ncu // bs
    rows, cols_n = lax.axis_size("row"), lax.axis_size("col")
    devices = rows * cols_n
    share = bs // own_rows
    table = partners(rows, cols_n)
    n0, n1 = nb * loads, nb1 * loads
    e0n, e1n = nb + 4 * g0, nb1 + 4 * g1
    r_halo0, r_halo1 = g0 * loads, g1 * loads
    r_pro = g1 * bs
    first_rows = r_halo0 + r_pro + 8

    rhs2 = rhs.reshape(n0, bs)
    d0, d1 = diag0.reshape(nb, bs), diag1.reshape(nb1, bs)
    c0, c1 = cols0.reshape(nb, k0), cols1.reshape(nb1, k1)
    s0, s1 = sends0.reshape(4, g0), sends1.reshape(4, g1)
    a0, a1 = agg0.reshape(nb), agg1.reshape(nb1)
    m0 = blocks0.reshape(nb, k0, bs, bs)
    m1 = blocks1.reshape(nb1, k1, bs, bs)
    p0, p1 = pro0.reshape(nb, bs, bs), pro1.reshape(nb1, bs, bs)
    x3 = pltpu.VMEM((nb, loads, bs), F32)
    y3 = pltpu.VMEM((nb1, loads, bs), F32)
    ext0 = pltpu.VMEM((e0n, 16, bs), BF16)
    ext1 = pltpu.VMEM((e1n, 16, bs), BF16)
    halo0 = [((r_halo0, bs), F32)] * 4
    halo1 = [((r_halo1, bs), F32)] * 4
    vec0, vec1 = ((n0, bs), F32), ((n1, bs), F32)

    def first(rhs_r, d0_r, d1_r, p1_r, s0_r, s1_r, a1_r, x_o, dd_o, di_o, ee_o, ei_o, *rest):
        out, xs = named(rest[:4]), rest[4]
        dd, ee = spread(d0_r[...], nb, loads), spread(d1_r[...], nb1, loads)
        di = OMEGA / dd
        dd_o[...], di_o[...] = dd, di
        ee_o[...], ei_o[...] = ee, OMEGA / ee
        x = rhs_r[...] * di
        x_o[...] = x
        keep(xs, x, nb, loads)
        pack(xs, s0_r, out, g0, loads)
        for name, (line, _, _) in sides().items():
            lines = []
            for g in range(g1):
                pick = s1_r[line, g]
                start = r_halo0 + g * bs
                out[name][start : start + bs, :] = p1_r[pick]
                lines.append(jnp.full((1, bs), a1_r[pick].astype(F32)))
            lines.append(jnp.zeros((8 - g1, bs), F32))
            out[name][r_halo0 + r_pro :, :] = jnp.concatenate(lines, axis=0)

    def ready0(m_r, w_o):
        for k in range(k0):
            w_o[0, k * bs : (k + 1) * bs, :] = split_weight(m_r[0, k].T)

    def ready1(m_r, p0_r, p1_r, cinv_r, *rest):
        got = named(rest[:4])
        w_o, p0_o, p0t_o, p1_o, p1t_o, idx_o, wc_o = rest[4:]
        for b in range(nb1):
            for k in range(k1):
                w_o[b, k * bs : (k + 1) * bs, :] = split_weight(m_r[b, k].T)
            p1_o[b] = split_weight(p1_r[b])
            p1t_o[b] = split_weight(p1_r[b].T)
        for b in range(nb):
            p0_o[b * bs : (b + 1) * bs, :] = split_weight(p0_r[b])
            p0t_o[b] = split_weight(p0_r[b].T)
        for name, (_, slot, inside) in sides().items():
            for g in range(g1):
                start = r_halo0 + g * bs
                block = jnp.where(inside, got[name][start : start + bs, :], 0.0)
                p1t_o[nb1 + slot * g1 + g] = split_weight(block.T)
                line = got[name][r_halo0 + r_pro + g : r_halo0 + r_pro + g + 1, :]
                idx_o[slot * g1 + g] = jnp.broadcast_to(line, (8, bs))
        me = lax.axis_index("row") * cols_n + lax.axis_index("col")
        place = me % share
        for c in range(ncb):
            mine = cinv_r[:, c * bs : (c + 1) * bs]
            tall = jnp.concatenate(
                [jnp.where(place == t, mine, 0.0) for t in range(share)], axis=0
            )
            wc_o[c * bs : (c + 1) * bs, :] = split_weight(tall.T)

    def fine_sweep(rhs_r, di_r, x_r, c_r, s_r, w_r, *rest):
        got, x_o, out = named(rest[:4]), rest[4], named(rest[5:9])
        ext, xs = rest[9:]
        x = x_r[...]
        own_halves(ext, x, nb, loads)
        fill_ghosts(ext, got, nb, g0, loads)
        y = coupled(ext, c_r, w_r, nb, k0, loads)
        x = (1.0 - OMEGA) * x + di_r[...] * (rhs_r[...] - y)
        x_o[...] = x
        keep(xs, x, nb, loads)
        pack(xs, s_r, out, g0, loads)

    def fine_last(rhs_r, di_r, x_r, c_r, w_r, *rest):
        got, x_o, ext = named(rest[:4]), rest[4], rest[5]
        x = x_r[...]
        own_halves(ext, x, nb, loads)
        fill_ghosts(ext, got, nb, g0, loads)
        y = coupled(ext, c_r, w_r, nb, k0, loads)
        x_o[...] = (1.0 - OMEGA) * x + di_r[...] * (rhs_r[...] - y)

    def restrict0(rhs_r, dd_r, x_r, c_r, w_r, p0_r, a0_r, ei_r, s1_r, *rest):
        got, b1_o, x1_o, out = named(rest[:4]), rest[4], rest[5], named(rest[6:10])
        ext, xs = rest[10:]
        x = x_r[...]
        own_halves(ext, x, nb, loads)
        fill_ghosts(ext, got, nb, g0, loads)
        y = coupled(ext, c_r, w_r, nb, k0, loads)
        res = rhs_r[...] - (dd_r[...] * x + y)
        parts = [halves(res[b * loads : (b + 1) * loads]) for b in range(nb)]
        total = []
        for c in range(nb1):
            left = jnp.concatenate(
                [jnp.where(a0_r[b] == c, parts[b], jnp.zeros_like(parts[b])) for b in range(nb)],
                axis=1,
            )
            total.append(folded(dot(left, p0_r[...]), loads))
        b1 = jnp.concatenate(total, axis=0)
        x1 = b1 * ei_r[...]
        b1_o[...], x1_o[...] = b1, x1
        keep(xs, x1, nb1, loads)
        pack(xs, s1_r, out, g1, loads)

    def level_sweep(b1_r, ei_r, x_r, c_r, s_r, w_r, *rest):
        got, x_o, out = named(rest[:4]), rest[4], named(rest[5:9])
        ext, xs = rest[9:]
        x = x_r[...]
        own_halves(ext, x, nb1, loads)
        fill_ghosts(ext, got, nb1, g1, loads)
        y = coupled(ext, c_r, w_r, nb1, k1, loads)
        x = (1.0 - OMEGA) * x + ei_r[...] * (b1_r[...] - y)
        x_o[...] = x
        keep(xs, x, nb1, loads)
        pack(xs, s_r, out, g1, loads)

    def restrict1(b1_r, ee_r, x_r, c_r, w_r, p1_r, a1_r, *rest):
        got, out, ext = named(rest[:4]), rest[4], rest[5]
        x = x_r[...]
        own_halves(ext, x, nb1, loads)
        fill_ghosts(ext, got, nb1, g1, loads)
        y = coupled(ext, c_r, w_r, nb1, k1, loads)
        res = b1_r[...] - (ee_r[...] * x + y)
        parts = [
            folded(dot(halves(res[b * loads : (b + 1) * loads]), p1_r[b]), loads)
            for b in range(nb1)
        ]
        index = [jnp.full((loads, bs), a1_r[b].astype(F32)) for b in range(nb1)]
        message = jnp.concatenate(parts + index, axis=0)
        out[...] = jnp.broadcast_to(message[None], out.shape)

    def coarse(term_r, wc_r, out, left_s):
        def gather(c, carry):
            values, index = term_r[:, :n1, :], term_r[:, n1:, :]
            block = jnp.sum(jnp.where(index == c.astype(F32), values, 0.0), axis=0)
            total = sum(block[b * loads : (b + 1) * loads] for b in range(nb1))
            left_s[c] = halves(total)
            return carry

        lax.fori_loop(0, ncb, gather, 0, unroll=ncb <= 8)
        left = jnp.concatenate([left_s[c] for c in range(ncb)], axis=1)
        mine = folded(dot(left, wc_r[...]), loads)
        mine = jnp.concatenate([mine, jnp.zeros((8 - loads, bs), F32)], axis=0)
        out[...] = jnp.broadcast_to(mine[None], out.shape)

    def level_correct(sol_r, b1_r, ei_r, x_r, c_r, s_r, w_r, p1t_r, idx_r, a1_r, *rest):
        got, x_o, out = named(rest[:4]), rest[4], named(rest[5:9])
        ext, xs, cx = rest[9:]
        for c in range(ncb):
            cx[c] = sum(sol_r[c * share + t] for t in range(share))
        x = x_r[...]
        lifted = [
            folded(dot(halves(cx[a1_r[b]][:loads]), p1t_r[b]), loads) for b in range(nb1)
        ]
        x = x + jnp.concatenate(lifted, axis=0)
        own_halves(ext, x, nb1, loads)
        for name, (_, slot, inside) in sides().items():
            for g in range(g1):
                place = slot * g1 + g
                index = idx_r[place]
                pick = jnp.zeros((8, bs), F32)
                for c in range(ncb):
                    pick = jnp.where(index == float(c), cx[c], pick)
                moved = folded(dot(halves(pick[:loads]), p1t_r[nb1 + place]), loads)
                old = got[name][g * loads : (g + 1) * loads, :]
                ext[nb1 + place] = halves(jnp.where(inside, old + moved, 0.0))
        y = coupled(ext, c_r, w_r, nb1, k1, loads)
        x = (1.0 - OMEGA) * x + ei_r[...] * (b1_r[...] - y)
        x_o[...] = x
        keep(xs, x, nb1, loads)
        pack(xs, s_r, out, g1, loads)

    def lift(b1_r, ei_r, x_r, c_r, w_r, p0t_r, a0_r, s0_r, x0_r, *rest):
        got, x_o, out = named(rest[:4]), rest[4], named(rest[5:9])
        ext, xs = rest[9:]
        x = x_r[...]
        own_halves(ext, x, nb1, loads)
        fill_ghosts(ext, got, nb1, g1, loads)
        y = coupled(ext, c_r, w_r, nb1, k1, loads)
        x = (1.0 - OMEGA) * x + ei_r[...] * (b1_r[...] - y)
        own_halves(ext, x, nb1, loads)
        parts = [folded(dot(ext[a0_r[b]], p0t_r[b]), loads) for b in range(nb)]
        fine = x0_r[...] + jnp.concatenate(parts, axis=0)
        x_o[...] = fine
        keep(xs, fine, nb, loads)
        pack(xs, s0_r, out, g0, loads)

    def swap(sent):
        got = exchange(named(sent), table)
        return [got[name] for name in ORDER]

    x0, dd, di, ee, ei, *sent = call(
        first,
        [vec0, vec0, vec0, vec1, vec1] + [((first_rows, bs), F32)] * 4,
        [VM] * 4 + [SM] * 3,
        [x3],
    )(rhs2, d0, d1, p1, s0, s1, a1)
    w0 = pl.pallas_call(
        ready0,
        grid=(nb,),
        in_specs=[pl.BlockSpec((1, k0, bs, bs), lambda b: (b, 0, 0, 0))],
        out_specs=pl.BlockSpec((1, k0 * bs, 2 * bs), lambda b: (b, 0, 0)),
        out_shape=jax.ShapeDtypeStruct((nb, k0 * bs, 2 * bs), BF16),
        compiler_params=pltpu.CompilerParams(vmem_limit_bytes=16 * MIB),
    )(m0)
    got = swap(sent)
    x0, *sent = call(
        fine_sweep, [vec0] + halo0, [VM] * 3 + [SM] * 2 + [VM] * 5, [ext0, x3]
    )(rhs2, di, x0, c0, s0, w0, *got)
    w1, p0w, p0t, p1w, p1t, idx, wc = call(
        ready1,
        [
            ((nb1, k1 * bs, 2 * bs), BF16),
            ((nb * bs, 2 * bs), BF16),
            ((nb, bs, 2 * bs), BF16),
            ((nb1, bs, 2 * bs), BF16),
            ((e1n, bs, 2 * bs), BF16),
            ((4 * g1, 8, bs), F32),
            ((ncu, 2 * bs), BF16),
        ],
        [VM] * 8,
        limit=24,
    )(m1, p0, p1, cinv, *got)
    got = swap(sent)
    b1, x1, *sent = call(
        restrict0,
        [vec1, vec1] + halo1,
        [VM] * 3 + [SM] + [VM] * 2 + [SM, VM, SM] + [VM] * 4,
        [ext0, y3],
    )(rhs2, dd, x0, c0, w0, p0w, a0, ei, s1, *got)
    got = swap(sent)
    x1, *sent = call(
        level_sweep, [vec1] + halo1, [VM] * 3 + [SM] * 2 + [VM] * 5, [ext1, y3]
    )(b1, ei, x1, c1, s1, w1, *got)
    got = swap(sent)
    (terms,) = call(
        restrict1,
        [((devices, 2 * n1, bs), F32)],
        [VM] * 3 + [SM] + [VM] * 2 + [SM] + [VM] * 4,
        [ext1],
    )(b1, ee, x1, c1, w1, p1w, a1, *got)
    terms = lax.all_to_all(terms, AXES, 0, 0, tiled=True)
    (mine,) = call(
        coarse, [((devices, 8, bs), F32)], [VM] * 2, [pltpu.VMEM((ncb, 16, bs), BF16)], limit=24
    )(terms, wc)
    sol = lax.all_to_all(mine, AXES, 0, 0, tiled=True)
    x1, *sent = call(
        level_correct,
        [vec1] + halo1,
        [VM] * 4 + [SM] * 2 + [VM] * 3 + [SM] + [VM] * 4,
        [ext1, y3, pltpu.VMEM((ncb, 8, bs), F32)],
    )(sol, b1, ei, x1, c1, s1, w1, p1t, idx, a1, *got)
    got = swap(sent)
    x0, *sent = call(
        lift,
        [vec0] + halo0,
        [VM] * 3 + [SM] + [VM] * 2 + [SM] * 2 + [VM] * 5,
        [ext1, x3],
    )(b1, ei, x1, c1, w1, p0t, a0, s0, x0, *got)
    got = swap(sent)
    x0, *sent = call(
        fine_sweep, [vec0] + halo0, [VM] * 3 + [SM] * 2 + [VM] * 5, [ext0, x3]
    )(rhs2, di, x0, c0, s0, w0, *got)
    got = swap(sent)
    (x0,) = call(fine_last, [vec0], [VM] * 3 + [SM] + [VM] * 5, [ext0])(
        rhs2, di, x0, c0, w0, *got
    )
    return x0.reshape(1, 1, nb, loads, bs)


def solution(mesh):
    return jax.shard_map(
        on_device,
        mesh=mesh,
        in_specs=(
            P("row", "col", None, None, None),
            P("row", "col", None, None),
            P("row", "col", None, None, None, None),
            P("row", "col", None, None),
            P("row", "col", None, None),
            P("row", "col", None, None, None),
            P("row", "col", None),
            P("row", "col", None, None),
            P("row", "col", None, None, None, None),
            P("row", "col", None, None),
            P("row", "col", None, None),
            P("row", "col", None, None, None),
            P("row", "col", None),
            P(("row", "col"), None),
        ),
        out_specs=P("row", "col", None, None, None),
        check_vma=False,
    )
```

time: 298 us -> 86.2 us (0.29)
  blocking collectives: 100 us -> 24.4 us
  starting transfers between devices: 84.3 us -> 29.5 us
  waiting for transfers between devices: 54.8 us -> 6.63 us
  matrix products: 43 us -> 0 us
  Pallas kernels: 0 us -> 16.4 us
  other arithmetic: 3.06 us -> 0 us
    all_gather x1 -> x0, blocking collectives: 61 us -> none  [on_device(): coarse_x = lax.all_gather(own_rows, ('row', 'col'), axis=1, tiled=True)]
    ppermute x32 -> x28, starting transfers between devices: 84.3 us -> 29.5 us  [exchange(): got[name] = lax.ppermute(sent[name], AXES, table[name])]
    ppermute x32 -> x28, waiting for transfers between devices: 54.8 us -> 6.63 us  [exchange(): got[name] = lax.ppermute(sent[name], AXES, table[name])]
    dot_general x17 -> x0, matrix products: 43 us -> none  [the longest x8 40 us: apply_op(): coupled = jnp.einsum('bkij,bkrj->bri', blocks, nearby, precision=HIGH)]
    psum x1 -> x0, blocking collectives: 39.2 us -> none  [on_device(): coarse_rhs = lax.psum(term, ('row', 'col'))]
    all_to_all x0 -> x2, blocking collectives: none -> 24.4 us  [the longest x1 14.1 us: on_device(): terms = lax.all_to_all(terms, AXES, 0, 0, tiled=True)]
    pallas_call x0 -> x12, Pallas kernels: none -> 16.4 us  [the longest x2 3.46 us: on_device(): call(fine_sweep, [vec0] + halo0, [VM] * 3 + [SM] * 2 + [VM] * 5, [ext0, x3])]
    gather x20 -> x0, local copies, waits for them, and re-layouts: 10.1 us -> none  [the longest x8 5.32 us: apply_op(): nearby = extended[cols]]
  transfers between devices with their start and end apart: 32 -> 28, of which waited for: 20 -> 10; matrix products, arithmetic and copies ran while one was open for 0% -> 0% of each run, Pallas kernels for 0% -> 4%
where the time goes in v1:
time: 86.2 us; the launch traced here: 85.4 us
  starting transfers between devices  29.5 us (34%)
  blocking collectives  24.4 us (28%)
  Pallas kernels  16.4 us (19%)
  local copies, waits for them, and re-layouts  8.25 us (10%)
  waiting for transfers between devices  6.63 us (8%)
    ppermute x28, starting transfers between devices, exchange(): got[name] = lax.ppermute(sent[name], AXES, table[name])  29.5 us
    all_to_all x1, blocking collectives, on_device(): terms = lax.all_to_all(terms, AXES, 0, 0, tiled=True)  14.1 us
    all_to_all x1, blocking collectives, on_device(): sol = lax.all_to_all(mine, AXES, 0, 0, tiled=True)  10.3 us
    unnamed x34, local copies, waits for them, and re-layouts  7.48 us
    ppermute x28, waiting for transfers between devices, exchange(): got[name] = lax.ppermute(sent[name], AXES, table[name])  6.63 us
    pallas_call x2, Pallas kernels, on_device(): call(fine_sweep, [vec0] + halo0, [VM] * 3 + [SM] * 2 + [VM] * 5, [ext0, x3])  3.46 us
    pallas_call x1, Pallas kernels, on_device(): pl.pallas_call(ready0, grid=(nb,), in_specs=[pl.BlockSpec((1, k0, bs, bs)...  2.52 us
    pallas_call x1, Pallas kernels, on_device(): call(fine_last, [vec0], [VM] * 3 + [SM] + [VM] * 5, [ext0])  2.3 us
  transfers between devices with their start and end apart: 28, of which 10 were waited for; matrix products, arithmetic and copies ran while one was open for 0% of the time, Pallas kernels for 4%

profile of v1, /device:TPU:1, one launch (start us, length us, event | category | flops | bytes accessed | tf_op | source)
XLA Modules:
  0.0 85.4 jit_solution(2236306270678204494)
XLA Ops:
  0.0 0.8 copy.15.s1_r.s_r
  0.8 0.9 %copy-done.3 = f32[1,1,2,128,128]{4,3,2,1,0:T(8,128)S(1)} copy-done((f32[1,1,2,128,128]{4,3,2,1,0:T(8,128)S(1)}, f32[1,1,2,128,128]{4,3,2,1,0:T(8,128)}, u32[]{:S(2)}) %copy-start.3) | copy-done | bytes 131096
  5.9 2.7 %collective-permute-start.1 = (f32[280,128]{1,0:T(8,128)S(1)}, f32[280,128]{1,0:T(8,128)S(1)}, u32[]{:S(2)}, u32[]{:S(2)}) collective-permute-start(f32[280,128]{1,0:T(8,128)S(1)} %get-tuple-element.56), channel_id=1, source_target_pairs={{0,24},{1,25},{2,26},{3,27},{4,28},{5,29},{6,30},{7,31},{8,16},{9,... | collective-permute-start | bytes 430088 | tf_op jit(solution)/shard_map/ppermute | solution.py:40
  8.5 2.7 %collective-permute-start.2 = (f32[280,128]{1,0:T(8,128)S(1)}, f32[280,128]{1,0:T(8,128)S(1)}, u32[]{:S(2)}, u32[]{:S(2)}) collective-permute-start(f32[280,128]{1,0:T(8,128)S(1)} %get-tuple-element.57), channel_id=1, source_target_pairs={{0,1},{1,0},{2,3},{3,2},{4,5},{5,4},{6,7},{7,6},{8,9},{9,8},{10,11... | collective-permute-start | bytes 430088 | tf_op jit(solution)/shard_map/ppermute | solution.py:40
  11.2 3.1 %copy-done = f32[1,1,8,14,128,128]{5,4,3,2,1,0:T(8,128)S(1)} copy-done((f32[1,1,8,14,128,128]{5,4,3,2,1,0:T(8,128)S(1)}, f32[1,1,8,14,128,128]{5,4,3,2,1,0:T(8,128)}, u32[]{:S(2)}) %copy-start) | copy-done | bytes 7340056
  14.3 2.5 %shard_map.137.w_r = bf16[8,1792,256]{2,1,0:T(8,128)(2,1)S(1)} custom-call(f32[8,14,128,128]{3,2,1,0:T(8,128)S(1)} %bitcast.14), custom_call_target="tpu_custom_call" | custom-call | tf_op jit(solution)/shard_map/pallas_call | solution.py:355
  17.0 1.7 %shard_map.138 = (f32[32,128]{1,0:T(8,128)S(1)}, f32[16,128]{1,0:T(8,128)S(1)}, f32[16,128]{1,0:T(8,128)S(1)}, f32[16,128]{1,0:T(8,128)S(1)}, f32[16,128]{1,0:T(8,128)S(1)}) custom-call(f32[32,128]{1,0:T(8,128)S(1)} %bitcast.20, f32[32,128]{1,0:T(8,128)S(1)} %get-tuple-element.52.di_r, f32[32,128]{1,0:T(8,128)S(1)} %get-tuple-element.54.x_r, ...), custom_call_target="tpu_custom_call" | custom-call | tf_op jit(solution)/shard_map/pallas_call | solution.py:364
  19.6 2.9 %collective-permute-start.6 = (f32[16,128]{1,0:T(8,128)S(1)}, f32[16,128]{1,0:T(8,128)S(1)}, u32[]{:S(2)}, u32[]{:S(2)}) collective-permute-start(f32[16,128]{1,0:T(8,128)S(1)} %get-tuple-element.64), channel_id=1, source_target_pairs={{0,1},{1,0},{2,3},{3,2},{4,5},{5,4},{6,7},{7,6},{8,9},{9,8},{10,11... | collective-permute-start | bytes 24584 | tf_op jit(solution)/shard_map/ppermute | solution.py:40
  22.6 1.0 %shard_map.139 = (bf16[2,1792,256]{2,1,0:T(8,128)(2,1)S(1)}, bf16[1024,256]{1,0:T(8,128)(2,1)S(1)}, bf16[8,128,256]{2,1,0:T(8,128)(2,1)S(1)}, bf16[2,128,256]{2,...) custom-call(f32[2,14,128,128]{3,2,1,0:T(8,128)S(1)} %bitcast.15, ...), custom_call_target="tpu_custom_call" | custom-call | tf_op jit(solution)/shard_map/pallas_call | solution.py:367
  23.9 1.9 %shard_map.140 = (f32[8,128]{1,0:T(8,128)S(1)}, f32[8,128]{1,0:T(8,128)S(1)}, f32[8,128]{1,0:T(8,128)S(1)}, f32[8,128]{1,0:T(8,128)S(1)}, f32[8,128]{1,0:T(8,128)S(1)}, /*index=5*/f32[8,128]{1,0:T(8,128)S(1)}) custom-call(f32[32,128]{1,0:T(8,128)S(1)} %bitcast.21, f32[32,128]{1,0:T(8,128)S(1)} %get-tuple-element.53.dd_r, ...), custom_call_target="tpu_custom_call" | custom-call | tf_op jit(solution)/shard_map/pallas_call | solution.py:382
  25.8 1.2 %collective-permute-start.10 = (f32[8,128]{1,0:T(8,128)S(1)}, f32[8,128]{1,0:T(8,128)S(1)}, u32[]{:S(2)}, u32[]{:S(2)}) collective-permute-start(f32[8,128]{1,0:T(8,128)S(1)} %get-tuple-element.72), channel_id=1, source_target_pairs={{0,1},{1,0},{2,3},{3,2},{4,5},{5,4},{6,7},{7,6},{8,9},{9,8},{10,11... | collective-permute-start | bytes 12296 | tf_op jit(solution)/shard_map/ppermute | solution.py:40
  26.9 1.2 %collective-permute-start.11 = (f32[8,128]{1,0:T(8,128)S(1)}, f32[8,128]{1,0:T(8,128)S(1)}, u32[]{:S(2)}, u32[]{:S(2)}) collective-permute-start(f32[8,128]{1,0:T(8,128)S(1)} %get-tuple-element.73), channel_id=1, source_target_pairs={{0,8},{1,9},{2,10},{3,11},{4,12},{5,13},{6,14},{7,15},{8,0},{9,1},... | collective-permute-start | bytes 12296 | tf_op jit(solution)/shard_map/ppermute | solution.py:40
  28.2 1.2 %collective-permute-start.9 = (f32[8,128]{1,0:T(8,128)S(1)}, f32[8,128]{1,0:T(8,128)S(1)}, u32[]{:S(2)}, u32[]{:S(2)}) collective-permute-start(f32[8,128]{1,0:T(8,128)S(1)} %get-tuple-element.71), channel_id=1, source_target_pairs={{0,24},{1,25},{2,26},{3,27},{4,28},{5,29},{6,30},{7,31},{8,16},{9,... | collective-permute-start | bytes 12296 | tf_op jit(solution)/shard_map/ppermute | solution.py:40
  29.4 1.9 %collective-permute-done.9.rest_1_ = f32[8,128]{1,0:T(8,128)S(1)} collective-permute-done((f32[8,128]{1,0:T(8,128)S(1)}, f32[8,128]{1,0:T(8,128)S(1)}, u32[]{:S(2)}, u32[]{:S(2)}) %collective-permute-start.9) | collective-permute-done | bytes 4128 | tf_op jit(solution)/shard_map/ppermute | solution.py:40
  31.3 0.9 %shard_map.141 = (f32[8,128]{1,0:T(8,128)S(1)}, f32[8,128]{1,0:T(8,128)S(1)}, f32[8,128]{1,0:T(8,128)S(1)}, f32[8,128]{1,0:T(8,128)S(1)}, f32[8,128]{1,0:T(8,128)S(1)}) custom-call(f32[8,128]{1,0:T(8,128)S(1)} %get-tuple-element.66.b1_r, f32[8,128]{1,0:T(8,128)S(1)} %get-tuple-element.61.ei_r, f32[8,128]{1,0:T(8,128)S(1)} %get-tuple-element.68.x_r, ...), custom_call_target="tpu_custom_call" | custom-call | tf_op jit(solution)/shard_map/pallas_call | solution.py:389
  32.7 0.8 collective-permute-start.13
  33.6 3.6 %collective-permute-start.14 = (f32[8,128]{1,0:T(8,128)S(1)}, f32[8,128]{1,0:T(8,128)S(1)}, u32[]{:S(2)}, u32[]{:S(2)}) collective-permute-start(f32[8,128]{1,0:T(8,128)S(1)} %get-tuple-element.78), channel_id=1, source_target_pairs={{0,1},{1,0},{2,3},{3,2},{4,5},{5,4},{6,7},{7,6},{8,9},{9,8},{10,11... | collective-permute-start | bytes 12296 | tf_op jit(solution)/shard_map/ppermute | solution.py:40
  37.2 1.0 %collective-permute-done.14.rest_2_ = f32[8,128]{1,0:T(8,128)S(1)} collective-permute-done((f32[8,128]{1,0:T(8,128)S(1)}, f32[8,128]{1,0:T(8,128)S(1)}, u32[]{:S(2)}, u32[]{:S(2)}) %collective-permute-start.14) | collective-permute-done | bytes 4128 | tf_op jit(solution)/shard_map/ppermute | solution.py:40
  38.3 1.0 %shard_map.142 = f32[32,16,128]{2,1,0:T(8,128)S(1)} custom-call(f32[8,128]{1,0:T(8,128)S(1)} %get-tuple-element.66.b1_r, f32[8,128]{1,0:T(8,128)S(1)} %get-tuple-element.67.ee_r, f32[8,128]{1,0:T(8,128)S(1)} %get-tuple-element.74.x_r, s32[2,14]{1,0:T(2,128)S(1)} %bitcast.33, bf16[2,1792,256]{2,1,0:T(8,128)(2,1)S(1)} %get-tuple-element.69.w_r, ...), custom_call_target="tpu_custom_call" | custom-call | tf_op jit(solution)/shard_map/pallas_call | solution.py:393
  39.4 14.1 %all_to_all.10.term_r = f32[32,16,128]{2,1,0:T(8,128)S(1)} all-to-all(f32[32,16,128]{2,1,0:T(8,128)S(1)} %shard_map.142), channel_id=1, replica_groups=mesh['row'=4,'col'=8] {'row','col'}, dimensions={0} | all-to-all | bytes 524288 | tf_op jit(solution)/shard_map/all_to_all | solution.py:399
  53.8 10.3 %all_to_all.11.sol_r = f32[32,8,128]{2,1,0:T(8,128)S(1)} all-to-all(f32[32,8,128]{2,1,0:T(8,128)S(1)} %shard_map.143), channel_id=1, replica_groups=mesh['row'=4,'col'=8] {'row','col'}, dimensions={0} | all-to-all | bytes 262144 | tf_op jit(solution)/shard_map/all_to_all | solution.py:403
  64.1 1.1 %shard_map.144 = (f32[8,128]{1,0:T(8,128)S(1)}, f32[8,128]{1,0:T(8,128)S(1)}, f32[8,128]{1,0:T(8,128)S(1)}, f32[8,128]{1,0:T(8,128)S(1)}, f32[8,128]{1,0:T(8,128)S(1)}) custom-call(f32[32,8,128]{2,1,0:T(8,128)S(1)} %all_to_all.11.sol_r, f32[8,128]{1,0:T(8,128)S(1)} %get-tuple-element.66.b1_r, f32[8,128]{1,0:T(8,128)S(1)} %get-tuple-element.61.ei_r, ...), custom_call_target="tpu_custom_call" | custom-call | tf_op jit(solution)/shard_map/pallas_call | solution.py:404
  66.3 1.5 %collective-permute-start.18 = (f32[8,128]{1,0:T(8,128)S(1)}, f32[8,128]{1,0:T(8,128)S(1)}, u32[]{:S(2)}, u32[]{:S(2)}) collective-permute-start(f32[8,128]{1,0:T(8,128)S(1)} %get-tuple-element.87), channel_id=1, source_target_pairs={{0,1},{1,0},{2,3},{3,2},{4,5},{5,4},{6,7},{7,6},{8,9},{9,8},{10,11... | collective-permute-start | bytes 12296 | tf_op jit(solution)/shard_map/ppermute | solution.py:40
  69.1 1.1 %shard_map.145 = (f32[32,128]{1,0:T(8,128)S(1)}, f32[16,128]{1,0:T(8,128)S(1)}, f32[16,128]{1,0:T(8,128)S(1)}, f32[16,128]{1,0:T(8,128)S(1)}, f32[16,128]{1,0:T(8,128)S(1)}) custom-call(f32[8,128]{1,0:T(8,128)S(1)} %get-tuple-element.66.b1_r, f32[8,128]{1,0:T(8,128)S(1)} %get-tuple-element.61.ei_r, f32[8,128]{1,0:T(8,128)S(1)} %get-tuple-element.83.x_r, ...), custom_call_target="tpu_custom_call" | custom-call | tf_op jit(solution)/shard_map/pallas_call | solution.py:411
  70.2 1.4 %collective-permute-start.20 = (f32[16,128]{1,0:T(8,128)S(1)}, f32[16,128]{1,0:T(8,128)S(1)}, u32[]{:S(2)}, u32[]{:S(2)}) collective-permute-start(f32[16,128]{1,0:T(8,128)S(1)} %get-tuple-element.90), channel_id=1, source_target_pairs={{0,8},{1,2},{2,1},{3,4},{4,3},{5,6},{6,5},{7,15},{8,0},{9,10},{10,... | collective-permute-start | bytes 24584 | tf_op jit(solution)/shard_map/ppermute | solution.py:40
  72.3 3.0 %collective-permute-start.22 = (f32[16,128]{1,0:T(8,128)S(1)}, f32[16,128]{1,0:T(8,128)S(1)}, u32[]{:S(2)}, u32[]{:S(2)}) collective-permute-start(f32[16,128]{1,0:T(8,128)S(1)} %get-tuple-element.92), channel_id=1, source_target_pairs={{0,1},{1,0},{2,3},{3,2},{4,5},{5,4},{6,7},{7,6},{8,9},{9,8},{10,11... | collective-permute-start | bytes 24584 | tf_op jit(solution)/shard_map/ppermute | solution.py:40
  75.4 1.0 %collective-permute-done.22.rest_2_ = f32[16,128]{1,0:T(8,128)S(1)} collective-permute-done((f32[16,128]{1,0:T(8,128)S(1)}, f32[16,128]{1,0:T(8,128)S(1)}, u32[]{:S(2)}, u32[]{:S(2)}) %collective-permute-start.22) | collective-permute-done | bytes 8224 | tf_op jit(solution)/shard_map/ppermute | solution.py:40
  76.5 1.7 %shard_map.146 = (f32[32,128]{1,0:T(8,128)S(1)}, f32[16,128]{1,0:T(8,128)S(1)}, f32[16,128]{1,0:T(8,128)S(1)}, f32[16,128]{1,0:T(8,128)S(1)}, f32[16,128]{1,0:T(8,128)S(1)}) custom-call(f32[32,128]{1,0:T(8,128)S(1)} %bitcast.22, f32[32,128]{1,0:T(8,128)S(1)} %get-tuple-element.52.di_r, f32[32,128]{1,0:T(8,128)S(1)} %get-tuple-element.89.x_r, ...), custom_call_target="tpu_custom_call" | custom-call | tf_op jit(solution)/shard_map/pallas_call | solution.py:418
  78.5 0.8 collective-permute-start.25
  79.3 2.5 %collective-permute-start.26 = (f32[16,128]{1,0:T(8,128)S(1)}, f32[16,128]{1,0:T(8,128)S(1)}, u32[]{:S(2)}, u32[]{:S(2)}) collective-permute-start(f32[16,128]{1,0:T(8,128)S(1)} %get-tuple-element.97), channel_id=1, source_target_pairs={{0,1},{1,0},{2,3},{3,2},{4,5},{5,4},{6,7},{7,6},{8,9},{9,8},{10,11... | collective-permute-start | bytes 24584 | tf_op jit(solution)/shard_map/ppermute | solution.py:40
  81.9 1.3 %collective-permute-done.26.rest_2_ = f32[16,128]{1,0:T(8,128)S(1)} collective-permute-done((f32[16,128]{1,0:T(8,128)S(1)}, f32[16,128]{1,0:T(8,128)S(1)}, u32[]{:S(2)}, u32[]{:S(2)}) %collective-permute-start.26) | collective-permute-done | bytes 8224 | tf_op jit(solution)/shard_map/ppermute | solution.py:40
  83.1 2.3 %shard_map.147 = f32[32,128]{1,0:T(8,128)} custom-call(f32[32,128]{1,0:T(8,128)S(1)} %bitcast.23, f32[32,128]{1,0:T(8,128)S(1)} %get-tuple-element.52.di_r, f32[32,128]{1,0:T(8,128)S(1)} %get-tuple-element.94.x_r, s32[8,14]{1,0:T(8,128)S(1)} %bitcast.27, bf16[8,1792,256]{2,1,0:T(8,128)(2,1)S(1)} %shard_map.137.w_r, ...), custom_call_target="tpu_custom_call" | custom-call | tf_op jit(solution)/shard_map/pallas_call | solution.py:422
  (73 shorter events, 9.9 us)
Async XLA Ops:
  5.8 11.1 %collective-permute-start = (f32[280,128]{1,0:T(8,128)S(1)}, f32[280,128]{1,0:T(8,128)S(1)}, u32[]{:S(2)}, u32[]{:S(2)}) collective-permute-start(f32[280,128]{1,0:T(8,128)S(1)} %get-tuple-element.55), channel_id=1, source_target_pairs={{0,8},{1,2},{2,1},{3,4},{4,3},{5,6},{6,5},{7,15},{8,0},{9,10},{10,... | collective-permute-start | bytes 430088 | tf_op jit(solution)/shard_map/ppermute | solution.py:40
  5.9 11.1 %collective-permute-start.1 = (f32[280,128]{1,0:T(8,128)S(1)}, f32[280,128]{1,0:T(8,128)S(1)}, u32[]{:S(2)}, u32[]{:S(2)}) collective-permute-start(f32[280,128]{1,0:T(8,128)S(1)} %get-tuple-element.56), channel_id=1, source_target_pairs={{0,24},{1,25},{2,26},{3,27},{4,28},{5,29},{6,30},{7,31},{8,16},{9,... | collective-permute-start | bytes 430088 | tf_op jit(solution)/shard_map/ppermute | solution.py:40
  8.5 8.4 %collective-permute-start.2 = (f32[280,128]{1,0:T(8,128)S(1)}, f32[280,128]{1,0:T(8,128)S(1)}, u32[]{:S(2)}, u32[]{:S(2)}) collective-permute-start(f32[280,128]{1,0:T(8,128)S(1)} %get-tuple-element.57), channel_id=1, source_target_pairs={{0,1},{1,0},{2,3},{3,2},{4,5},{5,4},{6,7},{7,6},{8,9},{9,8},{10,11... | collective-permute-start | bytes 430088 | tf_op jit(solution)/shard_map/ppermute | solution.py:40
  11.2 5.7 %collective-permute-start.3 = (f32[280,128]{1,0:T(8,128)S(1)}, f32[280,128]{1,0:T(8,128)S(1)}, u32[]{:S(2)}, u32[]{:S(2)}) collective-permute-start(f32[280,128]{1,0:T(8,128)S(1)} %get-tuple-element.58), channel_id=1, source_target_pairs={{0,8},{1,9},{2,10},{3,11},{4,12},{5,13},{6,14},{7,15},{8,0},{9,1},... | collective-permute-start | bytes 430088 | tf_op jit(solution)/shard_map/ppermute | solution.py:40
  16.8 5.8 %copy-start.1 = (f32[1,1,2,14,128,128]{5,4,3,2,1,0:T(8,128)S(1)}, f32[1,1,2,14,128,128]{5,4,3,2,1,0:T(8,128)}, u32[]{:S(2)}) copy-start(f32[1,1,2,14,128,128]{5,4,3,2,1,0:T(8,128)} %param.22) | copy-start | bytes 5505028
  16.9 7.0 %copy-start.15 = (s32[1,1,8]{2,1,0:T(1,128)S(1)}, s32[1,1,8]{2,1,0:T(1,128)}, u32[]{:S(2)}) copy-start(s32[1,1,8]{2,1,0:T(1,128)} %param.20) | copy-start | bytes 100
  18.7 12.6 %copy-start.11 = (s32[1,1,2,14]{3,2,1,0:T(2,128)S(1)}, s32[1,1,2,14]{3,2,1,0:T(2,128)}, u32[]{:S(2)}) copy-start(s32[1,1,2,14]{3,2,1,0:T(2,128)} %param.23) | copy-start | bytes 340
  18.7 19.6 %copy-start.13 = (s32[1,1,2]{2,1,0:T(1,128)S(1)}, s32[1,1,2]{2,1,0:T(1,128)}, u32[]{:S(2)}) copy-start(s32[1,1,2]{2,1,0:T(1,128)} %param.26) | copy-start | bytes 28
  18.7 4.9 %collective-permute-start.4 = (f32[16,128]{1,0:T(8,128)S(1)}, f32[16,128]{1,0:T(8,128)S(1)}, u32[]{:S(2)}, u32[]{:S(2)}) collective-permute-start(f32[16,128]{1,0:T(8,128)S(1)} %get-tuple-element.62), channel_id=1, source_target_pairs={{0,8},{1,2},{2,1},{3,4},{4,3},{5,6},{6,5},{7,15},{8,0},{9,10},{10,... | collective-permute-start | bytes 24584 | tf_op jit(solution)/shard_map/ppermute | solution.py:40
  19.3 4.4 %collective-permute-start.5 = (f32[16,128]{1,0:T(8,128)S(1)}, f32[16,128]{1,0:T(8,128)S(1)}, u32[]{:S(2)}, u32[]{:S(2)}) collective-permute-start(f32[16,128]{1,0:T(8,128)S(1)} %get-tuple-element.63), channel_id=1, source_target_pairs={{0,24},{1,25},{2,26},{3,27},{4,28},{5,29},{6,30},{7,31},{8,16},{9,... | collective-permute-start | bytes 24584 | tf_op jit(solution)/shard_map/ppermute | solution.py:40
  19.6 4.3 %collective-permute-start.6 = (f32[16,128]{1,0:T(8,128)S(1)}, f32[16,128]{1,0:T(8,128)S(1)}, u32[]{:S(2)}, u32[]{:S(2)}) collective-permute-start(f32[16,128]{1,0:T(8,128)S(1)} %get-tuple-element.64), channel_id=1, source_target_pairs={{0,1},{1,0},{2,3},{3,2},{4,5},{5,4},{6,7},{7,6},{8,9},{9,8},{10,11... | collective-permute-start | bytes 24584 | tf_op jit(solution)/shard_map/ppermute | solution.py:40
  22.5 1.4 %collective-permute-start.7 = (f32[16,128]{1,0:T(8,128)S(1)}, f32[16,128]{1,0:T(8,128)S(1)}, u32[]{:S(2)}, u32[]{:S(2)}) collective-permute-start(f32[16,128]{1,0:T(8,128)S(1)} %get-tuple-element.65), channel_id=1, source_target_pairs={{0,8},{1,9},{2,10},{3,11},{4,12},{5,13},{6,14},{7,15},{8,0},{9,1},... | collective-permute-start | bytes 24584 | tf_op jit(solution)/shard_map/ppermute | solution.py:40
  25.8 3.6 %collective-permute-start.10 = (f32[8,128]{1,0:T(8,128)S(1)}, f32[8,128]{1,0:T(8,128)S(1)}, u32[]{:S(2)}, u32[]{:S(2)}) collective-permute-start(f32[8,128]{1,0:T(8,128)S(1)} %get-tuple-element.72), channel_id=1, source_target_pairs={{0,1},{1,0},{2,3},{3,2},{4,5},{5,4},{6,7},{7,6},{8,9},{9,8},{10,11... | collective-permute-start | bytes 12296 | tf_op jit(solution)/shard_map/ppermute | solution.py:40
  26.9 2.5 %collective-permute-start.11 = (f32[8,128]{1,0:T(8,128)S(1)}, f32[8,128]{1,0:T(8,128)S(1)}, u32[]{:S(2)}, u32[]{:S(2)}) collective-permute-start(f32[8,128]{1,0:T(8,128)S(1)} %get-tuple-element.73), channel_id=1, source_target_pairs={{0,8},{1,9},{2,10},{3,11},{4,12},{5,13},{6,14},{7,15},{8,0},{9,1},... | collective-permute-start | bytes 12296 | tf_op jit(solution)/shard_map/ppermute | solution.py:40
  28.2 1.2 %collective-permute-start.8 = (f32[8,128]{1,0:T(8,128)S(1)}, f32[8,128]{1,0:T(8,128)S(1)}, u32[]{:S(2)}, u32[]{:S(2)}) collective-permute-start(f32[8,128]{1,0:T(8,128)S(1)} %get-tuple-element.70), channel_id=1, source_target_pairs={{0,8},{1,2},{2,1},{3,4},{4,3},{5,6},{6,5},{7,15},{8,0},{9,10},{10,... | collective-permute-start | bytes 12296 | tf_op jit(solution)/shard_map/ppermute | solution.py:40
  28.2 3.1 %collective-permute-start.9 = (f32[8,128]{1,0:T(8,128)S(1)}, f32[8,128]{1,0:T(8,128)S(1)}, u32[]{:S(2)}, u32[]{:S(2)}) collective-permute-start(f32[8,128]{1,0:T(8,128)S(1)} %get-tuple-element.71), channel_id=1, source_target_pairs={{0,24},{1,25},{2,26},{3,27},{4,28},{5,29},{6,30},{7,31},{8,16},{9,... | collective-permute-start | bytes 12296 | tf_op jit(solution)/shard_map/ppermute | solution.py:40
  32.3 4.9 %collective-permute-start.12 = (f32[8,128]{1,0:T(8,128)S(1)}, f32[8,128]{1,0:T(8,128)S(1)}, u32[]{:S(2)}, u32[]{:S(2)}) collective-permute-start(f32[8,128]{1,0:T(8,128)S(1)} %get-tuple-element.76), channel_id=1, source_target_pairs={{0,8},{1,2},{2,1},{3,4},{4,3},{5,6},{6,5},{7,15},{8,0},{9,10},{10,... | collective-permute-start | bytes 12296 | tf_op jit(solution)/shard_map/ppermute | solution.py:40
  32.7 4.4 %collective-permute-start.13 = (f32[8,128]{1,0:T(8,128)S(1)}, f32[8,128]{1,0:T(8,128)S(1)}, u32[]{:S(2)}, u32[]{:S(2)}) collective-permute-start(f32[8,128]{1,0:T(8,128)S(1)} %get-tuple-element.77), channel_id=1, source_target_pairs={{0,24},{1,25},{2,26},{3,27},{4,28},{5,29},{6,30},{7,31},{8,16},{9,... | collective-permute-start | bytes 12296 | tf_op jit(solution)/shard_map/ppermute | solution.py:40
  33.6 4.6 %collective-permute-start.14 = (f32[8,128]{1,0:T(8,128)S(1)}, f32[8,128]{1,0:T(8,128)S(1)}, u32[]{:S(2)}, u32[]{:S(2)}) collective-permute-start(f32[8,128]{1,0:T(8,128)S(1)} %get-tuple-element.78), channel_id=1, source_target_pairs={{0,1},{1,0},{2,3},{3,2},{4,5},{5,4},{6,7},{7,6},{8,9},{9,8},{10,11... | collective-permute-start | bytes 12296 | tf_op jit(solution)/shard_map/ppermute | solution.py:40
  37.2 1.2 %collective-permute-start.15 = (f32[8,128]{1,0:T(8,128)S(1)}, f32[8,128]{1,0:T(8,128)S(1)}, u32[]{:S(2)}, u32[]{:S(2)}) collective-permute-start(f32[8,128]{1,0:T(8,128)S(1)} %get-tuple-element.79), channel_id=1, source_target_pairs={{0,8},{1,9},{2,10},{3,11},{4,12},{5,13},{6,14},{7,15},{8,0},{9,1},... | collective-permute-start | bytes 12296 | tf_op jit(solution)/shard_map/ppermute | solution.py:40
  65.2 3.0 %collective-permute-start.16 = (f32[8,128]{1,0:T(8,128)S(1)}, f32[8,128]{1,0:T(8,128)S(1)}, u32[]{:S(2)}, u32[]{:S(2)}) collective-permute-start(f32[8,128]{1,0:T(8,128)S(1)} %get-tuple-element.85), channel_id=1, source_target_pairs={{0,8},{1,2},{2,1},{3,4},{4,3},{5,6},{6,5},{7,15},{8,0},{9,10},{10,... | collective-permute-start | bytes 12296 | tf_op jit(solution)/shard_map/ppermute | solution.py:40
  65.7 3.0 %collective-permute-start.17 = (f32[8,128]{1,0:T(8,128)S(1)}, f32[8,128]{1,0:T(8,128)S(1)}, u32[]{:S(2)}, u32[]{:S(2)}) collective-permute-start(f32[8,128]{1,0:T(8,128)S(1)} %get-tuple-element.86), channel_id=1, source_target_pairs={{0,24},{1,25},{2,26},{3,27},{4,28},{5,29},{6,30},{7,31},{8,16},{9,... | collective-permute-start | bytes 12296 | tf_op jit(solution)/shard_map/ppermute | solution.py:40
  66.3 2.5 %collective-permute-start.18 = (f32[8,128]{1,0:T(8,128)S(1)}, f32[8,128]{1,0:T(8,128)S(1)}, u32[]{:S(2)}, u32[]{:S(2)}) collective-permute-start(f32[8,128]{1,0:T(8,128)S(1)} %get-tuple-element.87), channel_id=1, source_target_pairs={{0,1},{1,0},{2,3},{3,2},{4,5},{5,4},{6,7},{7,6},{8,9},{9,8},{10,11... | collective-permute-start | bytes 12296 | tf_op jit(solution)/shard_map/ppermute | solution.py:40
  67.9 1.2 %collective-permute-start.19 = (f32[8,128]{1,0:T(8,128)S(1)}, f32[8,128]{1,0:T(8,128)S(1)}, u32[]{:S(2)}, u32[]{:S(2)}) collective-permute-start(f32[8,128]{1,0:T(8,128)S(1)} %get-tuple-element.88), channel_id=1, source_target_pairs={{0,8},{1,9},{2,10},{3,11},{4,12},{5,13},{6,14},{7,15},{8,0},{9,1},... | collective-permute-start | bytes 12296 | tf_op jit(solution)/shard_map/ppermute | solution.py:40
  70.2 5.1 %collective-permute-start.20 = (f32[16,128]{1,0:T(8,128)S(1)}, f32[16,128]{1,0:T(8,128)S(1)}, u32[]{:S(2)}, u32[]{:S(2)}) collective-permute-start(f32[16,128]{1,0:T(8,128)S(1)} %get-tuple-element.90), channel_id=1, source_target_pairs={{0,8},{1,2},{2,1},{3,4},{4,3},{5,6},{6,5},{7,15},{8,0},{9,10},{10,... | collective-permute-start | bytes 24584 | tf_op jit(solution)/shard_map/ppermute | solution.py:40
  71.6 3.8 %collective-permute-start.21 = (f32[16,128]{1,0:T(8,128)S(1)}, f32[16,128]{1,0:T(8,128)S(1)}, u32[]{:S(2)}, u32[]{:S(2)}) collective-permute-start(f32[16,128]{1,0:T(8,128)S(1)} %get-tuple-element.91), channel_id=1, source_target_pairs={{0,24},{1,25},{2,26},{3,27},{4,28},{5,29},{6,30},{7,31},{8,16},{9,... | collective-permute-start | bytes 24584 | tf_op jit(solution)/shard_map/ppermute | solution.py:40
  72.3 4.1 %collective-permute-start.22 = (f32[16,128]{1,0:T(8,128)S(1)}, f32[16,128]{1,0:T(8,128)S(1)}, u32[]{:S(2)}, u32[]{:S(2)}) collective-permute-start(f32[16,128]{1,0:T(8,128)S(1)} %get-tuple-element.92), channel_id=1, source_target_pairs={{0,1},{1,0},{2,3},{3,2},{4,5},{5,4},{6,7},{7,6},{8,9},{9,8},{10,11... | collective-permute-start | bytes 24584 | tf_op jit(solution)/shard_map/ppermute | solution.py:40
  75.4 1.2 %collective-permute-start.23 = (f32[16,128]{1,0:T(8,128)S(1)}, f32[16,128]{1,0:T(8,128)S(1)}, u32[]{:S(2)}, u32[]{:S(2)}) collective-permute-start(f32[16,128]{1,0:T(8,128)S(1)} %get-tuple-element.93), channel_id=1, source_target_pairs={{0,8},{1,9},{2,10},{3,11},{4,12},{5,13},{6,14},{7,15},{8,0},{9,1},... | collective-permute-start | bytes 24584 | tf_op jit(solution)/shard_map/ppermute | solution.py:40
  78.3 3.6 %collective-permute-start.24 = (f32[16,128]{1,0:T(8,128)S(1)}, f32[16,128]{1,0:T(8,128)S(1)}, u32[]{:S(2)}, u32[]{:S(2)}) collective-permute-start(f32[16,128]{1,0:T(8,128)S(1)} %get-tuple-element.95), channel_id=1, source_target_pairs={{0,8},{1,2},{2,1},{3,4},{4,3},{5,6},{6,5},{7,15},{8,0},{9,10},{10,... | collective-permute-start | bytes 24584 | tf_op jit(solution)/shard_map/ppermute | solution.py:40
  78.5 3.3 %collective-permute-start.25 = (f32[16,128]{1,0:T(8,128)S(1)}, f32[16,128]{1,0:T(8,128)S(1)}, u32[]{:S(2)}, u32[]{:S(2)}) collective-permute-start(f32[16,128]{1,0:T(8,128)S(1)} %get-tuple-element.96), channel_id=1, source_target_pairs={{0,24},{1,25},{2,26},{3,27},{4,28},{5,29},{6,30},{7,31},{8,16},{9,... | collective-permute-start | bytes 24584 | tf_op jit(solution)/shard_map/ppermute | solution.py:40
  79.3 3.9 %collective-permute-start.26 = (f32[16,128]{1,0:T(8,128)S(1)}, f32[16,128]{1,0:T(8,128)S(1)}, u32[]{:S(2)}, u32[]{:S(2)}) collective-permute-start(f32[16,128]{1,0:T(8,128)S(1)} %get-tuple-element.97), channel_id=1, source_target_pairs={{0,1},{1,0},{2,3},{3,2},{4,5},{5,4},{6,7},{7,6},{8,9},{9,8},{10,11... | collective-permute-start | bytes 24584 | tf_op jit(solution)/shard_map/ppermute | solution.py:40
  81.8 1.4 %collective-permute-start.27 = (f32[16,128]{1,0:T(8,128)S(1)}, f32[16,128]{1,0:T(8,128)S(1)}, u32[]{:S(2)}, u32[]{:S(2)}) collective-permute-start(f32[16,128]{1,0:T(8,128)S(1)} %get-tuple-element.98), channel_id=1, source_target_pairs={{0,8},{1,9},{2,10},{3,11},{4,12},{5,13},{6,14},{7,15},{8,0},{9,1},... | collective-permute-start | bytes 24584 | tf_op jit(solution)/shard_map/ppermute | solution.py:40
  (13 other events, 32.6 us)

commit v2 on v1

v2 whole, which is shorter than its diff:
```python
import jax
import jax.numpy as jnp
from jax import lax
from jax.experimental import pallas as pl
from jax.experimental.pallas import tpu as pltpu
from jax.sharding import PartitionSpec as P


OMEGA = 0.3
AXES = ("row", "col")
F32, BF16 = jnp.float32, jnp.bfloat16
VM = pl.BlockSpec(memory_space=pltpu.VMEM)
HB = pl.BlockSpec(memory_space=pltpu.HBM)
DMA = pltpu.SemaphoreType.DMA
MIB = 1 << 20

ORDER = ("colb", "rowb", "cola", "rowa")


def partners(rows, cols):
    def flip(i):
        return i + 1 if i % 2 == 0 else i - 1

    def step(i):
        return i + 1 if i % 2 else i - 1

    table = {name: [] for name in ORDER}
    for p in range(rows):
        for q in range(cols):
            inner = 0 <= step(q) < cols
            table["rowa"].append((p * cols + q, flip(p) * cols + q))
            table["rowb"].append((p * cols + q, (step(p) % rows) * cols + q))
            table["cola"].append((p * cols + q, p * cols + flip(q)))
            table["colb"].append((p * cols + q, p * cols + step(q) if inner else flip(p) * cols + q))
    return table


def exchange(sent, table):
    got = {}
    for name in ORDER:
        got[name] = lax.ppermute(sent[name], AXES, table[name])
    return got


def sides():
    p, q = lax.axis_index("row"), lax.axis_index("col")
    rows, cols = lax.axis_size("row"), lax.axis_size("col")
    pp, qq = p & 1, q & 1
    row_in = jnp.logical_and(p > 0, p < rows - 1)
    col_in = jnp.logical_and(q > 0, q < cols - 1)
    return {
        "colb": (3 - qq, 2 + qq, col_in),
        "rowb": (1 - pp, pp, row_in),
        "cola": (2 + qq, 3 - qq, None),
        "rowa": (pp, 1 - pp, None),
    }


def masked(inside, block):
    return block if inside is None else jnp.where(inside, block, 0.0)


def halves(block):
    high = block.astype(BF16).astype(F32)
    low = block - high
    rest = jnp.zeros((16 - 2 * block.shape[0], block.shape[1]), F32)
    return jnp.concatenate([high, low, rest], axis=0).astype(BF16)


def split_weight(weight):
    high = weight.astype(BF16)
    low = (weight - high.astype(F32)).astype(BF16)
    return jnp.concatenate([high, low], axis=1)


def folded(product, loads):
    both = product[:, :128] + product[:, 128:]
    return both[:loads] + both[loads : 2 * loads]


def dot(a, b):
    return jnp.dot(a, b, preferred_element_type=F32)


def named(refs):
    return dict(zip(ORDER, refs))


def fill(ext, x, recv, own, ghosts, loads):
    for b in range(own):
        ext[b] = halves(x[b * loads : (b + 1) * loads])
    for name, (_, slot, inside) in sides().items():
        for g in range(ghosts):
            block = masked(inside, recv[name][g * loads : (g + 1) * loads, :])
            ext[own + slot * ghosts + g] = halves(block)


def coupled(ext, cols, weights, own, count, loads):
    parts = []
    for b in range(own):
        left = jnp.concatenate([ext[cols[b, k]] for k in range(count)], axis=1)
        parts.append(folded(dot(left, weights[b]), loads))
    return jnp.concatenate(parts, axis=0)


def pack(x3, x, own, pick, out, ghosts, loads):
    for b in range(own):
        x3[b] = x[b * loads : (b + 1) * loads]
    for name, (line, _, _) in sides().items():
        for g in range(ghosts):
            out[name][g * loads : (g + 1) * loads, :] = x3[pick(line, g)]


def spread(diag, own, loads):
    return jnp.concatenate(
        [jnp.broadcast_to(diag[b : b + 1, :], (loads, diag.shape[1])) for b in range(own)], axis=0
    )


def call(body, outs, ins, tables=(), scratch=(), limit=16, where=VM):
    n_t, n_i, n_o = len(tables), len(ins), len(outs)

    def kernel(*refs):
        source, rest = refs[:n_t], refs[n_t:]
        inputs, outputs, rest = rest[:n_i], rest[n_i : n_i + n_o], rest[n_i + n_o :]
        smem, rest = rest[:n_t], rest[n_t:]
        copies = []
        if n_t:
            sems, rest = rest[0], rest[1:]
            copies = [
                pltpu.make_async_copy(a, b, sems.at[i])
                for i, (a, b) in enumerate(zip(source, smem))
            ]
        for copy in copies:
            copy.start()
        ready = set()

        def table(i):
            if i not in ready:
                copies[i].wait()
                ready.add(i)
            return smem[i]

        body(table, inputs, outputs, rest)
        for i in range(n_t):
            table(i)

    if where is HB:
        ins = [pltpu.with_memory_space_constraint(i, pltpu.HBM) for i in ins]
    extra = [pltpu.SMEM(t.shape, t.dtype) for t in tables]
    if n_t:
        extra.append(DMA((n_t,)))
    return pl.pallas_call(
        kernel,
        out_shape=[jax.ShapeDtypeStruct(s, d) for s, d in outs],
        in_specs=[where] * (n_t + n_i),
        out_specs=[VM] * n_o,
        scratch_shapes=extra + list(scratch),
        compiler_params=pltpu.CompilerParams(vmem_limit_bytes=limit * MIB),
    )(*tables, *ins)


def on_device(
    rhs, diag0, blocks0, cols0, sends0, pro0, agg0, diag1, blocks1, cols1, sends1, pro1, agg1, cinv
):
    nb, loads, bs = rhs.shape[2:]
    nb1 = diag1.shape[2]
    k0, k1 = cols0.shape[3], cols1.shape[3]
    g0, g1 = sends0.shape[3], sends1.shape[3]
    own_rows, ncu = cinv.shape
    ncb = ncu // bs
    cols_n = lax.axis_size("col")
    devices = lax.axis_size("row") * cols_n
    share = bs // own_rows
    table = partners(lax.axis_size("row"), cols_n)
    n0, n1 = nb * loads, nb1 * loads
    e0n, e1n = nb + 4 * g0, nb1 + 4 * g1
    r_halo0, r_halo1 = g0 * loads, g1 * loads
    r_pro = g1 * bs
    first_rows = r_halo0 + r_pro + 8
    row_n = n1 + nb1

    rhs2 = rhs.reshape(n0, bs)
    d0, d1 = diag0.reshape(nb, bs), diag1.reshape(nb1, bs)
    c0, c1 = cols0.reshape(nb, k0), cols1.reshape(nb1, k1)
    s0, s1t = sends0.reshape(4, g0), sends1.reshape(4, g1).T
    a0, a1 = agg0.reshape(nb), agg1.reshape(nb1)
    m0 = blocks0.reshape(nb, k0, bs, bs)
    m1 = blocks1.reshape(nb1, k1, bs, bs)
    p0, p1 = pro0.reshape(nb, bs, bs), pro1.reshape(nb1, bs, bs)
    x3 = pltpu.VMEM((nb, loads, bs), F32)
    y3 = pltpu.VMEM((nb1, loads, bs), F32)
    ext0 = pltpu.VMEM((e0n, 16, bs), BF16)
    ext1 = pltpu.VMEM((e1n, 16, bs), BF16)
    halo0 = [((r_halo0, bs), F32)] * 4
    halo1 = [((r_halo1, bs), F32)] * 4
    vec0, vec1 = ((n0, bs), F32), ((n1, bs), F32)
    keep = 1.0 - OMEGA

    def first(_, ins, outs, scratch):
        x_o, dd_o, di_o, ee_o, ei_o = outs[:5]
        out = named(outs[5:])
        held, sems, xs = scratch[:-2], scratch[-2], scratch[-1]
        copies = [
            pltpu.make_async_copy(a, b, sems.at[i]) for i, (a, b) in enumerate(zip(ins, held))
        ]
        for copy in copies:
            copy.start()
        for copy in copies:
            copy.wait()
        rhs_r, d0_r, d1_r, s0_r, s1_r, a1_r, p1_r = held
        dd, ee = spread(d0_r[...], nb, loads), spread(d1_r[...], nb1, loads)
        di = OMEGA / dd
        dd_o[...], di_o[...] = dd, di
        ee_o[...], ei_o[...] = ee, OMEGA / ee
        x = rhs_r[...] * di
        x_o[...] = x
        pack(xs, x, nb, lambda line, g: s0_r[line, g], out, g0, loads)
        for name, (line, _, _) in sides().items():
            lines = []
            for g in range(g1):
                pick = s1_r[g, line]
                start = r_halo0 + g * bs
                out[name][start : start + bs, :] = p1_r[pick]
                lines.append(jnp.full((1, bs), a1_r[pick].astype(F32)))
            lines.append(jnp.zeros((8 - g1, bs), F32))
            out[name][r_halo0 + r_pro :, :] = jnp.concatenate(lines, axis=0)

    def ready0(_, ins, outs, scratch):
        (m_r,), (w_o,), (raw, sems) = ins, outs, scratch
        for b in range(nb):
            pltpu.make_async_copy(m_r.at[b], raw.at[b], sems.at[b]).start()

        def block_row(b, carry):
            pltpu.make_async_copy(m_r.at[b], raw.at[b], sems.at[b]).wait()
            for k in range(k0):
                w_o[b, k * bs : (k + 1) * bs, :] = split_weight(raw[b, k].T)
            return carry

        lax.fori_loop(0, nb, block_row, 0)

    def ready1(_, ins, outs, scratch):
        m_r, p0_r, p1_r, cinv_r = ins[:4]
        got = named(ins[4:])
        w_o, p0_o, p0t_o, p1_o, p1t_o, idx_o, wc_o = outs
        for b in range(nb1):
            for k in range(k1):
                w_o[b, k * bs : (k + 1) * bs, :] = split_weight(m_r[b, k].T)
            p1_o[b] = split_weight(p1_r[b])
            p1t_o[b] = split_weight(p1_r[b].T)
        for b in range(nb):
            p0_o[b * bs : (b + 1) * bs, :] = split_weight(p0_r[b])
            p0t_o[b] = split_weight(p0_r[b].T)
        for name, (_, slot, inside) in sides().items():
            for g in range(g1):
                start = r_halo0 + g * bs
                block = masked(inside, got[name][start : start + bs, :])
                p1t_o[nb1 + slot * g1 + g] = split_weight(block.T)
                line = got[name][r_halo0 + r_pro + g : r_halo0 + r_pro + g + 1, :]
                idx_o[slot * g1 + g] = jnp.broadcast_to(line, (loads, bs))
        place = (lax.axis_index("row") * cols_n + lax.axis_index("col")) % share
        for c in range(ncb):
            mine = cinv_r[:, c * bs : (c + 1) * bs]
            tall = jnp.concatenate(
                [jnp.where(place == t, mine, 0.0) for t in range(share)], axis=0
            )
            wc_o[c * bs : (c + 1) * bs, :] = split_weight(tall.T)

    def fine_sweep(table, ins, outs, scratch):
        rhs_r, di_r, x_r, w_r = ins[:4]
        ext, xs = scratch
        x = x_r[...]
        fill(ext, x, named(ins[4:]), nb, g0, loads)
        y = coupled(ext, table(0), w_r, nb, k0, loads)
        x = keep * x + di_r[...] * (rhs_r[...] - y)
        outs[0][...] = x
        s_r = table(1)
        pack(xs, x, nb, lambda line, g: s_r[line, g], named(outs[1:]), g0, loads)

    def fine_last(table, ins, outs, scratch):
        rhs_r, di_r, x_r, w_r = ins[:4]
        x = x_r[...]
        fill(scratch[0], x, named(ins[4:]), nb, g0, loads)
        y = coupled(scratch[0], table(0), w_r, nb, k0, loads)
        outs[0][...] = keep * x + di_r[...] * (rhs_r[...] - y)

    def restrict0(table, ins, outs, scratch):
        rhs_r, dd_r, x_r, w_r, p0_r, ei_r = ins[:6]
        ext, xs = scratch
        x = x_r[...]
        fill(ext, x, named(ins[6:]), nb, g0, loads)
        y = coupled(ext, table(0), w_r, nb, k0, loads)
        res = rhs_r[...] - (dd_r[...] * x + y)
        parts = [halves(res[b * loads : (b + 1) * loads]) for b in range(nb)]
        a_r, s_r = table(1), table(2)
        total = []
        for c in range(nb1):
            left = jnp.concatenate(
                [jnp.where(a_r[b] == c, parts[b], jnp.zeros_like(parts[b])) for b in range(nb)],
                axis=1,
            )
            total.append(folded(dot(left, p0_r[...]), loads))
        b1 = jnp.concatenate(total, axis=0)
        x1 = b1 * ei_r[...]
        outs[0][...], outs[1][...] = b1, x1
        pack(xs, x1, nb1, lambda line, g: s_r[g, line], named(outs[2:]), g1, loads)

    def level_sweep(table, ins, outs, scratch):
        b1_r, ei_r, x_r, w_r = ins[:4]
        ext, xs = scratch
        x = x_r[...]
        fill(ext, x, named(ins[4:]), nb1, g1, loads)
        y = coupled(ext, table(0), w_r, nb1, k1, loads)
        x = keep * x + ei_r[...] * (b1_r[...] - y)
        outs[0][...] = x
        s_r = table(1)
        pack(xs, x, nb1, lambda line, g: s_r[g, line], named(outs[1:]), g1, loads)

    def restrict1(table, ins, outs, scratch):
        b1_r, ee_r, x_r, w_r, p1_r = ins[:5]
        x = x_r[...]
        fill(scratch[0], x, named(ins[5:]), nb1, g1, loads)
        y = coupled(scratch[0], table(0), w_r, nb1, k1, loads)
        res = b1_r[...] - (ee_r[...] * x + y)
        parts = [
            folded(dot(halves(res[b * loads : (b + 1) * loads]), p1_r[b]), loads)
            for b in range(nb1)
        ]
        a_r = table(1)
        index = [jnp.full((1, bs), a_r[b].astype(F32)) for b in range(nb1)]
        group = jnp.concatenate((parts + index) * 4, axis=0)
        for d in range(0, devices, 4):
            outs[0][d * row_n : (d + 4) * row_n, :] = group

    def coarse(_, ins, outs, scratch):
        term_r, wc_r = ins

        def message(d):
            start = d * row_n
            index = [
                jnp.broadcast_to(term_r[start + n1 + b : start + n1 + b + 1, :], (loads, bs))
                for b in range(nb1)
            ]
            return term_r[start : start + n1, :], jnp.concatenate(index, axis=0)

        def finish(block):
            return halves(sum(block[b * loads : (b + 1) * loads] for b in range(nb1)))

        if ncb <= 8:
            sums = [jnp.zeros((n1, bs), F32) for _ in range(ncb)]
            for d in range(devices):
                values, index = message(d)
                sums = [s + jnp.where(index == float(c), values, 0.0) for c, s in enumerate(sums)]
            left = [finish(s) for s in sums]
        else:
            left_s, value_s, index_s = scratch
            for d in range(devices):
                value_s[d], index_s[d] = message(d)

            def gather(c, carry):
                hit = jnp.where(index_s[...] == c.astype(F32), value_s[...], 0.0)
                left_s[c] = finish(jnp.sum(hit, axis=0))
                return carry

            lax.fori_loop(0, ncb, gather, 0)
            left = [left_s[c] for c in range(ncb)]
        mine = folded(dot(jnp.concatenate(left, axis=1), wc_r[...]), loads)
        outs[0][...] = jnp.broadcast_to(mine[None], outs[0].shape)

    def level_correct(table, ins, outs, scratch):
        sol_r, b1_r, ei_r, x_r, w_r, p1t_r, idx_r = ins[:7]
        got = named(ins[7:])
        ext, xs, cx = scratch
        blocks = [sum(sol_r[c * share + t] for t in range(share)) for c in range(ncb)]
        for c in range(ncb):
            cx[c] = blocks[c]
        for name, (_, slot, inside) in sides().items():
            for g in range(g1):
                place = slot * g1 + g
                index = idx_r[place]
                pick = jnp.zeros((loads, bs), F32)
                for c in range(ncb):
                    pick = jnp.where(index == float(c), blocks[c], pick)
                moved = folded(dot(halves(pick), p1t_r[nb1 + place]), loads)
                old = got[name][g * loads : (g + 1) * loads, :]
                ext[nb1 + place] = halves(masked(inside, old + moved))
        a_r = table(2)
        lifted = [folded(dot(halves(cx[a_r[b]]), p1t_r[b]), loads) for b in range(nb1)]
        x = x_r[...] + jnp.concatenate(lifted, axis=0)
        for b in range(nb1):
            ext[b] = halves(x[b * loads : (b + 1) * loads])
        y = coupled(ext, table(0), w_r, nb1, k1, loads)
        x = keep * x + ei_r[...] * (b1_r[...] - y)
        outs[0][...] = x
        s_r = table(1)
        pack(xs, x, nb1, lambda line, g: s_r[g, line], named(outs[1:]), g1, loads)

    def lift(table, ins, outs, scratch):
        b1_r, ei_r, x_r, w_r, p0t_r, x0_r = ins[:6]
        ext, xs = scratch
        x = x_r[...]
        fill(ext, x, named(ins[6:]), nb1, g1, loads)
        y = coupled(ext, table(0), w_r, nb1, k1, loads)
        x = keep * x + ei_r[...] * (b1_r[...] - y)
        for b in range(nb1):
            ext[b] = halves(x[b * loads : (b + 1) * loads])
        a_r, s_r = table(1), table(2)
        parts = [folded(dot(ext[a_r[b]], p0t_r[b]), loads) for b in range(nb)]
        fine = x0_r[...] + jnp.concatenate(parts, axis=0)
        outs[0][...] = fine
        pack(xs, fine, nb, lambda line, g: s_r[line, g], named(outs[1:]), g0, loads)

    def swap(sent):
        got = exchange(named(sent), table)
        return [got[name] for name in ORDER]

    firsts = [rhs2, d0, d1, s0, s1t, a1, p1]
    x0, dd, di, ee, ei, *sent = call(
        first,
        [vec0, vec0, vec0, vec1, vec1] + [((first_rows, bs), F32)] * 4,
        firsts,
        scratch=[
            (pltpu.VMEM if f.dtype == F32 else pltpu.SMEM)(f.shape, f.dtype) for f in firsts
        ]
        + [DMA((len(firsts),)), x3],
        where=HB,
    )
    (w0,) = call(
        ready0,
        [((nb, k0 * bs, 2 * bs), BF16)],
        [m0],
        scratch=[pltpu.VMEM(m0.shape, F32), DMA((nb,))],
        limit=24,
        where=HB,
    )
    got = swap(sent)
    x0, *sent = call(fine_sweep, [vec0] + halo0, [rhs2, di, x0, w0, *got], [c0, s0], [ext0, x3])
    w1, p0w, p0t, p1w, p1t, idx, wc = call(
        ready1,
        [
            ((nb1, k1 * bs, 2 * bs), BF16),
            ((nb * bs, 2 * bs), BF16),
            ((nb, bs, 2 * bs), BF16),
            ((nb1, bs, 2 * bs), BF16),
            ((e1n, bs, 2 * bs), BF16),
            ((4 * g1, loads, bs), F32),
            ((ncu, 2 * bs), BF16),
        ],
        [m1, p0, p1, cinv, *got],
        limit=24,
    )
    got = swap(sent)
    b1, x1, *sent = call(
        restrict0,
        [vec1, vec1] + halo1,
        [rhs2, dd, x0, w0, p0w, ei, *got],
        [c0, a0, s1t],
        [ext0, y3],
    )
    got = swap(sent)
    x1, *sent = call(level_sweep, [vec1] + halo1, [b1, ei, x1, w1, *got], [c1, s1t], [ext1, y3])
    got = swap(sent)
    (terms,) = call(
        restrict1, [((devices * row_n, bs), F32)], [b1, ee, x1, w1, p1w, *got], [c1, a1], [ext1]
    )
    terms = lax.all_to_all(terms.reshape(devices, loads + 1, nb1, bs), AXES, 0, 0, tiled=True)
    many = [] if ncb <= 8 else [pltpu.VMEM((devices, n1, bs), F32)] * 2
    (mine,) = call(
        coarse,
        [((devices, loads, bs), F32)],
        [terms.reshape(devices * row_n, bs), wc],
        scratch=[pltpu.VMEM((ncb, 16, bs), BF16)] + many,
        limit=24,
    )
    sol = lax.all_to_all(mine, AXES, 0, 0, tiled=True)
    x1, *sent = call(
        level_correct,
        [vec1] + halo1,
        [sol, b1, ei, x1, w1, p1t, idx, *got],
        [c1, s1t, a1],
        [ext1, y3, pltpu.VMEM((ncb, loads, bs), F32)],
    )
    got = swap(sent)
    x0, *sent = call(
        lift, [vec0] + halo0, [b1, ei, x1, w1, p0t, x0, *got], [c1, a0, s0], [ext1, x3]
    )
    got = swap(sent)
    x0, *sent = call(fine_sweep, [vec0] + halo0, [rhs2, di, x0, w0, *got], [c0, s0], [ext0, x3])
    got = swap(sent)
    (x0,) = call(fine_last, [vec0], [rhs2, di, x0, w0, *got], [c0], [ext0])
    return x0.reshape(1, 1, nb, loads, bs)


def solution(mesh):
    return jax.shard_map(
        on_device,
        mesh=mesh,
        in_specs=(
            P("row", "col", None, None, None),
            P("row", "col", None, None),
            P("row", "col", None, None, None, None),
            P("row", "col", None, None),
            P("row", "col", None, None),
            P("row", "col", None, None, None),
            P("row", "col", None),
            P("row", "col", None, None),
            P("row", "col", None, None, None, None),
            P("row", "col", None, None),
            P("row", "col", None, None),
            P("row", "col", None, None, None),
            P("row", "col", None),
            P(("row", "col"), None),
        ),
        out_specs=P("row", "col", None, None, None),
        check_vma=False,
    )
```

time: 86.2 us -> 78.6 us (0.912)
  local copies, waits for them, and re-layouts: 8.25 us -> 0.06 us
  blocking collectives: 24.4 us -> 22.1 us
  Pallas kernels: 16.4 us -> 18.2 us
  waiting for transfers between devices: 6.63 us -> 7.61 us
    unnamed x34 -> x22, local copies, waits for them, and re-layouts: 7.48 us -> 0.06 us
    all_to_all x1, blocking collectives: 14.1 us -> 12.2 us  [on_device(): lax.all_to_all(terms.reshape(devices, loads + 1, nb1, bs), AXES, 0, 0, ti...]
    pallas_call x12, Pallas kernels: 16.4 us -> 18.2 us  [call(): pl.pallas_call(kernel, out_shape=[jax.ShapeDtypeStruct(s, d) for s, d in...]
    ppermute x28, waiting for transfers between devices: 6.63 us -> 7.61 us  [exchange(): got[name] = lax.ppermute(sent[name], AXES, table[name])]
  transfers between devices with their start and end apart: 28 -> 28, of which waited for: 10 -> 10; matrix products, arithmetic and copies ran while one was open for 0% -> 0% of each run, Pallas kernels for 4% -> 6%
where the time goes in v2:
time: 78.6 us; the launch traced here: 77.9 us
  starting transfers between devices  29.7 us (38%)
  blocking collectives  22.1 us (28%)
  Pallas kernels  18.2 us (23%)
  waiting for transfers between devices  7.61 us (10%)
    ppermute x28, starting transfers between devices, exchange(): got[name] = lax.ppermute(sent[name], AXES, table[name])  29.7 us
    pallas_call x12, Pallas kernels, call(): pl.pallas_call(kernel, out_shape=[jax.ShapeDtypeStruct(s, d) for s, d in...  18.2 us
    all_to_all x1, blocking collectives, on_device(): lax.all_to_all(terms.reshape(devices, loads + 1, nb1, bs), AXES, 0, 0, ti...  12.2 us
    all_to_all x1, blocking collectives, on_device(): sol = lax.all_to_all(mine, AXES, 0, 0, tiled=True)  9.93 us
    ppermute x28, waiting for transfers between devices, exchange(): got[name] = lax.ppermute(sent[name], AXES, table[name])  7.61 us
  transfers between devices with their start and end apart: 28, of which 10 were waited for; matrix products, arithmetic and copies ran while one was open for 0% of the time, Pallas kernels for 6%

profile of v2, /device:TPU:1, one launch (start us, length us, event | category | flops | bytes accessed | tf_op | source)
XLA Modules:
  0.0 77.9 jit_solution(8465902012092636725)
XLA Ops:
  0.0 1.1 %shard_map.136 = (f32[32,128]{1,0:T(8,128)S(1)}, f32[32,128]{1,0:T(8,128)S(1)}, f32[32,128]{1,0:T(8,128)S(1)}, f32[8,128]{1,0:T(8,128)S(1)}, f32[8,128]{1,0:T(8,...) custom-call(f32[32,128]{1,0:T(8,128)} %bitcast.24, ...), custom_call_target="tpu_custom_call" | custom-call | tf_op jit(solution)/shard_map/pallas_call | solution.py:153
  1.2 2.6 %collective-permute-start.1 = (f32[280,128]{1,0:T(8,128)S(1)}, f32[280,128]{1,0:T(8,128)S(1)}, u32[]{:S(2)}, u32[]{:S(2)}) collective-permute-start(f32[280,128]{1,0:T(8,128)S(1)} %get-tuple-element.56), channel_id=1, source_target_pairs={{0,24},{1,25},{2,26},{3,27},{4,28},{5,29},{6,30},{7,31},{8,16},{9,... | collective-permute-start | bytes 430088 | tf_op jit(solution)/shard_map/ppermute | solution.py:41
  3.8 2.7 %collective-permute-start.2 = (f32[280,128]{1,0:T(8,128)S(1)}, f32[280,128]{1,0:T(8,128)S(1)}, u32[]{:S(2)}, u32[]{:S(2)}) collective-permute-start(f32[280,128]{1,0:T(8,128)S(1)} %get-tuple-element.57), channel_id=1, source_target_pairs={{0,1},{1,0},{2,3},{3,2},{4,5},{5,4},{6,7},{7,6},{8,9},{9,8},{10,11... | collective-permute-start | bytes 430088 | tf_op jit(solution)/shard_map/ppermute | solution.py:41
  6.5 3.8 %shard_map.137.refs_5_.refs_6_.refs_4_ = bf16[8,1792,256]{2,1,0:T(8,128)(2,1)S(1)} custom-call(f32[8,14,128,128]{3,2,1,0:T(8,128)} %bitcast.50), custom_call_target="tpu_custom_call" | custom-call | tf_op jit(solution)/shard_map/pallas_call | solution.py:153
  10.8 1.7 %shard_map.138 = (f32[32,128]{1,0:T(8,128)S(1)}, f32[16,128]{1,0:T(8,128)S(1)}, f32[16,128]{1,0:T(8,128)S(1)}, f32[16,128]{1,0:T(8,128)S(1)}, f32[16,128]{1,0:T(8,128)S(1)}) custom-call(s32[8,14]{1,0:T(8,128)S(1)} %bitcast.29, s32[4,4]{1,0:T(4,128)S(1)} %bitcast.34, f32[32,128]{1,0:T(8,128)S(1)} %bitcast.25, ...), custom_call_target="tpu_custom_call" | custom-call | tf_op jit(solution)/shard_map/pallas_call | solution.py:153
  13.0 1.2 %collective-permute-start.5 = (f32[16,128]{1,0:T(8,128)S(1)}, f32[16,128]{1,0:T(8,128)S(1)}, u32[]{:S(2)}, u32[]{:S(2)}) collective-permute-start(f32[16,128]{1,0:T(8,128)S(1)} %get-tuple-element.63), channel_id=1, source_target_pairs={{0,24},{1,25},{2,26},{3,27},{4,28},{5,29},{6,30},{7,31},{8,16},{9,... | collective-permute-start | bytes 24584 | tf_op jit(solution)/shard_map/ppermute | solution.py:41
  14.2 3.6 %collective-permute-start.6 = (f32[16,128]{1,0:T(8,128)S(1)}, f32[16,128]{1,0:T(8,128)S(1)}, u32[]{:S(2)}, u32[]{:S(2)}) collective-permute-start(f32[16,128]{1,0:T(8,128)S(1)} %get-tuple-element.64), channel_id=1, source_target_pairs={{0,1},{1,0},{2,3},{3,2},{4,5},{5,4},{6,7},{7,6},{8,9},{9,8},{10,11... | collective-permute-start | bytes 24584 | tf_op jit(solution)/shard_map/ppermute | solution.py:41
  17.9 1.0 %shard_map.139 = (bf16[2,1792,256]{2,1,0:T(8,128)(2,1)S(1)}, bf16[1024,256]{1,0:T(8,128)(2,1)S(1)}, bf16[8,128,256]{2,1,0:T(8,128)(2,1)S(1)}, bf16[2,128,256]{2,...) custom-call(f32[2,14,128,128]{3,2,1,0:T(8,128)S(1)} %bitcast.18, ...), custom_call_target="tpu_custom_call" | custom-call | tf_op jit(solution)/shard_map/pallas_call | solution.py:153
  19.2 2.0 %shard_map.140 = (f32[8,128]{1,0:T(8,128)S(1)}, f32[8,128]{1,0:T(8,128)S(1)}, f32[8,128]{1,0:T(8,128)S(1)}, f32[8,128]{1,0:T(8,128)S(1)}, f32[8,128]{1,0:T(8,128)S(1)}, /*index=5*/f32[8,128]{1,0:T(8,128)S(1)}) custom-call(s32[8,14]{1,0:T(8,128)S(1)} %bitcast.30, s32[8]{0:T(128)S(1)} %bitcast.48, s32[2,4]{1,0:T(2,128)S(1)} %bitcast.38, ...), custom_call_target="tpu_custom_call" | custom-call | tf_op jit(solution)/shard_map/pallas_call | solution.py:153
  21.2 1.2 %collective-permute-start.10 = (f32[8,128]{1,0:T(8,128)S(1)}, f32[8,128]{1,0:T(8,128)S(1)}, u32[]{:S(2)}, u32[]{:S(2)}) collective-permute-start(f32[8,128]{1,0:T(8,128)S(1)} %get-tuple-element.72), channel_id=1, source_target_pairs={{0,1},{1,0},{2,3},{3,2},{4,5},{5,4},{6,7},{7,6},{8,9},{9,8},{10,11... | collective-permute-start | bytes 12296 | tf_op jit(solution)/shard_map/ppermute | solution.py:41
  22.4 1.2 %collective-permute-start.11 = (f32[8,128]{1,0:T(8,128)S(1)}, f32[8,128]{1,0:T(8,128)S(1)}, u32[]{:S(2)}, u32[]{:S(2)}) collective-permute-start(f32[8,128]{1,0:T(8,128)S(1)} %get-tuple-element.73), channel_id=1, source_target_pairs={{0,8},{1,9},{2,10},{3,11},{4,12},{5,13},{6,14},{7,15},{8,0},{9,1},... | collective-permute-start | bytes 12296 | tf_op jit(solution)/shard_map/ppermute | solution.py:41
  23.6 0.7 collective-permute-start.9
  24.8 2.0 %collective-permute-done.9.refs_7_ = f32[8,128]{1,0:T(8,128)S(1)} collective-permute-done((f32[8,128]{1,0:T(8,128)S(1)}, f32[8,128]{1,0:T(8,128)S(1)}, u32[]{:S(2)}, u32[]{:S(2)}) %collective-permute-start.9) | collective-permute-done | bytes 4128 | tf_op jit(solution)/shard_map/ppermute | solution.py:41
  26.8 1.0 %shard_map.141 = (f32[8,128]{1,0:T(8,128)S(1)}, f32[8,128]{1,0:T(8,128)S(1)}, f32[8,128]{1,0:T(8,128)S(1)}, f32[8,128]{1,0:T(8,128)S(1)}, f32[8,128]{1,0:T(8,128)S(1)}) custom-call(s32[2,14]{1,0:T(2,128)S(1)} %bitcast.41, s32[2,4]{1,0:T(2,128)S(1)} %bitcast.39, f32[8,128]{1,0:T(8,128)S(1)} %get-tuple-element.66.refs_2_.refs_4_.refs_3_, ...), custom_call_target="tpu_custom_call" | custom-call | tf_op jit(solution)/shard_map/pallas_call | solution.py:153
  28.5 3.6 %collective-permute-start.14 = (f32[8,128]{1,0:T(8,128)S(1)}, f32[8,128]{1,0:T(8,128)S(1)}, u32[]{:S(2)}, u32[]{:S(2)}) collective-permute-start(f32[8,128]{1,0:T(8,128)S(1)} %get-tuple-element.78), channel_id=1, source_target_pairs={{0,1},{1,0},{2,3},{3,2},{4,5},{5,4},{6,7},{7,6},{8,9},{9,8},{10,11... | collective-permute-start | bytes 12296 | tf_op jit(solution)/shard_map/ppermute | solution.py:41
  32.2 1.2 %collective-permute-done.14.refs_9_.refs_12_ = f32[8,128]{1,0:T(8,128)S(1)} collective-permute-done((f32[8,128]{1,0:T(8,128)S(1)}, f32[8,128]{1,0:T(8,128)S(1)}, u32[]{:S(2)}, u32[]{:S(2)}) %collective-permute-start.14) | collective-permute-done | bytes 4128 | tf_op jit(solution)/shard_map/ppermute | solution.py:41
  33.4 1.1 %shard_map.142 = f32[320,128]{1,0:T(8,128)S(1)} custom-call(s32[2,14]{1,0:T(2,128)S(1)} %bitcast.42, s32[2]{0:T(128)S(1)} %bitcast.46, f32[8,128]{1,0:T(8,128)S(1)} %get-tuple-element.66.refs_2_.refs_4_.refs_3_, f32[8,128]{1,0:T(8,128)S(1)} %get-tuple-element.67.refs_3_, f32[8,128]{1,0:T(8,128)S(1)} %get-tuple-element.74.refs_4_.refs_6_, ...), custom_call_target="tpu_custom_call" | custom-call | tf_op jit(solution)/shard_map/pallas_call | solution.py:153
  34.5 12.2 %all_to_all.10 = f32[32,5,2,128]{3,2,1,0:T(2,128)S(1)} all-to-all(f32[32,5,2,128]{3,2,1,0:T(2,128)S(1)} %bitcast.19), channel_id=1, replica_groups=mesh['row'=4,'col'=8] {'row','col'}, dimensions={0} | all-to-all | bytes 327680 | tf_op jit(solution)/shard_map/all_to_all | solution.py:466
  47.0 9.9 %all_to_all.11.refs_3_ = f32[32,4,128]{2,1,0:T(4,128)S(1)} all-to-all(f32[32,4,128]{2,1,0:T(4,128)S(1)} %shard_map.143), channel_id=1, replica_groups=mesh['row'=4,'col'=8] {'row','col'}, dimensions={0} | all-to-all | bytes 131072 | tf_op jit(solution)/shard_map/all_to_all | solution.py:475
  56.9 1.2 %shard_map.144 = (f32[8,128]{1,0:T(8,128)S(1)}, f32[8,128]{1,0:T(8,128)S(1)}, f32[8,128]{1,0:T(8,128)S(1)}, f32[8,128]{1,0:T(8,128)S(1)}, f32[8,128]{1,0:T(8,128)S(1)}) custom-call(s32[2,14]{1,0:T(2,128)S(1)} %bitcast.43, s32[2,4]{1,0:T(2,128)S(1)} %bitcast.40, s32[2]{0:T(128)S(1)} %bitcast.47, f32[32,4,128]{2,1,0:T(4,128)S(1)} %all_to_all.11.refs_3_, ...), custom_call_target="tpu_custom_call" | custom-call | tf_op jit(solution)/shard_map/pallas_call | solution.py:153
  58.9 1.5 %collective-permute-start.18 = (f32[8,128]{1,0:T(8,128)S(1)}, f32[8,128]{1,0:T(8,128)S(1)}, u32[]{:S(2)}, u32[]{:S(2)}) collective-permute-start(f32[8,128]{1,0:T(8,128)S(1)} %get-tuple-element.87), channel_id=1, source_target_pairs={{0,1},{1,0},{2,3},{3,2},{4,5},{5,4},{6,7},{7,6},{8,9},{9,8},{10,11... | collective-permute-start | bytes 12296 | tf_op jit(solution)/shard_map/ppermute | solution.py:41
  60.7 0.9 %collective-permute-done.17.refs_10_ = f32[8,128]{1,0:T(8,128)S(1)} collective-permute-done((f32[8,128]{1,0:T(8,128)S(1)}, f32[8,128]{1,0:T(8,128)S(1)}, u32[]{:S(2)}, u32[]{:S(2)}) %collective-permute-start.17) | collective-permute-done | bytes 4128 | tf_op jit(solution)/shard_map/ppermute | solution.py:41
  61.6 1.2 %shard_map.145 = (f32[32,128]{1,0:T(8,128)S(1)}, f32[16,128]{1,0:T(8,128)S(1)}, f32[16,128]{1,0:T(8,128)S(1)}, f32[16,128]{1,0:T(8,128)S(1)}, f32[16,128]{1,0:T(8,128)S(1)}) custom-call(s32[2,14]{1,0:T(2,128)S(1)} %bitcast.44, s32[8]{0:T(128)S(1)} %bitcast.49, s32[4,4]{1,0:T(4,128)S(1)} %bitcast.35, f32[8,128]{1,0:T(8,128)S(1)} %get-tuple-element.66.refs_2_.refs_4_.refs_3_, ...), custom_call_target="tpu_custom_call" | custom-call | tf_op jit(solution)/shard_map/pallas_call | solution.py:153
  62.8 1.4 %collective-permute-start.20 = (f32[16,128]{1,0:T(8,128)S(1)}, f32[16,128]{1,0:T(8,128)S(1)}, u32[]{:S(2)}, u32[]{:S(2)}) collective-permute-start(f32[16,128]{1,0:T(8,128)S(1)} %get-tuple-element.90), channel_id=1, source_target_pairs={{0,8},{1,2},{2,1},{3,4},{4,3},{5,6},{6,5},{7,15},{8,0},{9,10},{10,... | collective-permute-start | bytes 24584 | tf_op jit(solution)/shard_map/ppermute | solution.py:41
  64.2 1.0 %collective-permute-start.21 = (f32[16,128]{1,0:T(8,128)S(1)}, f32[16,128]{1,0:T(8,128)S(1)}, u32[]{:S(2)}, u32[]{:S(2)}) collective-permute-start(f32[16,128]{1,0:T(8,128)S(1)} %get-tuple-element.91), channel_id=1, source_target_pairs={{0,24},{1,25},{2,26},{3,27},{4,28},{5,29},{6,30},{7,31},{8,16},{9,... | collective-permute-start | bytes 24584 | tf_op jit(solution)/shard_map/ppermute | solution.py:41
  65.2 2.7 %collective-permute-start.22 = (f32[16,128]{1,0:T(8,128)S(1)}, f32[16,128]{1,0:T(8,128)S(1)}, u32[]{:S(2)}, u32[]{:S(2)}) collective-permute-start(f32[16,128]{1,0:T(8,128)S(1)} %get-tuple-element.92), channel_id=1, source_target_pairs={{0,1},{1,0},{2,3},{3,2},{4,5},{5,4},{6,7},{7,6},{8,9},{9,8},{10,11... | collective-permute-start | bytes 24584 | tf_op jit(solution)/shard_map/ppermute | solution.py:41
  67.9 1.0 %collective-permute-done.22.refs_8_ = f32[16,128]{1,0:T(8,128)S(1)} collective-permute-done((f32[16,128]{1,0:T(8,128)S(1)}, f32[16,128]{1,0:T(8,128)S(1)}, u32[]{:S(2)}, u32[]{:S(2)}) %collective-permute-start.22) | collective-permute-done | bytes 8224 | tf_op jit(solution)/shard_map/ppermute | solution.py:41
  69.1 1.7 %shard_map.146 = (f32[32,128]{1,0:T(8,128)S(1)}, f32[16,128]{1,0:T(8,128)S(1)}, f32[16,128]{1,0:T(8,128)S(1)}, f32[16,128]{1,0:T(8,128)S(1)}, f32[16,128]{1,0:T(8,128)S(1)}) custom-call(s32[8,14]{1,0:T(8,128)S(1)} %bitcast.31, s32[4,4]{1,0:T(4,128)S(1)} %bitcast.36, f32[32,128]{1,0:T(8,128)S(1)} %bitcast.27, ...), custom_call_target="tpu_custom_call" | custom-call | tf_op jit(solution)/shard_map/pallas_call | solution.py:153
  71.1 0.7 collective-permute-start.25
  71.8 2.7 %collective-permute-start.26 = (f32[16,128]{1,0:T(8,128)S(1)}, f32[16,128]{1,0:T(8,128)S(1)}, u32[]{:S(2)}, u32[]{:S(2)}) collective-permute-start(f32[16,128]{1,0:T(8,128)S(1)} %get-tuple-element.97), channel_id=1, source_target_pairs={{0,1},{1,0},{2,3},{3,2},{4,5},{5,4},{6,7},{7,6},{8,9},{9,8},{10,11... | collective-permute-start | bytes 24584 | tf_op jit(solution)/shard_map/ppermute | solution.py:41
  74.5 1.1 %collective-permute-done.26.refs_7_ = f32[16,128]{1,0:T(8,128)S(1)} collective-permute-done((f32[16,128]{1,0:T(8,128)S(1)}, f32[16,128]{1,0:T(8,128)S(1)}, u32[]{:S(2)}, u32[]{:S(2)}) %collective-permute-start.26) | collective-permute-done | bytes 8224 | tf_op jit(solution)/shard_map/ppermute | solution.py:41
  75.7 2.3 %shard_map.147 = f32[32,128]{1,0:T(8,128)} custom-call(s32[8,14]{1,0:T(8,128)S(1)} %bitcast.32, f32[32,128]{1,0:T(8,128)S(1)} %bitcast.28, f32[32,128]{1,0:T(8,128)S(1)} %get-tuple-element.52.refs_3_.refs_2_, f32[32,128]{1,0:T(8,128)S(1)} %get-tuple-element.94.refs_3_, bf16[8,1792,256]{2,1,0:T(8,128)(2,1)S(1)} %shard_map.137.refs_5_.refs_6_.refs_4_, ...), custom_call_target="tpu_custom_call" | custom-call | tf_op jit(solution)/shard_map/pallas_call | solution.py:153
  (60 shorter events, 4.5 us)
Async XLA Ops:
  1.1 9.3 %collective-permute-start = (f32[280,128]{1,0:T(8,128)S(1)}, f32[280,128]{1,0:T(8,128)S(1)}, u32[]{:S(2)}, u32[]{:S(2)}) collective-permute-start(f32[280,128]{1,0:T(8,128)S(1)} %get-tuple-element.55), channel_id=1, source_target_pairs={{0,8},{1,2},{2,1},{3,4},{4,3},{5,6},{6,5},{7,15},{8,0},{9,10},{10,... | collective-permute-start | bytes 430088 | tf_op jit(solution)/shard_map/ppermute | solution.py:41
  1.2 9.2 %collective-permute-start.1 = (f32[280,128]{1,0:T(8,128)S(1)}, f32[280,128]{1,0:T(8,128)S(1)}, u32[]{:S(2)}, u32[]{:S(2)}) collective-permute-start(f32[280,128]{1,0:T(8,128)S(1)} %get-tuple-element.56), channel_id=1, source_target_pairs={{0,24},{1,25},{2,26},{3,27},{4,28},{5,29},{6,30},{7,31},{8,16},{9,... | collective-permute-start | bytes 430088 | tf_op jit(solution)/shard_map/ppermute | solution.py:41
  3.8 6.9 %collective-permute-start.2 = (f32[280,128]{1,0:T(8,128)S(1)}, f32[280,128]{1,0:T(8,128)S(1)}, u32[]{:S(2)}, u32[]{:S(2)}) collective-permute-start(f32[280,128]{1,0:T(8,128)S(1)} %get-tuple-element.57), channel_id=1, source_target_pairs={{0,1},{1,0},{2,3},{3,2},{4,5},{5,4},{6,7},{7,6},{8,9},{9,8},{10,11... | collective-permute-start | bytes 430088 | tf_op jit(solution)/shard_map/ppermute | solution.py:41
  6.5 4.3 %collective-permute-start.3 = (f32[280,128]{1,0:T(8,128)S(1)}, f32[280,128]{1,0:T(8,128)S(1)}, u32[]{:S(2)}, u32[]{:S(2)}) collective-permute-start(f32[280,128]{1,0:T(8,128)S(1)} %get-tuple-element.58), channel_id=1, source_target_pairs={{0,8},{1,9},{2,10},{3,11},{4,12},{5,13},{6,14},{7,15},{8,0},{9,1},... | collective-permute-start | bytes 430088 | tf_op jit(solution)/shard_map/ppermute | solution.py:41
  10.3 8.9 %copy-start.7 = (s32[1,1,4,2]{2,3,1,0:T(2,128)S(1)}, s32[1,1,4,2]{2,3,1,0:T(2,128)}, u32[]{:S(2)}) copy-start(s32[1,1,4,2]{2,3,1,0:T(2,128)} %param.24) | copy-start | bytes 100
  10.3 8.9 %copy-start.10 = (s32[1,1,8]{2,1,0:T(1,128)S(1)}, s32[1,1,8]{2,1,0:T(1,128)}, u32[]{:S(2)}) copy-start(s32[1,1,8]{2,1,0:T(1,128)} %param.20) | copy-start | bytes 100
  12.5 14.3 %copy-start.8 = (s32[1,1,2,14]{3,2,1,0:T(2,128)S(1)}, s32[1,1,2,14]{3,2,1,0:T(2,128)}, u32[]{:S(2)}) copy-start(s32[1,1,2,14]{3,2,1,0:T(2,128)} %param.23) | copy-start | bytes 340
  12.5 20.9 %copy-start.9 = (s32[1,1,2]{2,1,0:T(1,128)S(1)}, s32[1,1,2]{2,1,0:T(1,128)}, u32[]{:S(2)}) copy-start(s32[1,1,2]{2,1,0:T(1,128)} %param.26) | copy-start | bytes 28
  12.5 6.4 %collective-permute-start.4 = (f32[16,128]{1,0:T(8,128)S(1)}, f32[16,128]{1,0:T(8,128)S(1)}, u32[]{:S(2)}, u32[]{:S(2)}) collective-permute-start(f32[16,128]{1,0:T(8,128)S(1)} %get-tuple-element.62), channel_id=1, source_target_pairs={{0,8},{1,2},{2,1},{3,4},{4,3},{5,6},{6,5},{7,15},{8,0},{9,10},{10,... | collective-permute-start | bytes 24584 | tf_op jit(solution)/shard_map/ppermute | solution.py:41
  13.0 6.0 %collective-permute-start.5 = (f32[16,128]{1,0:T(8,128)S(1)}, f32[16,128]{1,0:T(8,128)S(1)}, u32[]{:S(2)}, u32[]{:S(2)}) collective-permute-start(f32[16,128]{1,0:T(8,128)S(1)} %get-tuple-element.63), channel_id=1, source_target_pairs={{0,24},{1,25},{2,26},{3,27},{4,28},{5,29},{6,30},{7,31},{8,16},{9,... | collective-permute-start | bytes 24584 | tf_op jit(solution)/shard_map/ppermute | solution.py:41
  14.2 5.0 %collective-permute-start.6 = (f32[16,128]{1,0:T(8,128)S(1)}, f32[16,128]{1,0:T(8,128)S(1)}, u32[]{:S(2)}, u32[]{:S(2)}) collective-permute-start(f32[16,128]{1,0:T(8,128)S(1)} %get-tuple-element.64), channel_id=1, source_target_pairs={{0,1},{1,0},{2,3},{3,2},{4,5},{5,4},{6,7},{7,6},{8,9},{9,8},{10,11... | collective-permute-start | bytes 24584 | tf_op jit(solution)/shard_map/ppermute | solution.py:41
  17.8 1.4 %collective-permute-start.7 = (f32[16,128]{1,0:T(8,128)S(1)}, f32[16,128]{1,0:T(8,128)S(1)}, u32[]{:S(2)}, u32[]{:S(2)}) collective-permute-start(f32[16,128]{1,0:T(8,128)S(1)} %get-tuple-element.65), channel_id=1, source_target_pairs={{0,8},{1,9},{2,10},{3,11},{4,12},{5,13},{6,14},{7,15},{8,0},{9,1},... | collective-permute-start | bytes 24584 | tf_op jit(solution)/shard_map/ppermute | solution.py:41
  21.2 3.1 %collective-permute-start.10 = (f32[8,128]{1,0:T(8,128)S(1)}, f32[8,128]{1,0:T(8,128)S(1)}, u32[]{:S(2)}, u32[]{:S(2)}) collective-permute-start(f32[8,128]{1,0:T(8,128)S(1)} %get-tuple-element.72), channel_id=1, source_target_pairs={{0,1},{1,0},{2,3},{3,2},{4,5},{5,4},{6,7},{7,6},{8,9},{9,8},{10,11... | collective-permute-start | bytes 12296 | tf_op jit(solution)/shard_map/ppermute | solution.py:41
  22.4 2.1 %collective-permute-start.11 = (f32[8,128]{1,0:T(8,128)S(1)}, f32[8,128]{1,0:T(8,128)S(1)}, u32[]{:S(2)}, u32[]{:S(2)}) collective-permute-start(f32[8,128]{1,0:T(8,128)S(1)} %get-tuple-element.73), channel_id=1, source_target_pairs={{0,8},{1,9},{2,10},{3,11},{4,12},{5,13},{6,14},{7,15},{8,0},{9,1},... | collective-permute-start | bytes 12296 | tf_op jit(solution)/shard_map/ppermute | solution.py:41
  23.6 1.2 %collective-permute-start.8 = (f32[8,128]{1,0:T(8,128)S(1)}, f32[8,128]{1,0:T(8,128)S(1)}, u32[]{:S(2)}, u32[]{:S(2)}) collective-permute-start(f32[8,128]{1,0:T(8,128)S(1)} %get-tuple-element.70), channel_id=1, source_target_pairs={{0,8},{1,2},{2,1},{3,4},{4,3},{5,6},{6,5},{7,15},{8,0},{9,10},{10,... | collective-permute-start | bytes 12296 | tf_op jit(solution)/shard_map/ppermute | solution.py:41
  23.6 3.1 %collective-permute-start.9 = (f32[8,128]{1,0:T(8,128)S(1)}, f32[8,128]{1,0:T(8,128)S(1)}, u32[]{:S(2)}, u32[]{:S(2)}) collective-permute-start(f32[8,128]{1,0:T(8,128)S(1)} %get-tuple-element.71), channel_id=1, source_target_pairs={{0,24},{1,25},{2,26},{3,27},{4,28},{5,29},{6,30},{7,31},{8,16},{9,... | collective-permute-start | bytes 12296 | tf_op jit(solution)/shard_map/ppermute | solution.py:41
  27.7 4.5 %collective-permute-start.12 = (f32[8,128]{1,0:T(8,128)S(1)}, f32[8,128]{1,0:T(8,128)S(1)}, u32[]{:S(2)}, u32[]{:S(2)}) collective-permute-start(f32[8,128]{1,0:T(8,128)S(1)} %get-tuple-element.76), channel_id=1, source_target_pairs={{0,8},{1,2},{2,1},{3,4},{4,3},{5,6},{6,5},{7,15},{8,0},{9,10},{10,... | collective-permute-start | bytes 12296 | tf_op jit(solution)/shard_map/ppermute | solution.py:41
  28.2 4.0 %collective-permute-start.13 = (f32[8,128]{1,0:T(8,128)S(1)}, f32[8,128]{1,0:T(8,128)S(1)}, u32[]{:S(2)}, u32[]{:S(2)}) collective-permute-start(f32[8,128]{1,0:T(8,128)S(1)} %get-tuple-element.77), channel_id=1, source_target_pairs={{0,24},{1,25},{2,26},{3,27},{4,28},{5,29},{6,30},{7,31},{8,16},{9,... | collective-permute-start | bytes 12296 | tf_op jit(solution)/shard_map/ppermute | solution.py:41
  28.5 4.9 %collective-permute-start.14 = (f32[8,128]{1,0:T(8,128)S(1)}, f32[8,128]{1,0:T(8,128)S(1)}, u32[]{:S(2)}, u32[]{:S(2)}) collective-permute-start(f32[8,128]{1,0:T(8,128)S(1)} %get-tuple-element.78), channel_id=1, source_target_pairs={{0,1},{1,0},{2,3},{3,2},{4,5},{5,4},{6,7},{7,6},{8,9},{9,8},{10,11... | collective-permute-start | bytes 12296 | tf_op jit(solution)/shard_map/ppermute | solution.py:41
  32.1 1.3 %collective-permute-start.15 = (f32[8,128]{1,0:T(8,128)S(1)}, f32[8,128]{1,0:T(8,128)S(1)}, u32[]{:S(2)}, u32[]{:S(2)}) collective-permute-start(f32[8,128]{1,0:T(8,128)S(1)} %get-tuple-element.79), channel_id=1, source_target_pairs={{0,8},{1,9},{2,10},{3,11},{4,12},{5,13},{6,14},{7,15},{8,0},{9,1},... | collective-permute-start | bytes 12296 | tf_op jit(solution)/shard_map/ppermute | solution.py:41
  58.1 2.6 %collective-permute-start.16 = (f32[8,128]{1,0:T(8,128)S(1)}, f32[8,128]{1,0:T(8,128)S(1)}, u32[]{:S(2)}, u32[]{:S(2)}) collective-permute-start(f32[8,128]{1,0:T(8,128)S(1)} %get-tuple-element.85), channel_id=1, source_target_pairs={{0,8},{1,2},{2,1},{3,4},{4,3},{5,6},{6,5},{7,15},{8,0},{9,10},{10,... | collective-permute-start | bytes 12296 | tf_op jit(solution)/shard_map/ppermute | solution.py:41
  58.6 3.0 %collective-permute-start.17 = (f32[8,128]{1,0:T(8,128)S(1)}, f32[8,128]{1,0:T(8,128)S(1)}, u32[]{:S(2)}, u32[]{:S(2)}) collective-permute-start(f32[8,128]{1,0:T(8,128)S(1)} %get-tuple-element.86), channel_id=1, source_target_pairs={{0,24},{1,25},{2,26},{3,27},{4,28},{5,29},{6,30},{7,31},{8,16},{9,... | collective-permute-start | bytes 12296 | tf_op jit(solution)/shard_map/ppermute | solution.py:41
  58.9 2.7 %collective-permute-start.18 = (f32[8,128]{1,0:T(8,128)S(1)}, f32[8,128]{1,0:T(8,128)S(1)}, u32[]{:S(2)}, u32[]{:S(2)}) collective-permute-start(f32[8,128]{1,0:T(8,128)S(1)} %get-tuple-element.87), channel_id=1, source_target_pairs={{0,1},{1,0},{2,3},{3,2},{4,5},{5,4},{6,7},{7,6},{8,9},{9,8},{10,11... | collective-permute-start | bytes 12296 | tf_op jit(solution)/shard_map/ppermute | solution.py:41
  60.5 1.2 %collective-permute-start.19 = (f32[8,128]{1,0:T(8,128)S(1)}, f32[8,128]{1,0:T(8,128)S(1)}, u32[]{:S(2)}, u32[]{:S(2)}) collective-permute-start(f32[8,128]{1,0:T(8,128)S(1)} %get-tuple-element.88), channel_id=1, source_target_pairs={{0,8},{1,9},{2,10},{3,11},{4,12},{5,13},{6,14},{7,15},{8,0},{9,1},... | collective-permute-start | bytes 12296 | tf_op jit(solution)/shard_map/ppermute | solution.py:41
  62.8 5.1 %collective-permute-start.20 = (f32[16,128]{1,0:T(8,128)S(1)}, f32[16,128]{1,0:T(8,128)S(1)}, u32[]{:S(2)}, u32[]{:S(2)}) collective-permute-start(f32[16,128]{1,0:T(8,128)S(1)} %get-tuple-element.90), channel_id=1, source_target_pairs={{0,8},{1,2},{2,1},{3,4},{4,3},{5,6},{6,5},{7,15},{8,0},{9,10},{10,... | collective-permute-start | bytes 24584 | tf_op jit(solution)/shard_map/ppermute | solution.py:41
  64.2 3.7 %collective-permute-start.21 = (f32[16,128]{1,0:T(8,128)S(1)}, f32[16,128]{1,0:T(8,128)S(1)}, u32[]{:S(2)}, u32[]{:S(2)}) collective-permute-start(f32[16,128]{1,0:T(8,128)S(1)} %get-tuple-element.91), channel_id=1, source_target_pairs={{0,24},{1,25},{2,26},{3,27},{4,28},{5,29},{6,30},{7,31},{8,16},{9,... | collective-permute-start | bytes 24584 | tf_op jit(solution)/shard_map/ppermute | solution.py:41
  65.2 3.7 %collective-permute-start.22 = (f32[16,128]{1,0:T(8,128)S(1)}, f32[16,128]{1,0:T(8,128)S(1)}, u32[]{:S(2)}, u32[]{:S(2)}) collective-permute-start(f32[16,128]{1,0:T(8,128)S(1)} %get-tuple-element.92), channel_id=1, source_target_pairs={{0,1},{1,0},{2,3},{3,2},{4,5},{5,4},{6,7},{7,6},{8,9},{9,8},{10,11... | collective-permute-start | bytes 24584 | tf_op jit(solution)/shard_map/ppermute | solution.py:41
  67.9 1.2 %collective-permute-start.23 = (f32[16,128]{1,0:T(8,128)S(1)}, f32[16,128]{1,0:T(8,128)S(1)}, u32[]{:S(2)}, u32[]{:S(2)}) collective-permute-start(f32[16,128]{1,0:T(8,128)S(1)} %get-tuple-element.93), channel_id=1, source_target_pairs={{0,8},{1,9},{2,10},{3,11},{4,12},{5,13},{6,14},{7,15},{8,0},{9,1},... | collective-permute-start | bytes 24584 | tf_op jit(solution)/shard_map/ppermute | solution.py:41
  70.8 3.7 %collective-permute-start.24 = (f32[16,128]{1,0:T(8,128)S(1)}, f32[16,128]{1,0:T(8,128)S(1)}, u32[]{:S(2)}, u32[]{:S(2)}) collective-permute-start(f32[16,128]{1,0:T(8,128)S(1)} %get-tuple-element.95), channel_id=1, source_target_pairs={{0,8},{1,2},{2,1},{3,4},{4,3},{5,6},{6,5},{7,15},{8,0},{9,10},{10,... | collective-permute-start | bytes 24584 | tf_op jit(solution)/shard_map/ppermute | solution.py:41
  71.1 3.4 %collective-permute-start.25 = (f32[16,128]{1,0:T(8,128)S(1)}, f32[16,128]{1,0:T(8,128)S(1)}, u32[]{:S(2)}, u32[]{:S(2)}) collective-permute-start(f32[16,128]{1,0:T(8,128)S(1)} %get-tuple-element.96), channel_id=1, source_target_pairs={{0,24},{1,25},{2,26},{3,27},{4,28},{5,29},{6,30},{7,31},{8,16},{9,... | collective-permute-start | bytes 24584 | tf_op jit(solution)/shard_map/ppermute | solution.py:41
  71.8 3.8 %collective-permute-start.26 = (f32[16,128]{1,0:T(8,128)S(1)}, f32[16,128]{1,0:T(8,128)S(1)}, u32[]{:S(2)}, u32[]{:S(2)}) collective-permute-start(f32[16,128]{1,0:T(8,128)S(1)} %get-tuple-element.97), channel_id=1, source_target_pairs={{0,1},{1,0},{2,3},{3,2},{4,5},{5,4},{6,7},{7,6},{8,9},{9,8},{10,11... | collective-permute-start | bytes 24584 | tf_op jit(solution)/shard_map/ppermute | solution.py:41
  74.5 1.2 %collective-permute-start.27 = (f32[16,128]{1,0:T(8,128)S(1)}, f32[16,128]{1,0:T(8,128)S(1)}, u32[]{:S(2)}, u32[]{:S(2)}) collective-permute-start(f32[16,128]{1,0:T(8,128)S(1)} %get-tuple-element.98), channel_id=1, source_target_pairs={{0,8},{1,9},{2,10},{3,11},{4,12},{5,13},{6,14},{7,15},{8,0},{9,1},... | collective-permute-start | bytes 24584 | tf_op jit(solution)/shard_map/ppermute | solution.py:41
  (7 other events, 43.2 us)

commit v3 on v2

--- a/solution.py
+++ b/solution.py
@@ -10,6 +10,7 @@
 AXES = ("row", "col")
 F32, BF16 = jnp.float32, jnp.bfloat16
 VM = pl.BlockSpec(memory_space=pltpu.VMEM)
+SM = pl.BlockSpec(memory_space=pltpu.SMEM)
 HB = pl.BlockSpec(memory_space=pltpu.HBM)
 DMA = pltpu.SemaphoreType.DMA
 MIB = 1 << 20
@@ -121,41 +122,18 @@
     n_t, n_i, n_o = len(tables), len(ins), len(outs)
 
     def kernel(*refs):
-        source, rest = refs[:n_t], refs[n_t:]
-        inputs, outputs, rest = rest[:n_i], rest[n_i : n_i + n_o], rest[n_i + n_o :]
-        smem, rest = rest[:n_t], rest[n_t:]
-        copies = []
-        if n_t:
-            sems, rest = rest[0], rest[1:]
-            copies = [
-                pltpu.make_async_copy(a, b, sems.at[i])
-                for i, (a, b) in enumerate(zip(source, smem))
-            ]
-        for copy in copies:
-            copy.start()
-        ready = set()
-
-        def table(i):
-            if i not in ready:
-                copies[i].wait()
-                ready.add(i)
-            return smem[i]
-
-        body(table, inputs, outputs, rest)
-        for i in range(n_t):
-            table(i)
+        rest = refs[n_t:]
+        body(refs[:n_t], rest[:n_i], rest[n_i : n_i + n_o], rest[n_i + n_o :])
 
     if where is HB:
         ins = [pltpu.with_memory_space_constraint(i, pltpu.HBM) for i in ins]
-    extra = [pltpu.SMEM(t.shape, t.dtype) for t in tables]
-    if n_t:
-        extra.append(DMA((n_t,)))
+    shapes = [o if isinstance(o, pl.MemoryRef) else jax.ShapeDtypeStruct(*o) for o in outs]
     return pl.pallas_call(
         kernel,
-        out_shape=[jax.ShapeDtypeStruct(s, d) for s, d in outs],
-        in_specs=[where] * (n_t + n_i),
-        out_specs=[VM] * n_o,
-        scratch_shapes=extra + list(scratch),
+        out_shape=shapes,
+        in_specs=[SM] * n_t + [where] * n_i,
+        out_specs=[SM if isinstance(o, pl.MemoryRef) else VM for o in outs],
+        scratch_shapes=list(scratch),
         compiler_params=pltpu.CompilerParams(vmem_limit_bytes=limit * MIB),
     )(*tables, *ins)
 
@@ -199,16 +177,18 @@
 
     def first(_, ins, outs, scratch):
         x_o, dd_o, di_o, ee_o, ei_o = outs[:5]
-        out = named(outs[5:])
+        out, smem = named(outs[5:9]), outs[9:]
         held, sems, xs = scratch[:-2], scratch[-2], scratch[-1]
         copies = [
-            pltpu.make_async_copy(a, b, sems.at[i]) for i, (a, b) in enumerate(zip(ins, held))
+            pltpu.make_async_copy(a, b, sems.at[i])
+            for i, (a, b) in enumerate(zip(ins, [*held, *smem]))
         ]
         for copy in copies:
             copy.start()
         for copy in copies:
             copy.wait()
-        rhs_r, d0_r, d1_r, s0_r, s1_r, a1_r, p1_r = held
+        rhs_r, d0_r, d1_r, p1_r = held
+        _, s0_r, _, _, s1_r, a1_r = smem
         dd, ee = spread(d0_r[...], nb, loads), spread(d1_r[...], nb1, loads)
         di = OMEGA / dd
         dd_o[...], di_o[...] = dd, di
@@ -266,33 +246,33 @@
             )
             wc_o[c * bs : (c + 1) * bs, :] = split_weight(tall.T)
 
-    def fine_sweep(table, ins, outs, scratch):
+    def fine_sweep(tables, ins, outs, scratch):
         rhs_r, di_r, x_r, w_r = ins[:4]
         ext, xs = scratch
         x = x_r[...]
         fill(ext, x, named(ins[4:]), nb, g0, loads)
-        y = coupled(ext, table(0), w_r, nb, k0, loads)
+        y = coupled(ext, tables[0], w_r, nb, k0, loads)
         x = keep * x + di_r[...] * (rhs_r[...] - y)
         outs[0][...] = x
-        s_r = table(1)
+        s_r = tables[1]
         pack(xs, x, nb, lambda line, g: s_r[line, g], named(outs[1:]), g0, loads)
 
-    def fine_last(table, ins, outs, scratch):
+    def fine_last(tables, ins, outs, scratch):
         rhs_r, di_r, x_r, w_r = ins[:4]
         x = x_r[...]
         fill(scratch[0], x, named(ins[4:]), nb, g0, loads)
-        y = coupled(scratch[0], table(0), w_r, nb, k0, loads)
+        y = coupled(scratch[0], tables[0], w_r, nb, k0, loads)
         outs[0][...] = keep * x + di_r[...] * (rhs_r[...] - y)
 
-    def restrict0(table, ins, outs, scratch):
+    def restrict0(tables, ins, outs, scratch):
         rhs_r, dd_r, x_r, w_r, p0_r, ei_r = ins[:6]
         ext, xs = scratch
         x = x_r[...]
         fill(ext, x, named(ins[6:]), nb, g0, loads)
-        y = coupled(ext, table(0), w_r, nb, k0, loads)
+        y = coupled(ext, tables[0], w_r, nb, k0, loads)
         res = rhs_r[...] - (dd_r[...] * x + y)
         parts = [halves(res[b * loads : (b + 1) * loads]) for b in range(nb)]
-        a_r, s_r = table(1), table(2)
+        a_r, s_r = tables[1], tables[2]
         total = []
         for c in range(nb1):
             left = jnp.concatenate(
@@ -305,28 +285,28 @@
         outs[0][...], outs[1][...] = b1, x1
         pack(xs, x1, nb1, lambda line, g: s_r[g, line], named(outs[2:]), g1, loads)
 
-    def level_sweep(table, ins, outs, scratch):
+    def level_sweep(tables, ins, outs, scratch):
         b1_r, ei_r, x_r, w_r = ins[:4]
         ext, xs = scratch
         x = x_r[...]
         fill(ext, x, named(ins[4:]), nb1, g1, loads)
-        y = coupled(ext, table(0), w_r, nb1, k1, loads)
+        y = coupled(ext, tables[0], w_r, nb1, k1, loads)
         x = keep * x + ei_r[...] * (b1_r[...] - y)
         outs[0][...] = x
-        s_r = table(1)
+        s_r = tables[1]
         pack(xs, x, nb1, lambda line, g: s_r[g, line], named(outs[1:]), g1, loads)
 
-    def restrict1(table, ins, outs, scratch):
+    def restrict1(tables, ins, outs, scratch):
         b1_r, ee_r, x_r, w_r, p1_r = ins[:5]
         x = x_r[...]
         fill(scratch[0], x, named(ins[5:]), nb1, g1, loads)
-        y = coupled(scratch[0], table(0), w_r, nb1, k1, loads)
+        y = coupled(scratch[0], tables[0], w_r, nb1, k1, loads)
         res = b1_r[...] - (ee_r[...] * x + y)
         parts = [
             folded(dot(halves(res[b * loads : (b + 1) * loads]), p1_r[b]), loads)
             for b in range(nb1)
         ]
-        a_r = table(1)
+        a_r = tables[1]
         index = [jnp.full((1, bs), a_r[b].astype(F32)) for b in range(nb1)]
         group = jnp.concatenate((parts + index) * 4, axis=0)
         for d in range(0, devices, 4):
@@ -367,7 +347,7 @@
         mine = folded(dot(jnp.concatenate(left, axis=1), wc_r[...]), loads)
         outs[0][...] = jnp.broadcast_to(mine[None], outs[0].shape)
 
-    def level_correct(table, ins, outs, scratch):
+    def level_correct(tables, ins, outs, scratch):
         sol_r, b1_r, ei_r, x_r, w_r, p1t_r, idx_r = ins[:7]
         got = named(ins[7:])
         ext, xs, cx = scratch
@@ -384,27 +364,27 @@
                 moved = folded(dot(halves(pick), p1t_r[nb1 + place]), loads)
                 old = got[name][g * loads : (g + 1) * loads, :]
                 ext[nb1 + place] = halves(masked(inside, old + moved))
-        a_r = table(2)
+        a_r = tables[2]
         lifted = [folded(dot(halves(cx[a_r[b]]), p1t_r[b]), loads) for b in range(nb1)]
         x = x_r[...] + jnp.concatenate(lifted, axis=0)
         for b in range(nb1):
             ext[b] = halves(x[b * loads : (b + 1) * loads])
-        y = coupled(ext, table(0), w_r, nb1, k1, loads)
+        y = coupled(ext, tables[0], w_r, nb1, k1, loads)
         x = keep * x + ei_r[...] * (b1_r[...] - y)
         outs[0][...] = x
-        s_r = table(1)
+        s_r = tables[1]
         pack(xs, x, nb1, lambda line, g: s_r[g, line], named(outs[1:]), g1, loads)
 
-    def lift(table, ins, outs, scratch):
+    def lift(tables, ins, outs, scratch):
         b1_r, ei_r, x_r, w_r, p0t_r, x0_r = ins[:6]
         ext, xs = scratch
         x = x_r[...]
         fill(ext, x, named(ins[6:]), nb1, g1, loads)
-        y = coupled(ext, table(0), w_r, nb1, k1, loads)
+        y = coupled(ext, tables[0], w_r, nb1, k1, loads)
         x = keep * x + ei_r[...] * (b1_r[...] - y)
         for b in range(nb1):
             ext[b] = halves(x[b * loads : (b + 1) * loads])
-        a_r, s_r = table(1), table(2)
+        a_r, s_r = tables[1], tables[2]
         parts = [folded(dot(ext[a_r[b]], p0t_r[b]), loads) for b in range(nb)]
         fine = x0_r[...] + jnp.concatenate(parts, axis=0)
         outs[0][...] = fine
@@ -414,17 +394,18 @@
         got = exchange(named(sent), table)
         return [got[name] for name in ORDER]
 
-    firsts = [rhs2, d0, d1, s0, s1t, a1, p1]
+    arrays, tables = [rhs2, d0, d1, p1], [c0, s0, a0, c1, s1t, a1]
     x0, dd, di, ee, ei, *sent = call(
         first,
-        [vec0, vec0, vec0, vec1, vec1] + [((first_rows, bs), F32)] * 4,
-        firsts,
-        scratch=[
-            (pltpu.VMEM if f.dtype == F32 else pltpu.SMEM)(f.shape, f.dtype) for f in firsts
-        ]
-        + [DMA((len(firsts),)), x3],
+        [vec0, vec0, vec0, vec1, vec1]
+        + [((first_rows, bs), F32)] * 4
+        + [pltpu.SMEM(t.shape, t.dtype) for t in tables],
+        arrays + tables,
+        scratch=[pltpu.VMEM(a.shape, F32) for a in arrays]
+        + [DMA((len(arrays) + len(tables),)), x3],
         where=HB,
     )
+    sent, (c0, s0, a0, c1, s1t, a1) = sent[:4], sent[4:]
     (w0,) = call(
         ready0,
         [((nb, k0 * bs, 2 * bs), BF16)],

time: 78.6 us -> 73.6 us (0.936)
  Pallas kernels: 18.2 us -> 13.3 us
    pallas_call x12, Pallas kernels: 18.2 us -> 13.3 us  [call(): pl.pallas_call(kernel, out_shape=shapes, in_specs=[SM] * n_t + [where] *...]
  transfers between devices with their start and end apart: 28 -> 28, of which waited for: 10 -> 10; matrix products, arithmetic and copies ran while one was open for 0% -> 0% of each run, Pallas kernels for 6% -> 7%
where the time goes in v3:
time: 73.6 us; the launch traced here: 73 us
  starting transfers between devices  29.7 us (40%)
  blocking collectives  22.1 us (30%)
  Pallas kernels  13.3 us (18%)
  waiting for transfers between devices  7.67 us (10%)
    ppermute x28, starting transfers between devices, exchange(): got[name] = lax.ppermute(sent[name], AXES, table[name])  29.7 us
    pallas_call x12, Pallas kernels, call(): pl.pallas_call(kernel, out_shape=shapes, in_specs=[SM] * n_t + [where] *...  13.3 us
    all_to_all x1, blocking collectives, on_device(): lax.all_to_all(terms.reshape(devices, loads + 1, nb1, bs), AXES, 0, 0, ti...  12.2 us
    all_to_all x1, blocking collectives, on_device(): sol = lax.all_to_all(mine, AXES, 0, 0, tiled=True)  9.93 us
    ppermute x28, waiting for transfers between devices, exchange(): got[name] = lax.ppermute(sent[name], AXES, table[name])  7.67 us
  transfers between devices with their start and end apart: 28, of which 10 were waited for; matrix products, arithmetic and copies ran while one was open for 0% of the time, Pallas kernels for 7%

profile of v3, /device:TPU:1, one launch (start us, length us, event | category | flops | bytes accessed | tf_op | source)
XLA Modules:
  0.0 73.0 jit_solution(959331826469140106)
XLA Ops:
  0.0 1.2 %shard_map.136 = (f32[32,128]{1,0:T(8,128)S(1)}, f32[32,128]{1,0:T(8,128)S(1)}, f32[32,128]{1,0:T(8,128)S(1)}, f32[8,128]{1,0:T(8,128)S(1)}, f32[8,128]{1,0:T(8,...) custom-call(f32[32,128]{1,0:T(8,128)} %bitcast.24, ...), custom_call_target="tpu_custom_call" | custom-call | tf_op jit(solution)/shard_map/pallas_call | solution.py:131
  1.3 2.7 %collective-permute-start.1 = (f32[280,128]{1,0:T(8,128)S(1)}, f32[280,128]{1,0:T(8,128)S(1)}, u32[]{:S(2)}, u32[]{:S(2)}) collective-permute-start(f32[280,128]{1,0:T(8,128)S(1)} %get-tuple-element.67), channel_id=1, source_target_pairs={{0,24},{1,25},{2,26},{3,27},{4,28},{5,29},{6,30},{7,31},{8,16},{9,... | collective-permute-start | bytes 430088 | tf_op jit(solution)/shard_map/ppermute | solution.py:42
  3.9 2.7 %collective-permute-start.2 = (f32[280,128]{1,0:T(8,128)S(1)}, f32[280,128]{1,0:T(8,128)S(1)}, u32[]{:S(2)}, u32[]{:S(2)}) collective-permute-start(f32[280,128]{1,0:T(8,128)S(1)} %get-tuple-element.68), channel_id=1, source_target_pairs={{0,1},{1,0},{2,3},{3,2},{4,5},{5,4},{6,7},{7,6},{8,9},{9,8},{10,11... | collective-permute-start | bytes 430088 | tf_op jit(solution)/shard_map/ppermute | solution.py:42
  6.6 3.7 %shard_map.137.refs_5_.refs_6_.refs_4_ = bf16[8,1792,256]{2,1,0:T(8,128)(2,1)S(1)} custom-call(f32[8,14,128,128]{3,2,1,0:T(8,128)} %bitcast.29), custom_call_target="tpu_custom_call" | custom-call | tf_op jit(solution)/shard_map/pallas_call | solution.py:131
  10.8 1.1 %shard_map.138 = (f32[32,128]{1,0:T(8,128)S(1)}, f32[16,128]{1,0:T(8,128)S(1)}, f32[16,128]{1,0:T(8,128)S(1)}, f32[16,128]{1,0:T(8,128)S(1)}, f32[16,128]{1,0:T(8,128)S(1)}) custom-call(s32[8,14]{1,0:T(8,128)S(4)} %get-tuple-element.58.refs_0_, s32[4,4]{1,0:T(4,128)S(4)} %get-tuple-element.60.refs_1_.refs_2_, f32[32,128]{1,0:T(8,128)S(1)} %bitcast.25, ...), custom_call_target="tpu_custom_call" | custom-call | tf_op jit(solution)/shard_map/pallas_call | solution.py:131
  12.4 1.2 %collective-permute-start.5 = (f32[16,128]{1,0:T(8,128)S(1)}, f32[16,128]{1,0:T(8,128)S(1)}, u32[]{:S(2)}, u32[]{:S(2)}) collective-permute-start(f32[16,128]{1,0:T(8,128)S(1)} %get-tuple-element.74), channel_id=1, source_target_pairs={{0,24},{1,25},{2,26},{3,27},{4,28},{5,29},{6,30},{7,31},{8,16},{9,... | collective-permute-start | bytes 24584 | tf_op jit(solution)/shard_map/ppermute | solution.py:42
  13.6 3.6 %collective-permute-start.6 = (f32[16,128]{1,0:T(8,128)S(1)}, f32[16,128]{1,0:T(8,128)S(1)}, u32[]{:S(2)}, u32[]{:S(2)}) collective-permute-start(f32[16,128]{1,0:T(8,128)S(1)} %get-tuple-element.75), channel_id=1, source_target_pairs={{0,1},{1,0},{2,3},{3,2},{4,5},{5,4},{6,7},{7,6},{8,9},{9,8},{10,11... | collective-permute-start | bytes 24584 | tf_op jit(solution)/shard_map/ppermute | solution.py:42
  17.3 1.0 %shard_map.139 = (bf16[2,1792,256]{2,1,0:T(8,128)(2,1)S(1)}, bf16[1024,256]{1,0:T(8,128)(2,1)S(1)}, bf16[8,128,256]{2,1,0:T(8,128)(2,1)S(1)}, bf16[2,128,256]{2,...) custom-call(f32[2,14,128,128]{3,2,1,0:T(8,128)S(1)} %bitcast.18, ...), custom_call_target="tpu_custom_call" | custom-call | tf_op jit(solution)/shard_map/pallas_call | solution.py:131
  18.6 1.2 %shard_map.140 = (f32[8,128]{1,0:T(8,128)S(1)}, f32[8,128]{1,0:T(8,128)S(1)}, f32[8,128]{1,0:T(8,128)S(1)}, f32[8,128]{1,0:T(8,128)S(1)}, f32[8,128]{1,0:T(8,128)S(1)}, /*index=5*/f32[8,128]{1,0:T(8,128)S(1)}) custom-call(s32[8,14]{1,0:T(8,128)S(4)} %get-tuple-element.58.refs_0_, s32[8]{0:T(128)S(4)} %get-tuple-element.62.refs_1_, ...), custom_call_target="tpu_custom_call" | custom-call | tf_op jit(solution)/shard_map/pallas_call | solution.py:131
  19.9 1.2 %collective-permute-start.10 = (f32[8,128]{1,0:T(8,128)S(1)}, f32[8,128]{1,0:T(8,128)S(1)}, u32[]{:S(2)}, u32[]{:S(2)}) collective-permute-start(f32[8,128]{1,0:T(8,128)S(1)} %get-tuple-element.84), channel_id=1, source_target_pairs={{0,1},{1,0},{2,3},{3,2},{4,5},{5,4},{6,7},{7,6},{8,9},{9,8},{10,11... | collective-permute-start | bytes 12296 | tf_op jit(solution)/shard_map/ppermute | solution.py:42
  21.0 1.2 %collective-permute-start.11 = (f32[8,128]{1,0:T(8,128)S(1)}, f32[8,128]{1,0:T(8,128)S(1)}, u32[]{:S(2)}, u32[]{:S(2)}) collective-permute-start(f32[8,128]{1,0:T(8,128)S(1)} %get-tuple-element.85), channel_id=1, source_target_pairs={{0,8},{1,9},{2,10},{3,11},{4,12},{5,13},{6,14},{7,15},{8,0},{9,1},... | collective-permute-start | bytes 12296 | tf_op jit(solution)/shard_map/ppermute | solution.py:42
  22.3 0.7 collective-permute-start.9
  23.4 2.0 %collective-permute-done.9.refs_7_ = f32[8,128]{1,0:T(8,128)S(1)} collective-permute-done((f32[8,128]{1,0:T(8,128)S(1)}, f32[8,128]{1,0:T(8,128)S(1)}, u32[]{:S(2)}, u32[]{:S(2)}) %collective-permute-start.9) | collective-permute-done | bytes 4128 | tf_op jit(solution)/shard_map/ppermute | solution.py:42
  26.6 3.6 %collective-permute-start.14 = (f32[8,128]{1,0:T(8,128)S(1)}, f32[8,128]{1,0:T(8,128)S(1)}, u32[]{:S(2)}, u32[]{:S(2)}) collective-permute-start(f32[8,128]{1,0:T(8,128)S(1)} %get-tuple-element.90), channel_id=1, source_target_pairs={{0,1},{1,0},{2,3},{3,2},{4,5},{5,4},{6,7},{7,6},{8,9},{9,8},{10,11... | collective-permute-start | bytes 12296 | tf_op jit(solution)/shard_map/ppermute | solution.py:42
  30.3 1.2 %collective-permute-done.14.refs_9_.refs_12_ = f32[8,128]{1,0:T(8,128)S(1)} collective-permute-done((f32[8,128]{1,0:T(8,128)S(1)}, f32[8,128]{1,0:T(8,128)S(1)}, u32[]{:S(2)}, u32[]{:S(2)}) %collective-permute-start.14) | collective-permute-done | bytes 4128 | tf_op jit(solution)/shard_map/ppermute | solution.py:42
  31.5 0.5 shard_map.142
  32.0 12.2 %all_to_all.10 = f32[32,5,2,128]{3,2,1,0:T(2,128)S(1)} all-to-all(f32[32,5,2,128]{3,2,1,0:T(2,128)S(1)} %bitcast.19), channel_id=1, replica_groups=mesh['row'=4,'col'=8] {'row','col'}, dimensions={0} | all-to-all | bytes 327680 | tf_op jit(solution)/shard_map/all_to_all | solution.py:447
  44.5 9.9 %all_to_all.11.refs_3_ = f32[32,4,128]{2,1,0:T(4,128)S(1)} all-to-all(f32[32,4,128]{2,1,0:T(4,128)S(1)} %shard_map.143), channel_id=1, replica_groups=mesh['row'=4,'col'=8] {'row','col'}, dimensions={0} | all-to-all | bytes 131072 | tf_op jit(solution)/shard_map/all_to_all | solution.py:456
  54.4 0.6 shard_map.144
  55.0 0.5 collective-permute-start.16
  55.8 1.5 %collective-permute-start.18 = (f32[8,128]{1,0:T(8,128)S(1)}, f32[8,128]{1,0:T(8,128)S(1)}, u32[]{:S(2)}, u32[]{:S(2)}) collective-permute-start(f32[8,128]{1,0:T(8,128)S(1)} %get-tuple-element.99), channel_id=1, source_target_pairs={{0,1},{1,0},{2,3},{3,2},{4,5},{5,4},{6,7},{7,6},{8,9},{9,8},{10,11... | collective-permute-start | bytes 12296 | tf_op jit(solution)/shard_map/ppermute | solution.py:42
  57.5 0.9 %collective-permute-done.17.refs_10_ = f32[8,128]{1,0:T(8,128)S(1)} collective-permute-done((f32[8,128]{1,0:T(8,128)S(1)}, f32[8,128]{1,0:T(8,128)S(1)}, u32[]{:S(2)}, u32[]{:S(2)}) %collective-permute-start.17) | collective-permute-done | bytes 4128 | tf_op jit(solution)/shard_map/ppermute | solution.py:42
  58.5 0.6 shard_map.145
  59.0 1.4 %collective-permute-start.20 = (f32[16,128]{1,0:T(8,128)S(1)}, f32[16,128]{1,0:T(8,128)S(1)}, u32[]{:S(2)}, u32[]{:S(2)}) collective-permute-start(f32[16,128]{1,0:T(8,128)S(1)} %get-tuple-element.102), channel_id=1, source_target_pairs={{0,8},{1,2},{2,1},{3,4},{4,3},{5,6},{6,5},{7,15},{8,0},{9,10},{10,... | collective-permute-start | bytes 24584 | tf_op jit(solution)/shard_map/ppermute | solution.py:42
  60.5 1.0 %collective-permute-start.21 = (f32[16,128]{1,0:T(8,128)S(1)}, f32[16,128]{1,0:T(8,128)S(1)}, u32[]{:S(2)}, u32[]{:S(2)}) collective-permute-start(f32[16,128]{1,0:T(8,128)S(1)} %get-tuple-element.103), channel_id=1, source_target_pairs={{0,24},{1,25},{2,26},{3,27},{4,28},{5,29},{6,30},{7,31},{8,16},{9,... | collective-permute-start | bytes 24584 | tf_op jit(solution)/shard_map/ppermute | solution.py:42
  61.5 2.7 %collective-permute-start.22 = (f32[16,128]{1,0:T(8,128)S(1)}, f32[16,128]{1,0:T(8,128)S(1)}, u32[]{:S(2)}, u32[]{:S(2)}) collective-permute-start(f32[16,128]{1,0:T(8,128)S(1)} %get-tuple-element.104), channel_id=1, source_target_pairs={{0,1},{1,0},{2,3},{3,2},{4,5},{5,4},{6,7},{7,6},{8,9},{9,8},{10,11... | collective-permute-start | bytes 24584 | tf_op jit(solution)/shard_map/ppermute | solution.py:42
  64.2 1.0 %collective-permute-done.22.refs_8_ = f32[16,128]{1,0:T(8,128)S(1)} collective-permute-done((f32[16,128]{1,0:T(8,128)S(1)}, f32[16,128]{1,0:T(8,128)S(1)}, u32[]{:S(2)}, u32[]{:S(2)}) %collective-permute-start.22) | collective-permute-done | bytes 8224 | tf_op jit(solution)/shard_map/ppermute | solution.py:42
  65.3 1.1 %shard_map.146 = (f32[32,128]{1,0:T(8,128)S(1)}, f32[16,128]{1,0:T(8,128)S(1)}, f32[16,128]{1,0:T(8,128)S(1)}, f32[16,128]{1,0:T(8,128)S(1)}, f32[16,128]{1,0:T(8,128)S(1)}) custom-call(s32[8,14]{1,0:T(8,128)S(4)} %get-tuple-element.58.refs_0_, s32[4,4]{1,0:T(4,128)S(4)} %get-tuple-element.60.refs_1_.refs_2_, f32[32,128]{1,0:T(8,128)S(1)} %bitcast.27, ...), custom_call_target="tpu_custom_call" | custom-call | tf_op jit(solution)/shard_map/pallas_call | solution.py:131
  66.7 0.7 collective-permute-start.25
  67.4 2.7 %collective-permute-start.26 = (f32[16,128]{1,0:T(8,128)S(1)}, f32[16,128]{1,0:T(8,128)S(1)}, u32[]{:S(2)}, u32[]{:S(2)}) collective-permute-start(f32[16,128]{1,0:T(8,128)S(1)} %get-tuple-element.109), channel_id=1, source_target_pairs={{0,1},{1,0},{2,3},{3,2},{4,5},{5,4},{6,7},{7,6},{8,9},{9,8},{10,11... | collective-permute-start | bytes 24584 | tf_op jit(solution)/shard_map/ppermute | solution.py:42
  70.1 1.1 %collective-permute-done.26.refs_7_ = f32[16,128]{1,0:T(8,128)S(1)} collective-permute-done((f32[16,128]{1,0:T(8,128)S(1)}, f32[16,128]{1,0:T(8,128)S(1)}, u32[]{:S(2)}, u32[]{:S(2)}) %collective-permute-start.26) | collective-permute-done | bytes 8224 | tf_op jit(solution)/shard_map/ppermute | solution.py:42
  71.3 1.7 %shard_map.147 = f32[32,128]{1,0:T(8,128)} custom-call(s32[8,14]{1,0:T(8,128)S(4)} %get-tuple-element.58.refs_0_, f32[32,128]{1,0:T(8,128)S(1)} %bitcast.28, f32[32,128]{1,0:T(8,128)S(1)} %get-tuple-element.59.refs_3_.refs_2_, f32[32,128]{1,0:T(8,128)S(1)} %get-tuple-element.106.refs_3_, bf16[8,1792,256]{2,1,0:T(8,128)(2,1)S(1)} %shard_map.137.refs_5_.refs_6_.refs_4_, ...), custom_call_target="tpu_custom_call" | custom-call | tf_op jit(solution)/shard_map/pallas_call | solution.py:131
  (48 shorter events, 4.4 us)
Async XLA Ops:
  1.2 9.2 %collective-permute-start = (f32[280,128]{1,0:T(8,128)S(1)}, f32[280,128]{1,0:T(8,128)S(1)}, u32[]{:S(2)}, u32[]{:S(2)}) collective-permute-start(f32[280,128]{1,0:T(8,128)S(1)} %get-tuple-element.66), channel_id=1, source_target_pairs={{0,8},{1,2},{2,1},{3,4},{4,3},{5,6},{6,5},{7,15},{8,0},{9,10},{10,... | collective-permute-start | bytes 430088 | tf_op jit(solution)/shard_map/ppermute | solution.py:42
  1.3 9.1 %collective-permute-start.1 = (f32[280,128]{1,0:T(8,128)S(1)}, f32[280,128]{1,0:T(8,128)S(1)}, u32[]{:S(2)}, u32[]{:S(2)}) collective-permute-start(f32[280,128]{1,0:T(8,128)S(1)} %get-tuple-element.67), channel_id=1, source_target_pairs={{0,24},{1,25},{2,26},{3,27},{4,28},{5,29},{6,30},{7,31},{8,16},{9,... | collective-permute-start | bytes 430088 | tf_op jit(solution)/shard_map/ppermute | solution.py:42
  3.9 6.9 %collective-permute-start.2 = (f32[280,128]{1,0:T(8,128)S(1)}, f32[280,128]{1,0:T(8,128)S(1)}, u32[]{:S(2)}, u32[]{:S(2)}) collective-permute-start(f32[280,128]{1,0:T(8,128)S(1)} %get-tuple-element.68), channel_id=1, source_target_pairs={{0,1},{1,0},{2,3},{3,2},{4,5},{5,4},{6,7},{7,6},{8,9},{9,8},{10,11... | collective-permute-start | bytes 430088 | tf_op jit(solution)/shard_map/ppermute | solution.py:42
  6.6 4.3 %collective-permute-start.3 = (f32[280,128]{1,0:T(8,128)S(1)}, f32[280,128]{1,0:T(8,128)S(1)}, u32[]{:S(2)}, u32[]{:S(2)}) collective-permute-start(f32[280,128]{1,0:T(8,128)S(1)} %get-tuple-element.69), channel_id=1, source_target_pairs={{0,8},{1,9},{2,10},{3,11},{4,12},{5,13},{6,14},{7,15},{8,0},{9,1},... | collective-permute-start | bytes 430088 | tf_op jit(solution)/shard_map/ppermute | solution.py:42
  10.3 7.0 %copy-start = (f32[1,1,2,14,128,128]{5,4,3,2,1,0:T(8,128)S(1)}, f32[1,1,2,14,128,128]{5,4,3,2,1,0:T(8,128)}, u32[]{:S(2)}) copy-start(f32[1,1,2,14,128,128]{5,4,3,2,1,0:T(8,128)} %param.22) | copy-start | bytes 5505028
  10.3 7.0 %copy-start.1 = (f32[1,1,8,128,128]{4,3,2,1,0:T(8,128)S(1)}, f32[1,1,8,128,128]{4,3,2,1,0:T(8,128)}, u32[]{:S(2)}) copy-start(f32[1,1,8,128,128]{4,3,2,1,0:T(8,128)} %param.19) | copy-start | bytes 1572868
  10.3 7.0 %copy-start.2 = (f32[1,1,2,128,128]{4,3,2,1,0:T(8,128)S(1)}, f32[1,1,2,128,128]{4,3,2,1,0:T(8,128)}, u32[]{:S(2)}) copy-start(f32[1,1,2,128,128]{4,3,2,1,0:T(8,128)} %param.25) | copy-start | bytes 393220
  10.4 7.0 %copy-start.4 = (f32[32,1024]{1,0:T(8,128)S(1)}, f32[32,1024]{1,0:T(8,128)}, u32[]{:S(2)}) copy-start(f32[32,1024]{1,0:T(8,128)} %refs_3_.1) | copy-start | bytes 393220
  12.0 6.4 %collective-permute-start.4 = (f32[16,128]{1,0:T(8,128)S(1)}, f32[16,128]{1,0:T(8,128)S(1)}, u32[]{:S(2)}, u32[]{:S(2)}) collective-permute-start(f32[16,128]{1,0:T(8,128)S(1)} %get-tuple-element.73), channel_id=1, source_target_pairs={{0,8},{1,2},{2,1},{3,4},{4,3},{5,6},{6,5},{7,15},{8,0},{9,10},{10,... | collective-permute-start | bytes 24584 | tf_op jit(solution)/shard_map/ppermute | solution.py:42
  12.4 6.0 %collective-permute-start.5 = (f32[16,128]{1,0:T(8,128)S(1)}, f32[16,128]{1,0:T(8,128)S(1)}, u32[]{:S(2)}, u32[]{:S(2)}) collective-permute-start(f32[16,128]{1,0:T(8,128)S(1)} %get-tuple-element.74), channel_id=1, source_target_pairs={{0,24},{1,25},{2,26},{3,27},{4,28},{5,29},{6,30},{7,31},{8,16},{9,... | collective-permute-start | bytes 24584 | tf_op jit(solution)/shard_map/ppermute | solution.py:42
  13.6 5.0 %collective-permute-start.6 = (f32[16,128]{1,0:T(8,128)S(1)}, f32[16,128]{1,0:T(8,128)S(1)}, u32[]{:S(2)}, u32[]{:S(2)}) collective-permute-start(f32[16,128]{1,0:T(8,128)S(1)} %get-tuple-element.75), channel_id=1, source_target_pairs={{0,1},{1,0},{2,3},{3,2},{4,5},{5,4},{6,7},{7,6},{8,9},{9,8},{10,11... | collective-permute-start | bytes 24584 | tf_op jit(solution)/shard_map/ppermute | solution.py:42
  17.2 1.4 %collective-permute-start.7 = (f32[16,128]{1,0:T(8,128)S(1)}, f32[16,128]{1,0:T(8,128)S(1)}, u32[]{:S(2)}, u32[]{:S(2)}) collective-permute-start(f32[16,128]{1,0:T(8,128)S(1)} %get-tuple-element.76), channel_id=1, source_target_pairs={{0,8},{1,9},{2,10},{3,11},{4,12},{5,13},{6,14},{7,15},{8,0},{9,1},... | collective-permute-start | bytes 24584 | tf_op jit(solution)/shard_map/ppermute | solution.py:42
  19.9 3.1 %collective-permute-start.10 = (f32[8,128]{1,0:T(8,128)S(1)}, f32[8,128]{1,0:T(8,128)S(1)}, u32[]{:S(2)}, u32[]{:S(2)}) collective-permute-start(f32[8,128]{1,0:T(8,128)S(1)} %get-tuple-element.84), channel_id=1, source_target_pairs={{0,1},{1,0},{2,3},{3,2},{4,5},{5,4},{6,7},{7,6},{8,9},{9,8},{10,11... | collective-permute-start | bytes 12296 | tf_op jit(solution)/shard_map/ppermute | solution.py:42
  21.0 2.1 %collective-permute-start.11 = (f32[8,128]{1,0:T(8,128)S(1)}, f32[8,128]{1,0:T(8,128)S(1)}, u32[]{:S(2)}, u32[]{:S(2)}) collective-permute-start(f32[8,128]{1,0:T(8,128)S(1)} %get-tuple-element.85), channel_id=1, source_target_pairs={{0,8},{1,9},{2,10},{3,11},{4,12},{5,13},{6,14},{7,15},{8,0},{9,1},... | collective-permute-start | bytes 12296 | tf_op jit(solution)/shard_map/ppermute | solution.py:42
  22.3 1.2 %collective-permute-start.8 = (f32[8,128]{1,0:T(8,128)S(1)}, f32[8,128]{1,0:T(8,128)S(1)}, u32[]{:S(2)}, u32[]{:S(2)}) collective-permute-start(f32[8,128]{1,0:T(8,128)S(1)} %get-tuple-element.82), channel_id=1, source_target_pairs={{0,8},{1,2},{2,1},{3,4},{4,3},{5,6},{6,5},{7,15},{8,0},{9,10},{10,... | collective-permute-start | bytes 12296 | tf_op jit(solution)/shard_map/ppermute | solution.py:42
  22.3 3.1 %collective-permute-start.9 = (f32[8,128]{1,0:T(8,128)S(1)}, f32[8,128]{1,0:T(8,128)S(1)}, u32[]{:S(2)}, u32[]{:S(2)}) collective-permute-start(f32[8,128]{1,0:T(8,128)S(1)} %get-tuple-element.83), channel_id=1, source_target_pairs={{0,24},{1,25},{2,26},{3,27},{4,28},{5,29},{6,30},{7,31},{8,16},{9,... | collective-permute-start | bytes 12296 | tf_op jit(solution)/shard_map/ppermute | solution.py:42
  25.8 4.5 %collective-permute-start.12 = (f32[8,128]{1,0:T(8,128)S(1)}, f32[8,128]{1,0:T(8,128)S(1)}, u32[]{:S(2)}, u32[]{:S(2)}) collective-permute-start(f32[8,128]{1,0:T(8,128)S(1)} %get-tuple-element.88), channel_id=1, source_target_pairs={{0,8},{1,2},{2,1},{3,4},{4,3},{5,6},{6,5},{7,15},{8,0},{9,10},{10,... | collective-permute-start | bytes 12296 | tf_op jit(solution)/shard_map/ppermute | solution.py:42
  26.2 4.0 %collective-permute-start.13 = (f32[8,128]{1,0:T(8,128)S(1)}, f32[8,128]{1,0:T(8,128)S(1)}, u32[]{:S(2)}, u32[]{:S(2)}) collective-permute-start(f32[8,128]{1,0:T(8,128)S(1)} %get-tuple-element.89), channel_id=1, source_target_pairs={{0,24},{1,25},{2,26},{3,27},{4,28},{5,29},{6,30},{7,31},{8,16},{9,... | collective-permute-start | bytes 12296 | tf_op jit(solution)/shard_map/ppermute | solution.py:42
  26.6 4.9 %collective-permute-start.14 = (f32[8,128]{1,0:T(8,128)S(1)}, f32[8,128]{1,0:T(8,128)S(1)}, u32[]{:S(2)}, u32[]{:S(2)}) collective-permute-start(f32[8,128]{1,0:T(8,128)S(1)} %get-tuple-element.90), channel_id=1, source_target_pairs={{0,1},{1,0},{2,3},{3,2},{4,5},{5,4},{6,7},{7,6},{8,9},{9,8},{10,11... | collective-permute-start | bytes 12296 | tf_op jit(solution)/shard_map/ppermute | solution.py:42
  30.2 1.3 %collective-permute-start.15 = (f32[8,128]{1,0:T(8,128)S(1)}, f32[8,128]{1,0:T(8,128)S(1)}, u32[]{:S(2)}, u32[]{:S(2)}) collective-permute-start(f32[8,128]{1,0:T(8,128)S(1)} %get-tuple-element.91), channel_id=1, source_target_pairs={{0,8},{1,9},{2,10},{3,11},{4,12},{5,13},{6,14},{7,15},{8,0},{9,1},... | collective-permute-start | bytes 12296 | tf_op jit(solution)/shard_map/ppermute | solution.py:42
  55.0 2.6 %collective-permute-start.16 = (f32[8,128]{1,0:T(8,128)S(1)}, f32[8,128]{1,0:T(8,128)S(1)}, u32[]{:S(2)}, u32[]{:S(2)}) collective-permute-start(f32[8,128]{1,0:T(8,128)S(1)} %get-tuple-element.97), channel_id=1, source_target_pairs={{0,8},{1,2},{2,1},{3,4},{4,3},{5,6},{6,5},{7,15},{8,0},{9,10},{10,... | collective-permute-start | bytes 12296 | tf_op jit(solution)/shard_map/ppermute | solution.py:42
  55.4 3.0 %collective-permute-start.17 = (f32[8,128]{1,0:T(8,128)S(1)}, f32[8,128]{1,0:T(8,128)S(1)}, u32[]{:S(2)}, u32[]{:S(2)}) collective-permute-start(f32[8,128]{1,0:T(8,128)S(1)} %get-tuple-element.98), channel_id=1, source_target_pairs={{0,24},{1,25},{2,26},{3,27},{4,28},{5,29},{6,30},{7,31},{8,16},{9,... | collective-permute-start | bytes 12296 | tf_op jit(solution)/shard_map/ppermute | solution.py:42
  55.8 2.7 %collective-permute-start.18 = (f32[8,128]{1,0:T(8,128)S(1)}, f32[8,128]{1,0:T(8,128)S(1)}, u32[]{:S(2)}, u32[]{:S(2)}) collective-permute-start(f32[8,128]{1,0:T(8,128)S(1)} %get-tuple-element.99), channel_id=1, source_target_pairs={{0,1},{1,0},{2,3},{3,2},{4,5},{5,4},{6,7},{7,6},{8,9},{9,8},{10,11... | collective-permute-start | bytes 12296 | tf_op jit(solution)/shard_map/ppermute | solution.py:42
  57.3 1.2 %collective-permute-start.19 = (f32[8,128]{1,0:T(8,128)S(1)}, f32[8,128]{1,0:T(8,128)S(1)}, u32[]{:S(2)}, u32[]{:S(2)}) collective-permute-start(f32[8,128]{1,0:T(8,128)S(1)} %get-tuple-element.100), channel_id=1, source_target_pairs={{0,8},{1,9},{2,10},{3,11},{4,12},{5,13},{6,14},{7,15},{8,0},{9,1},... | collective-permute-start | bytes 12296 | tf_op jit(solution)/shard_map/ppermute | solution.py:42
  59.0 5.1 %collective-permute-start.20 = (f32[16,128]{1,0:T(8,128)S(1)}, f32[16,128]{1,0:T(8,128)S(1)}, u32[]{:S(2)}, u32[]{:S(2)}) collective-permute-start(f32[16,128]{1,0:T(8,128)S(1)} %get-tuple-element.102), channel_id=1, source_target_pairs={{0,8},{1,2},{2,1},{3,4},{4,3},{5,6},{6,5},{7,15},{8,0},{9,10},{10,... | collective-permute-start | bytes 24584 | tf_op jit(solution)/shard_map/ppermute | solution.py:42
  60.5 3.7 %collective-permute-start.21 = (f32[16,128]{1,0:T(8,128)S(1)}, f32[16,128]{1,0:T(8,128)S(1)}, u32[]{:S(2)}, u32[]{:S(2)}) collective-permute-start(f32[16,128]{1,0:T(8,128)S(1)} %get-tuple-element.103), channel_id=1, source_target_pairs={{0,24},{1,25},{2,26},{3,27},{4,28},{5,29},{6,30},{7,31},{8,16},{9,... | collective-permute-start | bytes 24584 | tf_op jit(solution)/shard_map/ppermute | solution.py:42
  61.5 3.7 %collective-permute-start.22 = (f32[16,128]{1,0:T(8,128)S(1)}, f32[16,128]{1,0:T(8,128)S(1)}, u32[]{:S(2)}, u32[]{:S(2)}) collective-permute-start(f32[16,128]{1,0:T(8,128)S(1)} %get-tuple-element.104), channel_id=1, source_target_pairs={{0,1},{1,0},{2,3},{3,2},{4,5},{5,4},{6,7},{7,6},{8,9},{9,8},{10,11... | collective-permute-start | bytes 24584 | tf_op jit(solution)/shard_map/ppermute | solution.py:42
  64.2 1.2 %collective-permute-start.23 = (f32[16,128]{1,0:T(8,128)S(1)}, f32[16,128]{1,0:T(8,128)S(1)}, u32[]{:S(2)}, u32[]{:S(2)}) collective-permute-start(f32[16,128]{1,0:T(8,128)S(1)} %get-tuple-element.105), channel_id=1, source_target_pairs={{0,8},{1,9},{2,10},{3,11},{4,12},{5,13},{6,14},{7,15},{8,0},{9,1},... | collective-permute-start | bytes 24584 | tf_op jit(solution)/shard_map/ppermute | solution.py:42
  66.4 3.7 %collective-permute-start.24 = (f32[16,128]{1,0:T(8,128)S(1)}, f32[16,128]{1,0:T(8,128)S(1)}, u32[]{:S(2)}, u32[]{:S(2)}) collective-permute-start(f32[16,128]{1,0:T(8,128)S(1)} %get-tuple-element.107), channel_id=1, source_target_pairs={{0,8},{1,2},{2,1},{3,4},{4,3},{5,6},{6,5},{7,15},{8,0},{9,10},{10,... | collective-permute-start | bytes 24584 | tf_op jit(solution)/shard_map/ppermute | solution.py:42
  66.7 3.4 %collective-permute-start.25 = (f32[16,128]{1,0:T(8,128)S(1)}, f32[16,128]{1,0:T(8,128)S(1)}, u32[]{:S(2)}, u32[]{:S(2)}) collective-permute-start(f32[16,128]{1,0:T(8,128)S(1)} %get-tuple-element.108), channel_id=1, source_target_pairs={{0,24},{1,25},{2,26},{3,27},{4,28},{5,29},{6,30},{7,31},{8,16},{9,... | collective-permute-start | bytes 24584 | tf_op jit(solution)/shard_map/ppermute | solution.py:42
  67.4 3.8 %collective-permute-start.26 = (f32[16,128]{1,0:T(8,128)S(1)}, f32[16,128]{1,0:T(8,128)S(1)}, u32[]{:S(2)}, u32[]{:S(2)}) collective-permute-start(f32[16,128]{1,0:T(8,128)S(1)} %get-tuple-element.109), channel_id=1, source_target_pairs={{0,1},{1,0},{2,3},{3,2},{4,5},{5,4},{6,7},{7,6},{8,9},{9,8},{10,11... | collective-permute-start | bytes 24584 | tf_op jit(solution)/shard_map/ppermute | solution.py:42
  70.1 1.2 %collective-permute-start.27 = (f32[16,128]{1,0:T(8,128)S(1)}, f32[16,128]{1,0:T(8,128)S(1)}, u32[]{:S(2)}, u32[]{:S(2)}) collective-permute-start(f32[16,128]{1,0:T(8,128)S(1)} %get-tuple-element.110), channel_id=1, source_target_pairs={{0,8},{1,9},{2,10},{3,11},{4,12},{5,13},{6,14},{7,15},{8,0},{9,1},... | collective-permute-start | bytes 24584 | tf_op jit(solution)/shard_map/ppermute | solution.py:42
  (1 other events, 4.3 us)
